TPU v7x, 8 devices: a whole 2x2x1 slice. The times are simulated.
8 devices in a mesh: dp: 4 (over z, y, x), cp: 2 (over core).
Axes of the slice: x: 2, y: 2, z: 1, core: 2. Of those that a mesh axis runs over, the one named last changes fastest.
Arguments:
- inputs: bfloat16 [64, 2048, 261], P('dp', 'cp')
- latents: float32 [512, 1024], replicated
- x_gain: float32 [261], replicated
- x_shift: float32 [261], replicated
- z_gain: float32 [1024], replicated
- z_shift: float32 [1024], replicated
- w_query: bfloat16 [1024, 1024], replicated
- w_key: bfloat16 [261, 1024], replicated
- w_value: bfloat16 [261, 1024], replicated
- w_out: bfloat16 [1024, 1024], replicated
- m_gain: float32 [1024], replicated
- m_shift: float32 [1024], replicated
- w_up: bfloat16 [1024, 1024], replicated
- b_up: float32 [1024], replicated
- w_down: bfloat16 [1024, 1024], replicated
- b_down: float32 [1024], replicated
- d_out: bfloat16 [64, 512, 1024], P('dp')
Outputs:
- output 1: float32 [64, 512, 1024], P('dp')
- output 2: bfloat16 [64, 2048, 261], P('dp', 'cp')
- output 3: float32 [512, 1024], replicated
- output 4: float32 [261], replicated
- output 5: float32 [261], replicated
- output 6: float32 [1024], replicated
- output 7: float32 [1024], replicated
- output 8: float32 [1024, 1024], replicated
- output 9: float32 [261, 1024], replicated
- output 10: float32 [261, 1024], replicated
- output 11: float32 [1024, 1024], replicated
- output 12: float32 [1024], replicated
- output 13: float32 [1024], replicated
- output 14: float32 [1024, 1024], replicated
- output 15: float32 [1024], replicated
- output 16: float32 [1024, 1024], replicated
- output 17: float32 [1024], replicated
All inputs are finite; a program needn't handle non-finite values.
Results may differ from a plain program's by a relative error of at most 0.0171243.
Values sent between devices are 32-bit elements.
A program may use at most 1 GiB of HBM per device.

v0:
```python
import jax
import jax.numpy as jnp
from jax import lax
from jax.sharding import PartitionSpec as P

LN_EPS = 1e-5
LOW_TYPE = jnp.bfloat16
ACC_TYPE = jnp.float32


def layer_norm(tensor, ln_gain, ln_shift):
    row_mean = jnp.mean(tensor, axis=-1, keepdims=True)
    centred = tensor - row_mean
    variance = jnp.mean(centred * centred, axis=-1, keepdims=True)
    return centred * lax.rsqrt(variance + LN_EPS) * ln_gain + ln_shift


def contract(einsum_form, lhs_arr, rhs_arr):
    return jnp.einsum(einsum_form, lhs_arr, rhs_arr, preferred_element_type=ACC_TYPE)


def solution(mesh):
    x_spec = P('dp', 'cp', None)
    row_spec = P('dp', None, None)
    vec_spec = P(None)
    mat_spec = P(None, None)
    in_specs = (x_spec, mat_spec, vec_spec, vec_spec, vec_spec, vec_spec, mat_spec, mat_spec, mat_spec, mat_spec,
                vec_spec, vec_spec, mat_spec, vec_spec, mat_spec, vec_spec, row_spec)
    out_specs = (row_spec, x_spec, mat_spec, vec_spec, vec_spec, vec_spec, vec_spec, mat_spec, mat_spec, mat_spec, mat_spec,
                 vec_spec, vec_spec, mat_spec, vec_spec, mat_spec, vec_spec)

    def local_step(inputs, latents, x_gain, x_shift, z_gain, z_shift, w_query, w_key, w_value, w_out, m_gain, m_shift, w_up, b_up, w_down, b_down, d_out):
        qk_scale = w_query.shape[1] ** -0.5
        z_ln, z_pull = jax.vjp(layer_norm, latents, z_gain, z_shift)
        z_norm = z_ln.astype(LOW_TYPE)
        queries = contract('nd,dk->nk', z_norm, w_query).astype(LOW_TYPE)
        x_ln, x_pull = jax.vjp(layer_norm, inputs.astype(ACC_TYPE), x_gain, x_shift)
        x_norm = x_ln.astype(LOW_TYPE)
        key_rows = contract('bmc,ck->bmk', x_norm, w_key).astype(LOW_TYPE)
        value_rows = contract('bmc,cv->bmv', x_norm, w_value).astype(LOW_TYPE)
        logits = contract('nk,bmk->bnm', queries, key_rows) * qk_scale
        row_max = lax.pmax(jnp.max(logits, axis=-1, keepdims=True), 'cp')
        weights = jnp.exp(logits - row_max)
        row_sum, mixed_sum = lax.psum(
            (jnp.sum(weights, axis=-1, keepdims=True), contract('bnm,bmv->bnv', weights.astype(LOW_TYPE), value_rows)), 'cp')
        attn_out = (mixed_sum / row_sum).astype(LOW_TYPE)
        attn_probs = weights / row_sum
        z_mid = latents + contract('bnv,vd->bnd', attn_out, w_out)
        h_ln, h_pull = jax.vjp(layer_norm, z_mid, m_gain, m_shift)
        hidden = h_ln.astype(LOW_TYPE)
        act_f32, gelu_pull = jax.vjp(jax.nn.gelu, contract('bnd,de->bne', hidden, w_up) + b_up)
        act_val = act_f32.astype(LOW_TYPE)
        z_out = z_mid + contract('bne,ed->bnd', act_val, w_down) + b_down

        d_act = contract('bnd,ed->bne', d_out, w_down).astype(LOW_TYPE)
        (d_pre,) = gelu_pull(d_act.astype(ACC_TYPE))
        d_pre_low = d_pre.astype(LOW_TYPE)
        d_hidden = contract('bne,de->bnd', d_pre_low, w_up).astype(LOW_TYPE)
        d_mid_ln, d_m_gain_part, d_m_shift_part = h_pull(d_hidden.astype(ACC_TYPE))
        d_mid = d_out.astype(ACC_TYPE) + d_mid_ln
        d_mid_low = d_mid.astype(LOW_TYPE)
        d_attn = contract('bnd,vd->bnv', d_mid_low, w_out).astype(LOW_TYPE)
        mlp_grads = (
            contract('bnv,bnd->vd', attn_out, d_mid_low),
            d_m_gain_part, d_m_shift_part,
            contract('bnd,bne->de', hidden, d_pre_low),
            jnp.sum(d_pre, axis=(0, 1)),
            contract('bne,bnd->ed', act_val, d_out),
            jnp.sum(d_out.astype(ACC_TYPE), axis=(0, 1)),
            jnp.sum(d_mid, axis=0))
        d_w_out, d_m_gain, d_m_shift, d_w_up, d_b_up, d_w_down, d_b_down, d_mid_sum = lax.psum(mlp_grads, 'dp')

        d_probs = contract('bnv,bmv->bnm', d_attn, value_rows)
        row_dot = lax.psum(jnp.sum(attn_probs * d_probs, axis=-1, keepdims=True), 'cp')
        d_logits = (attn_probs * (d_probs - row_dot) * qk_scale).astype(LOW_TYPE)
        d_keys = contract('bnm,nk->bmk', d_logits, queries).astype(LOW_TYPE)
        d_values = contract('bnm,bnv->bmv', attn_probs.astype(LOW_TYPE), d_attn).astype(LOW_TYPE)
        d_x_norm = (contract('bmk,ck->bmc', d_keys, w_key) + contract('bmv,cv->bmc', d_values, w_value)).astype(LOW_TYPE)
        d_x_ln, d_x_gain_part, d_x_shift_part = x_pull(d_x_norm.astype(ACC_TYPE))
        d_query_part = contract('bnm,bmk->nk', d_logits, key_rows).astype(LOW_TYPE)
        shared_grads = (
            contract('nk,dk->nd', d_query_part, w_query),
            contract('nd,nk->dk', z_norm, d_query_part),
            contract('bmc,bmk->ck', x_norm, d_keys),
            contract('bmc,bmv->cv', x_norm, d_values),
            d_x_gain_part, d_x_shift_part)
        d_z_norm, d_w_query, d_w_key, d_w_value, d_x_gain, d_x_shift = lax.psum(shared_grads, ('dp', 'cp'))
        d_lat_ln, d_z_gain, d_z_shift = z_pull(d_z_norm)
        return (z_out, d_x_ln.astype(LOW_TYPE), d_lat_ln + d_mid_sum, d_x_gain, d_x_shift, d_z_gain, d_z_shift,
                d_w_query, d_w_key, d_w_value, d_w_out, d_m_gain, d_m_shift, d_w_up, d_b_up, d_w_down, d_b_down)

    return jax.shard_map(local_step, mesh=mesh, in_specs=in_specs, out_specs=out_specs, check_vma=False)
```

profile of v0, /device:TPU:0, one launch (start us, length us, event | category | flops | bytes accessed | tf_op | source)
XLA Modules:
  0.0 1253.6 jit_solution(4266020889819563715)
XLA Ops:
  7.2 0.0 copy-start
  7.2 0.0 slice-start
  7.3 0.0 all-reduce.8.cloned.1.call-start
  7.3 1.9 reduce_sum.204
  9.2 1.9 multiply_reduce_fusion.4
  11.2 8.1 convert_reduce_fusion.3
  19.4 0.0 slice-start.2
  19.4 8.5 fusion.27
  28.0 39.0 %convolution_convert_fusion.2 = bf16[16,1024,1024]{2,1,0:T(8,128)(2,1)} fusion(bf16[261,1024]{1,0:T(8,128)(2,1)S(1)} %copy-done.50, f32[261]{0:T(512)S(1)} %copy-done.59, f32[261]{0:T(512)S(1)} %copy-done.42, f32[16,1024]{1,0:T(8,128)S(1)} %fusion.56, f32[16,1024]{1,0:T(8,128)S(1)} %broadcast_multiply_fusion, bf16[16,1024,261]{1,0,2:T(8,128)(2,1)S(1)} %bitcast.99), kind=kOutput, calls=%fused_computation.52 | convolution fusion | flops 8800141312 | bytes 42774568 | tf_op jit(solution)/shard_map/bmc,cv->bmv/dot_general | solution.py:19
  67.1 39.0 %convolution_convert_fusion.3 = bf16[16,1024,1024]{2,1,0:T(8,128)(2,1)} fusion(bf16[261,1024]{1,0:T(8,128)(2,1)S(1)} %copy-done.48, f32[261]{0:T(512)S(1)} %copy-done.59, f32[261]{0:T(512)S(1)} %copy-done.42, f32[16,1024]{1,0:T(8,128)S(1)} %fusion.56, f32[16,1024]{1,0:T(8,128)S(1)} %broadcast_multiply_fusion, bf16[16,1024,261]{1,0,2:T(8,128)(2,1)S(1)} %bitcast.99), kind=kOutput, calls=%fused_computation.53 | convolution fusion | flops 8800141312 | bytes 42774568 | tf_op jit(solution)/shard_map/bmc,ck->bmk/dot_general | solution.py:19
  106.2 2.9 fusion.50
  109.1 31.7 %bitcast_reduce_fusion = (f32[16,512]{1,0:T(8,128)S(1)}, f32[16,1024,512]{2,1,0:T(8,128)}) fusion(bf16[16,1024,1024]{2,1,0:T(8,128)(2,1)} %convolution_convert_fusion.3, bf16[512,1024,1]{1,0,2:T(8,128)(2,1)S(1)} %fusion.50), kind=kOutput, calls=%fused_computation.24 | convolution fusion | flops 17196638208 | bytes 68190208 | tf_op jit(solution)/shard_map/nk,bmk->bnm/dot_general | solution.py:19
  140.7 4.1 pmax.7
  144.8 41.4 %fusion.30 = f32[16,512,1024]{1,2,0:T(8,128)} fusion(bf16[16,1024,1024]{2,1,0:T(8,128)(2,1)} %convolution_convert_fusion.2, f32[16,1024,512]{2,1,0:T(8,128)} %get-tuple-element.64, f32[16,512]{1,0:T(8,128)S(1)} %pmax.7), kind=kOutput, calls=%fused_computation.63 | convolution fusion | flops 17205035008 | bytes 100696064 | tf_op jit(solution)/shard_map/bnm,bmv->bnv/dot_general | solution.py:19
  186.3 0.0 all-reduce.8.cloned.1.call-update
  186.3 0.0 all-reduce.10.cloned.1.call-start
  186.4 17.6 %fusion.15 = f32[16,512]{1,0:T(8,128)S(1)} fusion(f32[16,1024,512]{2,1,0:T(8,128)} %get-tuple-element.64, f32[16,512]{1,0:T(8,128)S(1)} %pmax.7), kind=kLoop, calls=%fused_computation.40 | loop fusion | flops 25157632 | bytes 33619968 | tf_op jit(solution)/shard_map/reduce_sum | solution.py:45
  203.9 3.4 psum.120
  207.4 79.8 %all-reduce.8.cloned.1.call-done = f32[16,512,1024]{1,2,0:T(8,128)} async-done(((f32[16,512,1024]{1,2,0:T(8,128)}), f32[16,512,1024]{1,2,0:T(8,128)}) %all-reduce.8.cloned.1.call-update) | async-done | bytes 33554448 | tf_op jit(solution)/shard_map/psum | solution.py:44
  287.2 18.0 %divide_convert_fusion = bf16[16,512,1024]{1,2,0:T(8,128)(2,1)} fusion(f32[16,512,1024]{1,2,0:T(8,128)} %all-reduce.8.cloned.1.call-done, f32[16,512]{1,0:T(8,128)S(1)} %psum.120), kind=kLoop, calls=%fused_computation.32 | loop fusion | flops 16777216 | bytes 50364416 | tf_op jit(solution)/shard_map/convert_element_type | solution.py:46
  305.1 28.2 %add_reduce_fusion = (f32[16,512]{1,0:T(8,128)S(1)}, f32[16,512,1024]{2,1,0:T(8,128)}) fusion(f32[512,1024]{1,0:T(8,128)} %param.18, bf16[16,512,1024]{1,2,0:T(8,128)(2,1)} %divide_convert_fusion, bf16[1024,1024]{1,0:T(8,128)(2,1)} %param.26), kind=kOutput, calls=%fused_computation.34 | convolution fusion | flops 17196638208 | bytes 54558720 | tf_op jit(solution)/shard_map/bnv,vd->bnd/dot_general | solution.py:19
  333.3 13.8 %multiply_reduce_fusion.1 = f32[16,512]{1,0:T(8,128)S(1)} fusion(f32[16,512,1024]{2,1,0:T(8,128)} %get-tuple-element.66, f32[16,512]{1,0:T(8,128)S(1)} %broadcast_multiply_fusion.1, f32[512,1024]{1,0:T(8,128)} %param.18), kind=kLoop, calls=%fused_computation.31 | loop fusion | flops 33546240 | bytes 35717120 | tf_op jit(solution)/shard_map/jvp()/reduce_sum | solution.py:14
  347.2 0.6 copy-done.25
  347.8 31.7 %fusion.45 = f32[16,512,1024]{2,1,0:T(8,128)} fusion(bf16[1024,1024]{1,0:T(8,128)(2,1)S(1)} %copy-done, f32[16,512,1024]{2,1,0:T(8,128)} %get-tuple-element.66, f32[1024]{0:T(1024)S(1)} %copy-done.54, f32[1024]{0:T(1024)S(1)} %copy-done.40, f32[16,512]{1,0:T(8,128)S(1)} %fusion.57, f32[16,512]{1,0:T(8,128)S(1)} %broadcast_multiply_fusion.1, ...), kind=kOutput, calls=%fused_computation.81 | convolution fusion | flops 17230200832 | bytes 71376896 | tf_op jit(solution)/shard_map/bnd,de->bne/dot_general | solution.py:19
  379.5 29.1 %convolution_bitcast_fusion = f32[1024,1024]{1,0:T(8,128)} fusion(bf16[16,512,1024]{2,1,0:T(8,128)(2,1)} %param.33, f32[16,512,1024]{2,1,0:T(8,128)} %fusion.45, f32[1024]{0:T(1024)S(1)} %copy-done.57), kind=kOutput, calls=%fused_computation.75 | convolution fusion | flops 17263755264 | bytes 54530048 | tf_op jit(solution)/shard_map/bne,bnd->ed/dot_general | solution.py:19
  408.6 47.4 %fusion.68 = (f32[1024]{0:T(1024)}, bf16[16,512,1024]{2,1,0:T(8,128)(2,1)}) fusion(f32[16,512,1024]{2,1,0:T(8,128)} %fusion.45, f32[1024]{0:T(1024)S(1)} %copy-done.57, bf16[16,512,1024]{2,1,0:T(8,128)(2,1)} %param.33, bf16[1024,1024]{1,0:T(8,128)(2,1)S(1)} %copy-done.47), kind=kOutput, calls=%fused_computation.119 | convolution fusion | flops 17381195776 | bytes 69214208 | tf_op jit(solution)/shard_map/bnd,ed->bne/dot_general | solution.py:19
  456.0 30.2 %convert_reduce_fusion = (f32[1024]{0:T(1024)}, f32[16,512]{1,0:T(8,128)S(1)}, bf16[16,512,1024]{2,1,0:T(8,128)(2,1)}) fusion(f32[1024]{0:T(1024)S(1)} %copy-done.40, f32[16,512]{1,0:T(8,128)S(1)} %broadcast_multiply_fusion.1, f32[16,512,1024]{2,1,0:T(8,128)} %get-tuple-element.66, f32[512,1024]{1,0:T(8,128)} %param.18, bf16[1024,1024]{1,0:T(8,128)(2,1)S(1)} %copy-done, ...), kind=kOutput, calls=%fused_computation.1 | convolution fusion | flops 17246969856 | bytes 71376896 | tf_op jit(solution)/shard_map/bne,de->bnd/dot_general | solution.py:19
  486.3 21.6 %fusion.61 = f32[16,512]{1,0:T(8,128)S(1)} fusion(f32[16,512]{1,0:T(8,128)S(1)} %multiply_multiply_fusion.3, f32[16,512]{1,0:T(8,128)S(1)} %broadcast_multiply_fusion.1, f32[16,512,1024]{2,1,0:T(8,128)} %get-tuple-element.66, f32[512,1024]{1,0:T(8,128)} %param.18, f32[16,512]{1,0:T(8,128)S(1)} %copy-done.19, f32[1024]{0:T(1024)S(1)} %copy-done.40, ...), kind=kLoop, calls=%fused_computation.117 | loop fusion | flops 75489280 | bytes 52563968 | tf_op jit(solution)/shard_map/transpose(jvp())/reduce_sum | solution.py:13
  507.9 0.4 copy-done.5
  508.3 31.4 %fusion.12 = (f32[1024]{0:T(1024)}, f32[512,1024]{1,0:T(8,128)}, f32[1024]{0:T(1024)}, bf16[16,512,1024]{2,1,0:T(8,128)(2,1)}) fusion(bf16[16,512,1024]{2,1,0:T(8,128)(2,1)S(1)} %copy-done.5, f32[16,512,1024]{2,1,0:T(8,128)} %get-tuple-element.66, f32[16,512]{1,0:T(8,128)S(1)} %copy-done.19, f32[16,512]{1,0:T(8,128)S(1)} %broadcast_multiply_fusion.1, ...), kind=kLoop, calls=%fused_computation.22 | loop fusion | flops 142080000 | bytes 88223744 | tf_op jit(solution)/shard_map/transpose(jvp())/reduce_sum | solution.py:15
  539.7 24.1 %convolution_bitcast_fusion.1 = f32[1024,1024]{1,0:T(8,128)} fusion(bf16[16,512,1024]{1,2,0:T(8,128)(2,1)} %divide_convert_fusion, bf16[16,512,1024]{2,1,0:T(8,128)(2,1)} %get-tuple-element.62), kind=kOutput, calls=%fused_computation.76 | convolution fusion | flops 17179869184 | bytes 37748736 | tf_op jit(solution)/shard_map/bnv,bnd->vd/dot_general | solution.py:19
  563.8 27.4 %convolution_convert_fusion.4 = bf16[16,512,1024]{2,1,0:T(8,128)(2,1)} fusion(bf16[16,512,1024]{2,1,0:T(8,128)(2,1)} %get-tuple-element.62, bf16[1024,1024]{1,0:T(8,128)(2,1)} %param.26), kind=kOutput, calls=%fused_computation.68 | convolution fusion | flops 17188257792 | bytes 35651584 | tf_op jit(solution)/shard_map/bnd,vd->bnv/dot_general | solution.py:19
  591.2 43.9 %multiply_reduce_fusion = (f32[16,512]{1,0:T(8,128)S(1)}, f32[16,512,1024]{1,2,0:T(8,128)}) fusion(f32[16,512]{1,0:T(8,128)S(1)} %copy-done.24, f32[16,512]{1,0:T(8,128)S(1)} %copy-done.22, f32[16,1024,512]{2,1,0:T(8,128)} %get-tuple-element.64, bf16[16,512,1024]{2,1,0:T(8,128)(2,1)} %convolution_convert_fusion.4, ...), kind=kOutput, calls=%fused_computation.27 | convolution fusion | flops 17221804032 | bytes 117538816 | tf_op jit(solution)/shard_map/bnv,bmv->bnm/dot_general | solution.py:19
  635.1 35.0 %convolution_convert_fusion = bf16[16,1024,1024]{2,1,0:T(8,128)(2,1)} fusion(bf16[16,512,1024]{2,1,0:T(8,128)(2,1)} %convolution_convert_fusion.4, f32[16,1024,512]{2,1,0:T(8,128)} %get-tuple-element.64, f32[16,512]{1,0:T(8,128)S(1)} %copy-done.24, f32[16,512]{1,0:T(8,128)S(1)} %copy-done.22), kind=kOutput, calls=%fused_computation.50 | convolution fusion | flops 17230200832 | bytes 83951616 | tf_op jit(solution)/shard_map/bnm,bnv->bmv/dot_general | solution.py:19
  670.1 3.5 psum.121
  673.5 27.9 %multiply_convert_fusion = bf16[16,512,1024]{1,2,0:T(8,128)(2,1)} fusion(f32[16,512,1024]{1,2,0:T(8,128)} %get-tuple-element.69, f32[16,512]{1,0:T(8,128)S(1)} %psum.121, f32[16,512]{1,0:T(8,128)S(1)} %copy-done.24, f32[16,512]{1,0:T(8,128)S(1)} %copy-done.22, f32[16,1024,512]{2,1,0:T(8,128)} %get-tuple-element.64), kind=kLoop, calls=%fused_computation.26 | loop fusion | flops 58720256 | bytes 83984384 | tf_op jit(solution)/shard_map/convert_element_type | solution.py:75
  701.4 24.7 %bitcast_convert_fusion = bf16[512,1024]{1,0:T(8,128)(2,1)S(1)} fusion(bf16[16,512,1024]{1,2,0:T(8,128)(2,1)} %multiply_convert_fusion, bf16[16,1024,1024]{2,1,0:T(8,128)(2,1)} %convolution_convert_fusion.3), kind=kOutput, calls=%fused_computation.77 | convolution fusion | flops 17180393472 | bytes 51380224 | tf_op jit(solution)/shard_map/bnm,bmk->nk/dot_general | solution.py:19
  726.1 2.6 fusion.69
  728.8 3.5 fusion.60
  732.3 27.4 %convolution_convert_fusion.1 = bf16[16,1024,1024]{2,1,0:T(8,128)(2,1)} fusion(bf16[16,512,1024]{1,2,0:T(8,128)(2,1)} %multiply_convert_fusion, bf16[512,1024,1]{1,0,2:T(8,128)(2,1)S(1)} %copy-done.62), kind=kOutput, calls=%fused_computation.51 | convolution fusion | flops 17196646400 | bytes 51380224 | tf_op jit(solution)/shard_map/bnm,nk->bmk/dot_general | solution.py:19
  759.8 31.4 %convolution_bitcast_fusion.3 = f32[261,1024]{1,0:T(8,128)} fusion(bf16[16,1024,1024]{2,1,0:T(8,128)(2,1)} %convolution_convert_fusion.1, f32[261]{0:T(512)S(1)} %copy-done.60, f32[261]{0:T(512)S(1)} %copy-done.43, f32[16,1024]{1,0:T(8,128)S(1)} %copy-done.15, f32[16,1024]{1,0:T(8,128)S(1)} %copy-done.11, bf16[16,1024,261]{1,0,2:T(8,128)(2,1)} %param.17), kind=kOutput, calls=%fused_computation.93 | convolution fusion | flops 8783364096 | bytes 43309096 | tf_op jit(solution)/shard_map/bmc,bmk->ck/dot_general | solution.py:19
  791.2 18.8 %fusion.53 = f32[16,1024,261]{1,2,0:T(8,128)} fusion(bf16[16,1024,1024]{2,1,0:T(8,128)(2,1)} %convolution_convert_fusion.1, bf16[261,1024]{1,0:T(8,128)(2,1)S(1)} %copy-done.49), kind=kOutput, calls=%fused_computation.97 | convolution fusion | flops 8757706752 | bytes 51193856 | tf_op jit(solution)/shard_map/bmk,ck->bmc/dot_general | solution.py:19
  810.0 31.1 %convolution_bitcast_fusion.2 = f32[261,1024]{1,0:T(8,128)} fusion(bf16[16,1024,1024]{2,1,0:T(8,128)(2,1)} %convolution_convert_fusion, f32[261]{0:T(512)S(1)} %copy-done.60, f32[261]{0:T(512)S(1)} %copy-done.43, f32[16,1024]{1,0:T(8,128)S(1)} %copy-done.15, f32[16,1024]{1,0:T(8,128)S(1)} %copy-done.11, bf16[16,1024,261]{1,0,2:T(8,128)(2,1)} %param.17), kind=kOutput, calls=%fused_computation.92 | convolution fusion | flops 8783364096 | bytes 43309096 | tf_op jit(solution)/shard_map/bmc,bmv->cv/dot_general | solution.py:19
  841.1 0.0 all-reduce.10.cloned.1.call-update
  841.1 0.0 all-reduce.12.cloned.1.call-start
  841.2 28.9 %fusion.39 = f32[1024,1024]{1,0:T(8,128)} fusion(bf16[16,512,1024]{2,1,0:T(8,128)(2,1)} %get-tuple-element.72, f32[16,512,1024]{2,1,0:T(8,128)} %get-tuple-element.66, f32[1024]{0:T(1024)S(1)} %copy-done.55, f32[1024]{0:T(1024)S(1)} %copy-done.41, f32[16,512]{1,0:T(8,128)S(1)} %copy-done.20, f32[16,512]{1,0:T(8,128)S(1)} %copy-done.17, ...), kind=kOutput, calls=%fused_computation.74 | convolution fusion | flops 17230200832 | bytes 56696832 | tf_op jit(solution)/shard_map/bnd,bne->de/dot_general | solution.py:19
  870.1 0.0 all-reduce.12.cloned.1.call-update
  870.1 27.1 %convert_reduce_fusion.2 = (f32[261]{0:T(512)S(1)}, f32[16,1024]{1,0:T(8,128)S(1)}, bf16[16,1024,261]{1,2,0:T(8,128)(2,1)}) fusion(f32[261]{0:T(512)S(1)} %copy-done.43, f32[16,1024]{1,0:T(8,128)S(1)} %copy-done.11, bf16[16,1024,261]{1,0,2:T(8,128)(2,1)} %param.17, f32[16,1024,261]{1,2,0:T(8,128)} %fusion.53, ...), kind=kOutput, calls=%fused_computation.36 | convolution fusion | flops 8796176384 | bytes 68431912 | tf_op jit(solution)/shard_map/bmv,cv->bmc/dot_general | solution.py:19
  897.4 26.4 %fusion.29 = (f32[261]{0:T(512)S(1)}, f32[16,1024]{1,0:T(8,128)S(1)}) fusion(bf16[16,1024,261]{1,2,0:T(8,128)(2,1)} %get-tuple-element.70, f32[16,1024]{1,0:T(8,128)S(1)} %copy-done.15, f32[16,1024]{1,0:T(8,128)S(1)} %copy-done.11, bf16[16,1024,261]{1,0,2:T(8,128)(2,1)S(1)} %bitcast.101, f32[16,1024]{1,0:T(8,128)S(1)} %multiply_multiply_fusion.2, ...), kind=kLoop, calls=%fused_computation.60 | loop fusion | flops 51298044 | bytes 17369128 | tf_op jit(solution)/shard_map/transpose(jvp())/reduce_sum | solution.py:15
  924.0 21.9 %add_convert_fusion.1 = bf16[16,1024,261]{1,2,0:T(8,128)(2,1)} fusion(bf16[16,1024,261]{1,2,0:T(8,128)(2,1)S(1)} %bitcast.103, f32[16,1024]{1,0:T(8,128)S(1)} %negate_multiply_fusion, f32[16,1024]{1,0:T(8,128)S(1)} %multiply_multiply_fusion.2, f32[261]{0:T(512)S(1)} %copy-done.43, f32[16,1024]{1,0:T(8,128)S(1)} %copy-done.15, f32[16,1024]{1,0:T(8,128)S(1)} %copy-done.11, ...), kind=kLoop, calls=%fused_computation.61 | loop fusion | flops 42762240 | bytes 25920532 | tf_op jit(solution)/shard_map/convert_element_type | solution.py:89
  945.9 11.9 copy.43
  957.8 24.5 %all-reduce = (f32[261]{0:T(512)}, f32[261]{0:T(512)}) all-reduce(f32[261]{0:T(512)S(1)} %get-tuple-element.36, f32[261]{0:T(512)S(1)} %get-tuple-element.41), channel_id=1, replica_groups=mesh['dp'=4,'cp'=2] {'dp','cp'}, use_global_device_ids=true, to_apply=%region_23.0 | all-reduce | flops 522 | bytes 4176 | tf_op jit(solution)/shard_map/psum | solution.py:87
  982.3 17.7 %all-reduce.2 = (f32[1024]{0:T(1024)}, f32[1024]{0:T(1024)}, f32[1024]{0:T(1024)}, f32[1024]{0:T(1024)}) all-reduce(f32[1024]{0:T(1024)S(1)} %copy-done.35, f32[1024]{0:T(1024)S(1)} %copy-done.45, f32[1024]{0:T(1024)S(1)} %copy-done.44, f32[1024]{0:T(1024)S(1)} %copy-done.36), channel_id=1, replica_groups=mesh['dp'=4,'cp'=2] {'dp'}, use_global_device_ids=true, to_apply=%region_33.0 | all-reduce | flops 4096 | bytes 32768 | tf_op jit(solution)/shard_map/psum | solution.py:71
  1000.1 41.2 %add_add_fusion.1 = f32[16,512,1024]{2,1,0:T(8,128)} fusion(f32[16,512,1024]{2,1,0:T(8,128)} %get-tuple-element.66, f32[1024]{0:T(1024)S(1)} %copy-done.56, f32[512,1024]{1,0:T(8,128)S(1)} %copy-done.4, bf16[1024,1024]{1,0:T(8,128)(2,1)} %param.31, f32[16,512,1024]{2,1,0:T(8,128)} %fusion.45, f32[1024]{0:T(1024)S(1)} %copy-done.58), kind=kOutput, calls=%fused_computation.28 | convolution fusion | flops 17288921088 | bytes 104865792 | tf_op jit(solution)/shard_map/bne,ed->bnd/dot_general | solution.py:19
  1041.3 3.0 multiply_reduce_fusion.2
  1044.4 3.5 fusion.67
  1047.9 179.9 %all-reduce.12.cloned.1.call-done = (f32[512,1024]{1,0:T(8,128)}, f32[1024,1024]{1,0:T(8,128)}, f32[1024,1024]{1,0:T(8,128)}, f32[1024,1024]{1,0:T(8,128)}) async-done(((f32[512,1024]{1,0:T(8,128)}, f32[1024,1024]{1,0:T(8,128)}, f32[1024,1024]{1,0:T(8,128)}, f32[1024,1024]{1,0:T(8,128)}), (f32[512,1024]{1,0:T(8,128)}, f32[1024,1024]{1,0:T(8,128)}, f32[1024,1024]{1,0:T(8,128)}, ...) | async-done | bytes 14680080 | tf_op jit(solution)/shard_map/psum | solution.py:71
  1227.8 4.0 add_add_fusion.4
  1231.7 5.6 copy.71
  1237.3 2.3 copy.72
  1239.7 1.0 copy.73
  1240.6 2.0 copy.74
  1242.7 2.0 copy.75
  1244.7 2.0 copy.76
  (155 shorter events, 0.5 us)
Async XLA Ops:
  7.2 340.6 %copy-start = (bf16[1024,1024]{1,0:T(8,128)(2,1)S(1)}, bf16[1024,1024]{1,0:T(8,128)(2,1)}, u32[]{:S(2)}) copy-start(bf16[1024,1024]{1,0:T(8,128)(2,1)} %param.29) | copy-start | bytes 6291460
  7.2 20.7 %slice-start = ((s8[8552448]{0:T(1024)(128)(4,1)}), s8[163840]{0:T(1024)(128)(4,1)S(1)}, s32[]{:S(2)}) async-start(s8[8552448]{0:T(1024)(128)(4,1)} %bitcast.98), calls=%async_computation.3 | async-start | bytes 327680
  7.2 20.7 %copy-start.42 = (f32[261]{0:T(512)S(1)}, f32[261]{0:T(512)}, u32[]{:S(2)}) copy-start(f32[261]{0:T(512)} %param.19) | copy-start | bytes 3136
  7.2 20.7 %copy-start.59 = (f32[261]{0:T(512)S(1)}, f32[261]{0:T(512)}, u32[]{:S(2)}) copy-start(f32[261]{0:T(512)} %param.20) | copy-start | bytes 3136
  7.3 279.9 %all-reduce.8.cloned.1.call-start = ((), (), s32[]{:S(2)}) async-start(), calls=%async_computation | async-start | bytes 67108864 | tf_op jit(solution)/shard_map/psum | solution.py:44
  9.2 96.9 %copy-start.27 = (f32[512]{0:T(512)}, f32[512]{0:T(512)S(1)}, u32[]{:S(2)}) copy-start(f32[512]{0:T(512)S(1)} %broadcast_multiply_fusion.2) | copy-start | bytes 6148
  11.2 55.9 %copy-start.33 = (f32[512]{0:T(512)}, f32[512]{0:T(512)S(1)}, u32[]{:S(2)}) copy-start(f32[512]{0:T(512)S(1)} %multiply_reduce_fusion.4) | copy-start | bytes 6148
  11.2 94.9 %copy-start.30 = (f32[512]{0:T(512)}, f32[512]{0:T(512)S(1)}, u32[]{:S(2)}) copy-start(f32[512]{0:T(512)S(1)} %fusion.58) | copy-start | bytes 6148
  19.4 47.7 %copy-start.10 = (f32[16,1024]{1,0:T(8,128)}, f32[16,1024]{1,0:T(8,128)S(1)}, u32[]{:S(2)}) copy-start(f32[16,1024]{1,0:T(8,128)S(1)} %broadcast_multiply_fusion) | copy-start | bytes 196612
  27.9 39.1 %copy-start.12 = (f32[16,1024]{1,0:T(8,128)}, f32[16,1024]{1,0:T(8,128)S(1)}, u32[]{:S(2)}) copy-start(f32[16,1024]{1,0:T(8,128)S(1)} %fusion.27) | copy-start | bytes 196612
  28.0 39.0 %copy-start.14 = (f32[16,1024]{1,0:T(8,128)}, f32[16,1024]{1,0:T(8,128)S(1)}, u32[]{:S(2)}) copy-start(f32[16,1024]{1,0:T(8,128)S(1)} %fusion.56) | copy-start | bytes 196612
  28.0 39.0 %copy-start.48 = (bf16[261,1024]{1,0:T(8,128)(2,1)S(1)}, bf16[261,1024]{1,0:T(8,128)(2,1)}, u32[]{:S(2)}) copy-start(bf16[261,1024]{1,0:T(8,128)(2,1)} %param.24) | copy-start | bytes 1603588
  67.1 39.1 %copy-start.2 = (f32[512,1024]{1,0:T(8,128)S(1)}, f32[512,1024]{1,0:T(8,128)}, u32[]{:S(2)}) copy-start(f32[512,1024]{1,0:T(8,128)} %param.18) | copy-start | bytes 6291460
  67.1 39.0 %copy-start.37 = (f32[1024]{0:T(1024)S(1)}, f32[1024]{0:T(1024)}, u32[]{:S(2)}) copy-start(f32[1024]{0:T(1024)} %param.21) | copy-start | bytes 12292
  67.1 39.0 %copy-start.52 = (f32[1024]{0:T(1024)S(1)}, f32[1024]{0:T(1024)}, u32[]{:S(2)}) copy-start(f32[1024]{0:T(1024)} %param.22) | copy-start | bytes 12292
  109.1 31.7 %copy-start.61 = (bf16[512,1024,1]{1,0,2:T(8,128)(2,1)}, bf16[512,1024,1]{1,0,2:T(8,128)(2,1)S(1)}, u32[]{:S(2)}) copy-start(bf16[512,1024,1]{1,0,2:T(8,128)(2,1)S(1)} %fusion.50) | copy-start | bytes 3145732
  144.8 41.5 %copy-start.21 = (f32[16,512]{1,0:T(8,128)}, f32[16,512]{1,0:T(8,128)S(1)}, u32[]{:S(2)}) copy-start(f32[16,512]{1,0:T(8,128)S(1)} %pmax.7) | copy-start | bytes 98308
  186.3 855.0 %all-reduce.10.cloned.1.call-start = ((), (), s32[]{:S(2)}) async-start(), calls=%async_computation.1 | async-start | bytes 16908288 | tf_op jit(solution)/shard_map/psum | solution.py:87
  207.4 97.7 %copy-start.23 = (f32[16,512]{1,0:T(8,128)}, f32[16,512]{1,0:T(8,128)S(1)}, u32[]{:S(2)}) copy-start(f32[16,512]{1,0:T(8,128)S(1)} %psum.120) | copy-start | bytes 98308
  333.3 174.6 %copy-start.16 = (f32[16,512]{1,0:T(8,128)}, f32[16,512]{1,0:T(8,128)S(1)}, u32[]{:S(2)}) copy-start(f32[16,512]{1,0:T(8,128)S(1)} %broadcast_multiply_fusion.1) | copy-start | bytes 98308
  347.8 31.7 %copy-start.18 = (f32[16,512]{1,0:T(8,128)}, f32[16,512]{1,0:T(8,128)S(1)}, u32[]{:S(2)}) copy-start(f32[16,512]{1,0:T(8,128)S(1)} %fusion.57) | copy-start | bytes 98308
  347.8 31.7 %copy-start.57 = (f32[1024]{0:T(1024)S(1)}, f32[1024]{0:T(1024)}, u32[]{:S(2)}) copy-start(f32[1024]{0:T(1024)} %param.30) | copy-start | bytes 12292
  379.5 29.1 %copy-start.47 = (bf16[1024,1024]{1,0:T(8,128)(2,1)S(1)}, bf16[1024,1024]{1,0:T(8,128)(2,1)}, u32[]{:S(2)}) copy-start(bf16[1024,1024]{1,0:T(8,128)(2,1)} %param.31) | copy-start | bytes 6291460
  456.0 30.2 %copy-start.26 = (f32[16,512]{1,0:T(8,128)S(1)}, f32[16,512]{1,0:T(8,128)}, u32[]{:S(2)}) copy-start(f32[16,512]{1,0:T(8,128)} %copy-done.25) | copy-start | bytes 98308
  456.0 30.2 %copy-start.19 = (f32[16,512]{1,0:T(8,128)S(1)}, f32[16,512]{1,0:T(8,128)}, u32[]{:S(2)}) copy-start(f32[16,512]{1,0:T(8,128)} %copy-done.18) | copy-start | bytes 98308
  486.2 21.6 %copy-start.3 = (f32[512,1024]{1,0:T(8,128)S(1)}, f32[512,1024]{1,0:T(8,128)}, u32[]{:S(2)}) copy-start(f32[512,1024]{1,0:T(8,128)} %param.18) | copy-start | bytes 6291460
  486.3 22.0 %copy-start.5 = (bf16[16,512,1024]{2,1,0:T(8,128)(2,1)S(1)}, bf16[16,512,1024]{2,1,0:T(8,128)(2,1)}, u32[]{:S(2)}) copy-start(bf16[16,512,1024]{2,1,0:T(8,128)(2,1)} %get-tuple-element.67) | copy-start | bytes 50331652
  563.8 27.4 %copy-start.22 = (f32[16,512]{1,0:T(8,128)S(1)}, f32[16,512]{1,0:T(8,128)}, u32[]{:S(2)}) copy-start(f32[16,512]{1,0:T(8,128)} %copy-done.21) | copy-start | bytes 98308
  563.8 27.4 %copy-start.24 = (f32[16,512]{1,0:T(8,128)S(1)}, f32[16,512]{1,0:T(8,128)}, u32[]{:S(2)}) copy-start(f32[16,512]{1,0:T(8,128)} %copy-done.23) | copy-start | bytes 98308
  701.4 24.7 %copy-start.46 = (bf16[1024,1024]{1,0:T(8,128)(2,1)S(1)}, bf16[1024,1024]{1,0:T(8,128)(2,1)}, u32[]{:S(2)}) copy-start(bf16[1024,1024]{1,0:T(8,128)(2,1)} %param.23) | copy-start | bytes 6291460
  701.4 27.4 %copy-start.4 = (f32[512,1024]{1,0:T(8,128)S(1)}, f32[512,1024]{1,0:T(8,128)}, u32[]{:S(2)}) copy-start(f32[512,1024]{1,0:T(8,128)} %param.18) | copy-start | bytes 6291460
  701.4 27.4 %copy-start.28 = (f32[512]{0:T(512)S(1)}, f32[512]{0:T(512)}, u32[]{:S(2)}) copy-start(f32[512]{0:T(512)} %copy-done.27) | copy-start | bytes 6148
  701.4 27.4 %copy-start.31 = (f32[512]{0:T(512)S(1)}, f32[512]{0:T(512)}, u32[]{:S(2)}) copy-start(f32[512]{0:T(512)} %copy-done.30) | copy-start | bytes 6148
  701.4 27.4 %copy-start.38 = (f32[1024]{0:T(1024)S(1)}, f32[1024]{0:T(1024)}, u32[]{:S(2)}) copy-start(f32[1024]{0:T(1024)} %param.21) | copy-start | bytes 12292
  701.4 27.3 %copy-start.53 = (f32[1024]{0:T(1024)S(1)}, f32[1024]{0:T(1024)}, u32[]{:S(2)}) copy-start(f32[1024]{0:T(1024)} %param.22) | copy-start | bytes 12292
  732.3 27.5 %copy-start.11 = (f32[16,1024]{1,0:T(8,128)S(1)}, f32[16,1024]{1,0:T(8,128)}, u32[]{:S(2)}) copy-start(f32[16,1024]{1,0:T(8,128)} %copy-done.10) | copy-start | bytes 196612
  732.3 27.5 %copy-start.15 = (f32[16,1024]{1,0:T(8,128)S(1)}, f32[16,1024]{1,0:T(8,128)}, u32[]{:S(2)}) copy-start(f32[16,1024]{1,0:T(8,128)} %copy-done.14) | copy-start | bytes 196612
  732.3 27.5 %copy-start.43 = (f32[261]{0:T(512)S(1)}, f32[261]{0:T(512)}, u32[]{:S(2)}) copy-start(f32[261]{0:T(512)} %param.19) | copy-start | bytes 3136
  732.3 27.5 %copy-start.60 = (f32[261]{0:T(512)S(1)}, f32[261]{0:T(512)}, u32[]{:S(2)}) copy-start(f32[261]{0:T(512)} %param.20) | copy-start | bytes 3136
  759.8 31.5 %copy-start.49 = (bf16[261,1024]{1,0:T(8,128)(2,1)S(1)}, bf16[261,1024]{1,0:T(8,128)(2,1)}, u32[]{:S(2)}) copy-start(bf16[261,1024]{1,0:T(8,128)(2,1)} %param.24) | copy-start | bytes 1603588
  810.0 31.2 %copy-start.17 = (f32[16,512]{1,0:T(8,128)S(1)}, f32[16,512]{1,0:T(8,128)}, u32[]{:S(2)}) copy-start(f32[16,512]{1,0:T(8,128)} %copy-done.16) | copy-start | bytes 98308
  810.0 31.2 %copy-start.20 = (f32[16,512]{1,0:T(8,128)S(1)}, f32[16,512]{1,0:T(8,128)}, u32[]{:S(2)}) copy-start(f32[16,512]{1,0:T(8,128)} %copy-done.18) | copy-start | bytes 98308
  810.0 31.2 %copy-start.41 = (f32[1024]{0:T(1024)S(1)}, f32[1024]{0:T(1024)}, u32[]{:S(2)}) copy-start(f32[1024]{0:T(1024)} %param.27) | copy-start | bytes 12292
  810.0 31.2 %copy-start.55 = (f32[1024]{0:T(1024)S(1)}, f32[1024]{0:T(1024)}, u32[]{:S(2)}) copy-start(f32[1024]{0:T(1024)} %param.28) | copy-start | bytes 12292
  841.1 29.0 %copy-start.51 = (bf16[261,1024]{1,0:T(8,128)(2,1)S(1)}, bf16[261,1024]{1,0:T(8,128)(2,1)}, u32[]{:S(2)}) copy-start(bf16[261,1024]{1,0:T(8,128)(2,1)} %param.25) | copy-start | bytes 1603588
  841.1 386.7 %all-reduce.12.cloned.1.call-start = ((), (), s32[]{:S(2)}) async-start(), calls=%async_computation.2 | async-start | bytes 29360128 | tf_op jit(solution)/shard_map/psum | solution.py:71
  870.1 27.3 %slice-start.3 = ((s8[8552448]{0:T(1024)(128)(4,1)}), s8[163840]{0:T(1024)(128)(4,1)S(1)}, s32[]{:S(2)}) async-start(s8[8552448]{0:T(1024)(128)(4,1)} %bitcast.100), calls=%async_computation.6 | async-start | bytes 327680
  870.1 27.2 %copy-start.13 = (f32[16,1024]{1,0:T(8,128)S(1)}, f32[16,1024]{1,0:T(8,128)}, u32[]{:S(2)}) copy-start(f32[16,1024]{1,0:T(8,128)} %copy-done.12) | copy-start | bytes 196612
  870.1 27.2 %slice-start.4 = ((s8[8552448]{0:T(1024)(128)(4,1)}), s8[4194304]{0:T(1024)(128)(4,1)S(1)}, s32[]{:S(2)}) async-start(s8[8552448]{0:T(1024)(128)(4,1)} %bitcast.100), calls=%async_computation.7 | async-start | bytes 8388608
  870.1 27.2 %slice-start.5 = ((s8[8552448]{0:T(1024)(128)(4,1)}), s8[4194304]{0:T(1024)(128)(4,1)S(1)}, s32[]{:S(2)}) async-start(s8[8552448]{0:T(1024)(128)(4,1)} %bitcast.100), calls=%async_computation.8 | async-start | bytes 8388608
  897.3 26.6 %slice-start.6 = ((s8[8650752]{0:T(1024)(128)(4,1)}), s8[4194304]{0:T(1024)(128)(4,1)S(1)}, s32[]{:S(2)}) async-start(s8[8650752]{0:T(1024)(128)(4,1)} %bitcast.102), calls=%async_computation.9 | async-start | bytes 8388608
  897.4 26.5 %slice-start.7 = ((s8[8650752]{0:T(1024)(128)(4,1)}), s8[4194304]{0:T(1024)(128)(4,1)S(1)}, s32[]{:S(2)}) async-start(s8[8650752]{0:T(1024)(128)(4,1)} %bitcast.102), calls=%async_computation.10 | async-start | bytes 8388608
  897.4 26.5 %slice-start.8 = ((s8[8650752]{0:T(1024)(128)(4,1)}), s8[262144]{0:T(1024)(128)(4,1)S(1)}, s32[]{:S(2)}) async-start(s8[8650752]{0:T(1024)(128)(4,1)} %bitcast.102), calls=%async_computation.11 | async-start | bytes 524288
  923.9 58.4 %copy-start.35 = (f32[1024]{0:T(1024)S(1)}, f32[1024]{0:T(1024)}, u32[]{:S(2)}) copy-start(f32[1024]{0:T(1024)} %get-tuple-element.34) | copy-start | bytes 12292
  923.9 58.4 %copy-start.36 = (f32[1024]{0:T(1024)S(1)}, f32[1024]{0:T(1024)}, u32[]{:S(2)}) copy-start(f32[1024]{0:T(1024)} %get-tuple-element.38) | copy-start | bytes 12292
  923.9 58.4 %copy-start.44 = (f32[1024]{0:T(1024)S(1)}, f32[1024]{0:T(1024)}, u32[]{:S(2)}) copy-start(f32[1024]{0:T(1024)} %get-tuple-element.71) | copy-start | bytes 12292
  923.9 58.4 %copy-start.45 = (f32[1024]{0:T(1024)S(1)}, f32[1024]{0:T(1024)}, u32[]{:S(2)}) copy-start(f32[1024]{0:T(1024)} %get-tuple-element.39) | copy-start | bytes 12292
  923.9 76.1 %copy-start.56 = (f32[1024]{0:T(1024)S(1)}, f32[1024]{0:T(1024)}, u32[]{:S(2)}) copy-start(f32[1024]{0:T(1024)} %param.32) | copy-start | bytes 12292
  923.9 76.1 %copy-start.58 = (f32[1024]{0:T(1024)S(1)}, f32[1024]{0:T(1024)}, u32[]{:S(2)}) copy-start(f32[1024]{0:T(1024)} %param.30) | copy-start | bytes 12292
  1000.0 41.3 %copy-start.29 = (f32[512]{0:T(512)S(1)}, f32[512]{0:T(512)}, u32[]{:S(2)}) copy-start(f32[512]{0:T(512)} %copy-done.27) | copy-start | bytes 6148
  1000.0 41.3 %copy-start.32 = (f32[512]{0:T(512)S(1)}, f32[512]{0:T(512)}, u32[]{:S(2)}) copy-start(f32[512]{0:T(512)} %copy-done.30) | copy-start | bytes 6148
  1000.0 41.3 %copy-start.39 = (f32[1024]{0:T(1024)S(1)}, f32[1024]{0:T(1024)}, u32[]{:S(2)}) copy-start(f32[1024]{0:T(1024)} %param.21) | copy-start | bytes 12292
  1000.1 44.3 %copy-start.34 = (f32[512]{0:T(512)S(1)}, f32[512]{0:T(512)}, u32[]{:S(2)}) copy-start(f32[512]{0:T(512)} %copy-done.33) | copy-start | bytes 6148
  1041.3 198.3 %copy-start.9 = (f32[261,1024]{1,0:T(8,128)S(1)}, f32[261,1024]{1,0:T(8,128)}, u32[]{:S(2)}) copy-start(f32[261,1024]{1,0:T(8,128)} %get-tuple-element.84) | copy-start | bytes 3207172
  (11 other events, 141.5 us)
Sparse Core Ops, SparseCore 0:
  186.4 100.6 all-reduce.7
  841.2 117.6 all-reduce.9
  964.0 263.7 all-reduce.11
where the time goes:
time: 1260 us; the launch traced here: 1250 us
  matrix products  688 us (55%)
  waiting for transfers between devices  260 us (21%)
  other arithmetic  210 us (17%)
  blocking collectives  53.2 us (4%)
  local copies, waits for them, and re-layouts  28.2 us (2%)
  between operations  15 us (1%)
    dot_general x24, matrix products, contract(): jnp.einsum(einsum_form, lhs_arr, rhs_arr, preferred_element_type=ACC_TYPE)  688 us
    psum x1, waiting for transfers between devices, local_step(): lax.psum(mlp_grads, 'dp')  180 us
    psum x1, waiting for transfers between devices, local_step(): lax.psum((jnp.sum(weights, axis=-1, keepdims=True), contract('bnm,bmv->bn...  79.8 us
    reduce_sum x3, other arithmetic, layer_norm(): return centred * lax.rsqrt(variance + LN_EPS) * ln_gain + ln_shift  60.9 us
    unnamed x151, local copies, waits for them, and re-layouts  28.2 us
    convert_element_type x1, other arithmetic, local_step(): d_logits = (attn_probs * (d_probs - row_dot) * qk_scale).astype(LOW_TYPE)  27.9 us
  transfers between devices with their start and end apart: 3, of which 2 were waited for; matrix products, arithmetic and copies ran while one was open for 14% of the time, Pallas kernels for 0%

commit v1 on v0

v1 whole, which is shorter than its diff:
```python
import functools
import math

import jax
import jax.numpy as jnp
from jax import lax
from jax.experimental import pallas as pl
from jax.experimental.pallas import tpu as pltpu
from jax.sharding import PartitionSpec as P


LN_EPS = 1e-5
F32 = jnp.float32
BF16 = jnp.bfloat16
CH = 261
CPAD = 272
AXW = 384
ROW_GAP = 8
ACC_ROWS = 896
VEC_ROW = 784
SUM_LANE = 261
MAX_LANE = 262
INV_LANE = 263
LOG2E = math.log2(math.e)
GELU_A = math.sqrt(2.0 / math.pi)
GELU_B = 0.044715
VMEM_LIMIT = 60 * 1024 * 1024


def layer_norm(tensor, ln_gain, ln_shift):
    row_mean = jnp.mean(tensor, axis=-1, keepdims=True)
    centred = tensor - row_mean
    variance = jnp.mean(centred * centred, axis=-1, keepdims=True)
    return centred * lax.rsqrt(variance + LN_EPS) * ln_gain + ln_shift


def mm(lhs, rhs):
    return lax.dot_general(lhs, rhs, (((1,), (0,)), ((), ())), preferred_element_type=F32)


def mm_nt(lhs, rhs):
    return lax.dot_general(lhs, rhs, (((1,), (1,)), ((), ())), preferred_element_type=F32)


def mm_tn(lhs, rhs):
    return lax.dot_general(lhs, rhs, (((0,), (0,)), ((), ())), preferred_element_type=F32)


def params(semantics=1):
    return pltpu.CompilerParams(
        vmem_limit_bytes=VMEM_LIMIT, dimension_semantics=("arbitrary",) * semantics)


def cost(flops, nbytes):
    return pl.CostEstimate(flops=int(flops), bytes_accessed=int(nbytes), transcendentals=0)


def x_prep_kernel(gain_ref, shift_ref, x_ref, xn_ref, mean_ref, rstd_ref, rows_ref):
    nb = x_ref.shape[1]
    lanes = x_ref.shape[2]
    pitch = nb + ROW_GAP
    zero = jnp.zeros((nb, lanes), F32)

    def add_up(c, acc):
        return acc + x_ref[c].astype(F32)

    mean = lax.fori_loop(0, CH, add_up, zero, unroll=9) * (1.0 / CH)

    def add_sq(c, acc):
        d = x_ref[c].astype(F32) - mean
        return acc + d * d

    var = lax.fori_loop(0, CH, add_sq, zero, unroll=9) * (1.0 / CH)
    rstd = lax.rsqrt(var + LN_EPS)
    mean_ref[...] = mean
    rstd_ref[...] = rstd

    def put(c, carry):
        xn = (x_ref[c].astype(F32) - mean) * rstd * gain_ref[c] + shift_ref[c]
        rows_ref[pl.ds(pl.multiple_of(c * pitch, ROW_GAP), nb), :] = xn
        return carry

    lax.fori_loop(0, CH, put, 0, unroll=9)
    rows_ref[CH * pitch:CPAD * pitch, :] = jnp.zeros(((CPAD - CH) * pitch, lanes), F32)
    for b in range(nb):
        xn_ref[b] = rows_ref[pl.ds(b, CPAD, stride=pitch), :].astype(BF16)


def x_prep(x_cm, x_gain, x_shift):
    _, nb, m = x_cm.shape
    lanes = 128
    stat = pl.BlockSpec((nb, lanes), lambda i: (0, i))
    return pl.pallas_call(
        x_prep_kernel,
        grid=(m // lanes,),
        in_specs=[
            pl.BlockSpec(memory_space=pltpu.SMEM),
            pl.BlockSpec(memory_space=pltpu.SMEM),
            pl.BlockSpec((CH, nb, lanes), lambda i: (0, 0, i)),
        ],
        out_specs=[pl.BlockSpec((nb, CPAD, lanes), lambda i: (0, 0, i)), stat, stat],
        out_shape=[
            jax.ShapeDtypeStruct((nb, CPAD, m), BF16),
            jax.ShapeDtypeStruct((nb, m), F32),
            jax.ShapeDtypeStruct((nb, m), F32),
        ],
        scratch_shapes=[pltpu.VMEM((CPAD * (nb + ROW_GAP), lanes), F32)],
        compiler_params=params(),
        cost_estimate=cost(3e9, 4 * nb * CH * m),
        name="x_prep",
    )(x_gain, x_shift, x_cm)


def attn_fwd_kernel(base_ref, qp_ref, xn_ref, e_ref, ax_ref):
    xn = xn_ref[0]
    s = mm(qp_ref[...], xn)
    top = jnp.max(s, axis=1, keepdims=True)
    e = jnp.exp2(s - top)
    total = jnp.sum(e, axis=1, keepdims=True)
    e_low = e.astype(BF16)
    e_ref[0] = e_low
    ax = jnp.concatenate([mm_nt(e_low, xn), jnp.zeros((e.shape[0], AXW - CPAD), F32)], axis=1)
    lane = lax.broadcasted_iota(jnp.int32, ax.shape, 1)
    ax_ref[0] = jnp.where(lane == SUM_LANE, total, jnp.where(lane == MAX_LANE, top, ax))


def attn_fwd(base, qp, xn, half):
    n = qp.shape[0]
    m = xn.shape[2]
    return pl.pallas_call(
        attn_fwd_kernel,
        grid_spec=pltpu.PrefetchScalarGridSpec(
            num_scalar_prefetch=1,
            grid=(half,),
            in_specs=[
                pl.BlockSpec((n, CPAD), lambda i, base: (0, 0)),
                pl.BlockSpec((1, CPAD, m), lambda i, base: (base[0] + i, 0, 0)),
            ],
            out_specs=[
                pl.BlockSpec((1, n, m), lambda i, base: (i, 0, 0)),
                pl.BlockSpec((1, n, AXW), lambda i, base: (i, 0, 0)),
            ],
        ),
        out_shape=[
            jax.ShapeDtypeStruct((half, n, m), BF16),
            jax.ShapeDtypeStruct((half, n, AXW), F32),
        ],
        compiler_params=params(),
        cost_estimate=cost(4 * half * n * m * 512, half * n * m * 3),
        name="attn_fwd",
    )(base, qp, xn)


def combine(mine, other):
    top_a, top_b = mine[:, MAX_LANE:MAX_LANE + 1], other[:, MAX_LANE:MAX_LANE + 1]
    top = jnp.maximum(top_a, top_b)
    fa, fb = jnp.exp2(top_a - top), jnp.exp2(top_b - top)
    inv = 1.0 / (mine[:, SUM_LANE:SUM_LANE + 1] * fa + other[:, SUM_LANE:SUM_LANE + 1] * fb)
    ax = mine * (fa * inv) + other * (fb * inv)
    lane = lax.broadcasted_iota(jnp.int32, ax.shape, 1)
    return jnp.where(lane < CH, ax, 0.0), top, inv


def mlp_a_kernel(where_ref, axa_ref, axb_ref, z0_ref, wvo_ref, mg_ref, ms_ref, w1_ref, b1_ref, w2_ref, do_ref,
                 z1_ref, act_ref, dpre_ref, dw1_ref, dw2_ref, db1_ref):
    ax, _, _ = combine(axa_ref[0], axb_ref[0])
    z1 = z0_ref[...] + mm(ax[:, :CPAD].astype(BF16), wvo_ref[...])
    z1_ref[0] = z1
    h = layer_norm(z1, mg_ref[...], ms_ref[...]).astype(BF16)
    h_t = h.T
    d_out = do_ref[0]

    @pl.when(pl.program_id(0) == 0)
    def _():
        for ref in (dw1_ref, dw2_ref, db1_ref):
            ref[...] = jnp.zeros_like(ref)

    width = w1_ref.shape[1]
    step = 256
    for lo in range(0, width, step):
        cols = slice(lo, lo + step)
        pre = mm(h, w1_ref[:, cols]) + b1_ref[:, cols]
        d_act = mm_nt(d_out, w2_ref[cols, :]).astype(BF16).astype(F32)
        sq = pre * pre
        t = jnp.tanh(pre * (GELU_A + (GELU_A * GELU_B) * sq))
        half_t = 0.5 + 0.5 * t
        act = (pre * half_t).astype(BF16)
        slope = half_t + (0.5 * pre) * (1.0 - t * t) * (GELU_A + (3.0 * GELU_A * GELU_B) * sq)
        d_pre = d_act * slope
        db1_ref[:, cols] += jnp.sum(d_pre, axis=0, keepdims=True)
        d_pre_low = d_pre.astype(BF16)
        act_ref[0, :, cols] = act
        dpre_ref[0, :, cols] = d_pre_low
        dw1_ref[:, cols] += mm(h_t, d_pre_low)
        dw2_ref[cols, :] += mm(act.T, d_out)


def mlp_a(where, axa, axb, z0, wvo, mg, ms, w1, b1, w2, d_out):
    half, n, _ = axa.shape
    d = z0.shape[1]
    whole = lambda shape: pl.BlockSpec(shape, lambda i, base: (0,) * len(shape))
    per = lambda c: pl.BlockSpec((1, n, c), lambda i, base: (i, 0, 0))
    return pl.pallas_call(
        mlp_a_kernel,
        grid_spec=pltpu.PrefetchScalarGridSpec(
            num_scalar_prefetch=1,
            grid=(half,),
            in_specs=[per(AXW), per(AXW), whole((n, d)), whole((CPAD, d)), whole((1, d)), whole((1, d)),
                      whole((d, d)), whole((1, d)), whole((d, d)),
                      pl.BlockSpec((1, n, d), lambda i, base: (base[0] + i, 0, 0))],
            out_specs=[per(d), per(d), per(d), whole((d, d)), whole((d, d)), whole((1, d))],
        ),
        out_shape=[
            jax.ShapeDtypeStruct((half, n, d), F32),
            jax.ShapeDtypeStruct((half, n, d), BF16),
            jax.ShapeDtypeStruct((half, n, d), BF16),
            jax.ShapeDtypeStruct((d, d), F32),
            jax.ShapeDtypeStruct((d, d), F32),
            jax.ShapeDtypeStruct((1, d), F32),
        ],
        compiler_params=params(),
        cost_estimate=cost(2 * half * n * d * (4 * d + 512), half * n * d * 10),
        name="mlp_a",
    )(where, axa, axb, z0, wvo, mg, ms, w1, b1, w2, d_out)


def mlp_b_kernel(axa_ref, axb_ref, z1_ref, act_ref, dpre_ref, do_ref, wvo_ref, mg_ref, w1_ref, w2_ref, b2_ref, db1_ref, acc_in_ref,
                 z2_ref, full_ref, g_ref, acc_ref):
    ax, top, inv = combine(axa_ref[0], axb_ref[0])
    n, _ = z1_ref.shape[1:]
    z1 = z1_ref[0]
    z2 = z1 + mm(act_ref[0], w2_ref[...]) + b2_ref[...]
    z2_ref[0] = z2
    full_ref[0] = z2
    d_hid = mm_nt(dpre_ref[0], w1_ref[...]).astype(BF16).astype(F32)
    centred = z1 - jnp.mean(z1, axis=1, keepdims=True)
    rstd = lax.rsqrt(jnp.mean(centred * centred, axis=1, keepdims=True) + LN_EPS)
    hat = centred * rstd
    d_hat = d_hid * mg_ref[...]
    mean_a = jnp.mean(d_hat, axis=1, keepdims=True)
    mean_b = jnp.mean(d_hat * hat, axis=1, keepdims=True)
    d_out = do_ref[0].astype(F32)
    d_mid = d_out + rstd * (d_hat - mean_a - hat * mean_b)
    d_mid_low = d_mid.astype(BF16)

    @pl.when(pl.program_id(0) == 0)
    def _():
        acc_ref[...] = jnp.zeros_like(acc_ref) if acc_in_ref is None else acc_in_ref[...]
        if acc_in_ref is None:
            acc_ref[VEC_ROW + 3:VEC_ROW + 4, :] = db1_ref[...]

    p = mm(ax[:, :CPAD].astype(BF16).T, d_mid_low)
    acc_ref[0:n, :] += d_mid
    acc_ref[n:n + CPAD, :] += p
    acc_ref[VEC_ROW:VEC_ROW + 1, :] += jnp.sum(d_hid * hat, axis=0, keepdims=True)
    acc_ref[VEC_ROW + 1:VEC_ROW + 2, :] += jnp.sum(d_hid, axis=0, keepdims=True)
    acc_ref[VEC_ROW + 2:VEC_ROW + 3, :] += jnp.sum(d_out, axis=0, keepdims=True)
    d_ax = jnp.concatenate([mm_nt(d_mid_low, wvo_ref[...]), jnp.zeros((n, AXW - CPAD), F32)], axis=1)
    delta = jnp.sum(d_ax * ax, axis=1, keepdims=True)
    lane = lax.broadcasted_iota(jnp.int32, d_ax.shape, 1)
    g_ref[0] = jnp.where(lane == SUM_LANE, delta, jnp.where(lane == MAX_LANE, top, jnp.where(lane == INV_LANE, inv, d_ax)))


def mlp_b(base, axa, axb, z1, act, dpre, d_out, wvo, mg, w1, w2, b2, db1, start, count, acc_in, full_in):
    n = axa.shape[1]
    d = z1.shape[2]
    whole = lambda shape: pl.BlockSpec(shape, lambda i, base: (0,) * len(shape))
    part = lambda c: pl.BlockSpec((1, n, c), lambda i, base: (i + start, 0, 0))
    per = lambda c: pl.BlockSpec((1, n, c), lambda i, base: (i, 0, 0))
    shifted = pl.BlockSpec((1, n, d), lambda i, base: (base[0] + start + i, 0, 0))
    in_specs = [part(AXW), part(AXW), part(d), part(d), part(d), shifted, whole((CPAD, d)), whole((1, d)),
                whole((d, d)), whole((d, d)), whole((1, d)), whole((1, d))]
    args = [axa, axb, z1, act, dpre, d_out, wvo, mg, w1, w2, b2, db1]
    aliases = {}
    if acc_in is not None:
        in_specs += [whole((ACC_ROWS, d)), pl.BlockSpec(memory_space=pl.ANY)]
        args += [acc_in, full_in]
        aliases = {14: 1}

    def body(base_ref, *refs):
        mlp_b_kernel(*refs[:12], refs[12] if acc_in is not None else None, *refs[-4:])

    return pl.pallas_call(
        body,
        grid_spec=pltpu.PrefetchScalarGridSpec(
            num_scalar_prefetch=1,
            grid=(count,),
            in_specs=in_specs,
            out_specs=[per(d), shifted, per(AXW), whole((ACC_ROWS, d))],
        ),
        out_shape=[
            jax.ShapeDtypeStruct((count, n, d), F32),
            jax.ShapeDtypeStruct(d_out.shape, F32),
            jax.ShapeDtypeStruct((count, n, AXW), F32),
            jax.ShapeDtypeStruct((ACC_ROWS, d), F32),
        ],
        input_output_aliases=aliases,
        compiler_params=params(),
        cost_estimate=cost(2 * count * n * d * (2 * d + 800), count * n * d * 18),
        name="mlp_b",
    )(base, *args)


def places():
    core, chip = lax.axis_index('cp'), lax.axis_index('dp')
    x, y = lax.rem(chip, 2), chip // 2
    at_x = (y * 2 + (1 - x), core)
    at_y = ((1 - y) * 2 + x, core)
    return core, x, y, (chip, 1 - core), at_x, at_y


def meet(devices):
    barrier = pltpu.get_barrier_semaphore()
    for dev in devices:
        pl.semaphore_signal(barrier, inc=1, device_id=dev, device_id_type=pl.DeviceIdType.MESH)
    pl.semaphore_wait(barrier, len(devices))


def remote(src, dst, sems, k, dev):
    return pltpu.make_async_remote_copy(
        src_ref=src, dst_ref=dst, send_sem=sems[0].at[k], recv_sem=sems[1].at[k],
        device_id=dev, device_id_type=pl.DeviceIdType.MESH)


def rows(ref, start, size):
    return ref.at[pl.ds(pl.multiple_of(start, 8), size)]


def scatter_step(step, acc_ref, piece_ref, half_ref, rx0_ref, rx1_ref, rx2_ref, sems):
    half, quarter, eighth, part = (ACC_ROWS // k for k in (2, 4, 8, 16))
    core, x, y, at_core, at_x, at_y = places()
    p0 = remote(rows(acc_ref, (1 - core) * half, half), rx0_ref, sems, 0, at_core)
    p1a = remote(rows(half_ref, (1 - x) * eighth, eighth), rx1_ref.at[0], sems, 1, at_x)
    p1b = remote(rows(half_ref, quarter + (1 - y) * eighth, eighth), rx1_ref.at[1], sems, 2, at_y)
    a, b = x * eighth, quarter + y * eighth
    p2a = remote(rows(half_ref, a + (1 - y) * part, part), rx2_ref.at[0], sems, 3, at_y)
    p2b = remote(rows(half_ref, b + (1 - x) * part, part), rx2_ref.at[1], sems, 4, at_x)

    @pl.when(step == 0)
    def _():
        meet((at_core, at_x, at_y))
        p0.start()

    @pl.when(step == 2)
    def _():
        p0.wait()
        half_ref[...] = acc_ref[pl.ds(pl.multiple_of(core * half, 8), half), :] + rx0_ref[...]
        p1a.start()
        p1b.start()

    @pl.when(step == 5)
    def _():
        p1a.wait()
        p1b.wait()
        half_ref[pl.ds(pl.multiple_of(a, 8), eighth), :] += rx1_ref[0]
        half_ref[pl.ds(pl.multiple_of(b, 8), eighth), :] += rx1_ref[1]
        p2a.start()
        p2b.start()

    @pl.when(step == 7)
    def _():
        p2a.wait()
        p2b.wait()
        piece_ref[0] = half_ref[pl.ds(pl.multiple_of(a + y * part, 8), part), :] + rx2_ref[0]
        piece_ref[1] = half_ref[pl.ds(pl.multiple_of(b + x * part, 8), part), :] + rx2_ref[1]


def gather_step(step, piece_ref, out_ref, buf_ref, sems):
    half, quarter, eighth, part = (ACC_ROWS // k for k in (2, 4, 8, 16))
    core, x, y, at_core, at_x, at_y = places()
    own = core * half
    a, b = own + x * eighth, own + quarter + y * eighth

    def spread(start, size, k, dev):
        return remote(rows(buf_ref, start, size), rows(buf_ref, start, size), sems, k, dev)

    p3a = remote(piece_ref.at[0], rows(buf_ref, a + y * part, part), sems, 0, at_y)
    p3b = remote(piece_ref.at[1], rows(buf_ref, b + x * part, part), sems, 1, at_x)
    p4a = spread(a, eighth, 2, at_x)
    p4b = spread(b, eighth, 3, at_y)
    p5 = spread(own, half, 4, at_core)

    @pl.when(step == 0)
    def _():
        buf_ref[pl.ds(pl.multiple_of(a + y * part, 8), part), :] = piece_ref[0]
        buf_ref[pl.ds(pl.multiple_of(b + x * part, 8), part), :] = piece_ref[1]
        meet((at_core, at_x, at_y))
        p3a.start()
        p3b.start()

    @pl.when(step == 2)
    def _():
        p3a.wait()
        p3b.wait()
        p4a.start()
        p4b.start()

    @pl.when(step == 6)
    def _():
        p4a.wait()
        p4b.wait()
        p5.start()

    @pl.when(step == 7)
    def _():
        p5.wait()
        out_ref[...] = buf_ref[...]


def attn_bwd_body(ga_ref, gb_ref, ax_ref, e_ref, xn_ref, qpt_ref, t_in_ref, dxn_ref, t_ref):
    g = jnp.where(pl.program_id(0) < pl.num_programs(0) // 2, ga_ref[0], gb_ref[0])
    xn = xn_ref[0]
    e = e_ref[0]
    beta = jnp.exp2(ax_ref[0][:, MAX_LANE:MAX_LANE + 1] - g[:, MAX_LANE:MAX_LANE + 1]) * g[:, INV_LANE:INV_LANE + 1]
    lane = lax.broadcasted_iota(jnp.int32, g.shape, 1)
    scaled = g * beta
    d_low = jnp.where(lane < CH, scaled, 0.0)[:, :CPAD].astype(BF16)
    d_a = mm(d_low, xn)
    d_s = (e.astype(F32) * (d_a - scaled[:, SUM_LANE:SUM_LANE + 1])).astype(BF16)

    @pl.when(pl.program_id(0) == 0)
    def _():
        t_ref[...] = t_in_ref[...]

    t_ref[...] += mm_nt(xn, d_s)
    dxn_ref[0] = (mm(qpt_ref[...], d_s) + mm(d_low.T, e)).astype(BF16)


def bwd_scatter_kernel(*refs):
    step = pl.program_id(0)
    sems = refs[15:17]
    scatter_step(step, refs[7], refs[10], *refs[11:15], sems)
    attn_bwd_body(*refs[:7], *refs[8:10])


def bwd_gather_kernel(*refs):
    step = pl.program_id(0)
    sems = refs[13:15]
    gather_step(step, refs[7], refs[11], refs[12], sems)
    attn_bwd_body(*refs[:7], *refs[9:11])


def attn_bwd(own, ga, gb, ax, e, xn, qpt, t_in, travel, dxn_in):
    half, n, m = e.shape
    width = travel.shape[-1]
    whole = lambda shape: pl.BlockSpec(shape, lambda i: (0,) * len(shape))
    per = lambda c: pl.BlockSpec((1, n, c), lambda i: (i, 0, 0))

    def at(i):
        core = lax.axis_index('cp')
        return ((core if own else 1 - core) * half + i, 0, 0)

    shifted = pl.BlockSpec((1, CPAD, m), at)
    first = pl.BlockSpec((1, n, AXW), lambda i: (jnp.minimum(i, half // 2 - 1), 0, 0))
    second = pl.BlockSpec((1, n, AXW), lambda i: (jnp.maximum(i - half // 2, 0), 0, 0))
    in_specs = [first, second, per(AXW), per(m), shifted, whole((CPAD, n)), whole((CPAD, n)), whole(travel.shape)]
    out_specs = [shifted, whole((CPAD, n))]
    out_shape = [jax.ShapeDtypeStruct(xn.shape, BF16), jax.ShapeDtypeStruct((CPAD, n), F32)]
    args = [ga, gb, ax, e, xn, qpt, t_in, travel]
    eighth, part = ACC_ROWS // 8, ACC_ROWS // 16
    if own:
        kernel, aliases, count, ident = bwd_scatter_kernel, {}, 5, 1
        out_specs.append(whole((2, part, width)))
        out_shape.append(jax.ShapeDtypeStruct((2, part, width), F32))
        scratch = [pltpu.VMEM((ACC_ROWS // 2, width), F32), pltpu.VMEM((ACC_ROWS // 2, width), F32),
                   pltpu.VMEM((2, eighth, width), F32), pltpu.VMEM((2, part, width), F32)]
    else:
        kernel, aliases, count, ident = bwd_gather_kernel, {8: 0}, 5, 2
        in_specs.append(pl.BlockSpec(memory_space=pl.ANY))
        args.append(dxn_in)
        out_specs.append(whole((ACC_ROWS, width)))
        out_shape.append(jax.ShapeDtypeStruct((ACC_ROWS, width), F32))
        scratch = [pltpu.VMEM((ACC_ROWS, width), F32)]
    scratch += [pltpu.SemaphoreType.DMA((count,)), pltpu.SemaphoreType.DMA((count,))]
    return pl.pallas_call(
        kernel,
        grid=(half,),
        in_specs=in_specs,
        out_specs=out_specs,
        out_shape=out_shape,
        scratch_shapes=scratch,
        input_output_aliases=aliases,
        compiler_params=pltpu.CompilerParams(
            vmem_limit_bytes=VMEM_LIMIT, dimension_semantics=("arbitrary",), collective_id=ident, has_side_effects=True),
        cost_estimate=cost(8 * half * n * m * 512, half * n * m * 6),
        name="attn_bwd",
    )(*args)


def x_post_kernel(base_ref, gain_ref, x_ref, mean_ref, rstd_ref, dxn_ref, z2a_ref, z2b_ref, full_in_ref, dx_ref, sums_ref, full_ref,
                  rows_ref, dg_ref, ds_ref):
    nb, lanes = x_ref.shape[1:]
    pitch = CPAD + ROW_GAP
    early = pl.program_id(0) < pl.num_programs(0) // 2

    @pl.when(early)
    def _():
        full_ref[0] = z2a_ref[0]

    @pl.when(jnp.logical_not(early))
    def _():
        full_ref[0] = z2b_ref[0]

    for b in range(nb):
        rows_ref[b * pitch:b * pitch + CPAD, :] = dxn_ref[b].astype(F32)
    zero = jnp.zeros((nb, lanes), F32)
    mean = mean_ref[...]
    rstd = rstd_ref[...]

    @pl.when(pl.program_id(0) == 0)
    def _():
        dg_ref[...] = jnp.zeros_like(dg_ref)
        ds_ref[...] = jnp.zeros_like(ds_ref)

    def gather(c, acc):
        da, db = acc
        hat = (x_ref[c].astype(F32) - mean) * rstd
        dxn = rows_ref[pl.ds(c, nb, stride=pitch), :]
        dh = dxn * gain_ref[c]
        prod = dxn * hat
        dg_ref[c] += prod[:8] + prod[8:]
        ds_ref[c] += dxn[:8] + dxn[8:]
        return da + dh, db + dh * hat

    da, db = lax.fori_loop(0, CH, gather, (zero, zero), unroll=9)
    mean_a = da * (1.0 / CH)
    mean_b = db * (1.0 / CH)

    def put(c, carry):
        hat = (x_ref[c].astype(F32) - mean) * rstd
        dxn = rows_ref[pl.ds(c, nb, stride=pitch), :]
        dx_ref[c] = (rstd * (dxn * gain_ref[c] - mean_a - hat * mean_b)).astype(BF16)
        return carry

    lax.fori_loop(0, CH, put, 0, unroll=9)

    @pl.when(pl.program_id(0) == pl.num_programs(0) - 1)
    def _():
        for k, ref in enumerate((dg_ref, ds_ref)):
            part = jnp.concatenate([jnp.sum(ref[...], axis=1), jnp.zeros((AXW - CH, lanes), F32)], axis=0)
            sums_ref[k:k + 1, :] = jnp.sum(part.T, axis=0, keepdims=True)


def x_post(base, x_gain, x_cm, mean, rstd, dxn, z2a, z2b, full):
    _, nb, m = x_cm.shape
    part, n, d = z2a.shape
    half = 2 * part
    lanes = m // half
    whole = lambda shape: pl.BlockSpec(shape, lambda i, base: (0,) * len(shape))
    chan = pl.BlockSpec((CH, nb, lanes), lambda i, base: (0, 0, i))
    stat = pl.BlockSpec((nb, lanes), lambda i, base: (0, i))
    return pl.pallas_call(
        x_post_kernel,
        grid_spec=pltpu.PrefetchScalarGridSpec(
            num_scalar_prefetch=1,
            grid=(half,),
            in_specs=[
                pl.BlockSpec(memory_space=pltpu.SMEM),
                chan, stat, stat,
                pl.BlockSpec((nb, CPAD, lanes), lambda i, base: (0, 0, i)),
                pl.BlockSpec((1, n, d), lambda i, base: (jnp.minimum(i, part - 1), 0, 0)),
                pl.BlockSpec((1, n, d), lambda i, base: (jnp.maximum(i - part, 0), 0, 0)),
                pl.BlockSpec(memory_space=pl.ANY),
            ],
            out_specs=[chan, whole((2, AXW)), pl.BlockSpec((1, n, d), lambda i, base: (base[0] + i, 0, 0))],
            scratch_shapes=[pltpu.VMEM(((CPAD + ROW_GAP) * nb, lanes), F32),
                            pltpu.VMEM((CH, 8, lanes), F32), pltpu.VMEM((CH, 8, lanes), F32)],
        ),
        out_shape=[
            jax.ShapeDtypeStruct(x_cm.shape, BF16),
            jax.ShapeDtypeStruct((2, AXW), F32),
            jax.ShapeDtypeStruct(full.shape, F32),
        ],
        input_output_aliases={8: 2},
        compiler_params=params(),
        cost_estimate=cost(6e9, 6 * nb * CH * m + 8 * half * n * d),
        name="x_post",
    )(base, x_gain, x_cm, mean, rstd, dxn, z2a, z2b, full)


def small_sum_kernel(devices, x_ref, o_ref, got_ref, send_sem, recv_sem):
    dp, cp = devices
    my_dp, my_cp = lax.axis_index('dp'), lax.axis_index('cp')
    barrier = pltpu.get_barrier_semaphore()
    peers = [(i, j) for i in range(dp) for j in range(cp)][1:]
    ids = [(lax.rem(my_dp + i, dp), lax.rem(my_cp + j, cp)) for i, j in peers]
    for dev in ids:
        pl.semaphore_signal(barrier, inc=1, device_id=dev, device_id_type=pl.DeviceIdType.MESH)
    pl.semaphore_wait(barrier, len(ids))
    copies = []
    for k, dev in enumerate(ids):
        copies.append(pltpu.make_async_remote_copy(
            src_ref=x_ref, dst_ref=got_ref.at[k], send_sem=send_sem.at[k], recv_sem=recv_sem.at[k],
            device_id=dev, device_id_type=pl.DeviceIdType.MESH))
        copies[-1].start()
    for copy in copies:
        copy.wait()
    o_ref[...] = x_ref[...] + jnp.sum(got_ref[...], axis=0)


def small_sum(mesh, x):
    count = mesh.size - 1
    return pl.pallas_call(
        functools.partial(small_sum_kernel, (mesh.shape['dp'], mesh.shape['cp'])),
        in_specs=[pl.BlockSpec(memory_space=pltpu.VMEM)],
        out_specs=pl.BlockSpec(memory_space=pltpu.VMEM),
        out_shape=jax.ShapeDtypeStruct(x.shape, F32),
        scratch_shapes=[pltpu.VMEM((count,) + x.shape, F32),
                        pltpu.SemaphoreType.DMA((count,)), pltpu.SemaphoreType.DMA((count,))],
        compiler_params=pltpu.CompilerParams(collective_id=0, has_side_effects=True),
        name="small_sum",
    )(x)


def solution(mesh):
    x_spec = P('dp', 'cp', None)
    row_spec = P('dp', None, None)
    vec_spec = P(None)
    mat_spec = P(None, None)
    in_specs = (x_spec, mat_spec, vec_spec, vec_spec, vec_spec, vec_spec, mat_spec, mat_spec, mat_spec, mat_spec,
                vec_spec, vec_spec, mat_spec, vec_spec, mat_spec, vec_spec, row_spec)
    out_specs = (row_spec, x_spec, mat_spec, vec_spec, vec_spec, vec_spec, vec_spec, mat_spec, mat_spec, mat_spec, mat_spec,
                 vec_spec, vec_spec, mat_spec, vec_spec, mat_spec, vec_spec)
    swap = [(0, 1), (1, 0)]

    def step(inputs, latents, x_gain, x_shift, z_gain, z_shift, w_query, w_key, w_value, w_out, m_gain, m_shift, w_up, b_up, w_down, b_down, d_out):
        qk_scale = w_query.shape[1] ** -0.5
        n, d = latents.shape
        half = inputs.shape[0] // 2
        core = lax.axis_index('cp')
        as_ints = lambda *vals: jnp.stack([v.astype(jnp.int32) for v in vals])
        mine = as_ints(core * half, core * (d // 2))
        other = as_ints((1 - core) * half, (1 - core) * (d // 2))
        row = lambda vec: vec.reshape(1, -1)

        def both(own, axis):
            got = lax.ppermute(own, 'cp', swap)
            return jnp.where(core == 0, jnp.concatenate([own, got], axis), jnp.concatenate([got, own], axis))

        x_cm = jnp.transpose(inputs, (2, 0, 1))
        xn, x_mean, x_rstd = x_prep(x_cm, x_gain, x_shift)

        z_ln, z_pull = jax.vjp(layer_norm, latents, z_gain, z_shift)
        z_norm = z_ln.astype(BF16)
        queries = mm(z_norm, w_query).astype(BF16)
        wk_pad = jnp.pad(w_key, ((0, CPAD - CH), (0, 0)))
        q_key = mm_nt(queries, wk_pad)
        qp = (q_key * (qk_scale * LOG2E)).astype(BF16)
        qpt = (mm_nt(wk_pad, queries) * qk_scale).astype(BF16)
        wvo = mm(jnp.pad(w_value, ((0, CPAD - CH), (0, 0))), w_out).astype(BF16)

        e_other, ax_other = attn_fwd(other, qp, xn, half)
        ax_got = lax.ppermute(ax_other, 'cp', swap)
        e_mine, ax_mine = attn_fwd(mine, qp, xn, half)

        z1, act, dpre, dw1, dw2, db1 = mlp_a(
            mine, ax_mine, ax_got, latents, wvo, row(m_gain), row(m_shift), w_up, row(b_up), w_down, d_out)
        d_w_up, d_w_down = lax.psum((dw1, dw2), ('dp', 'cp'))
        mlp_args = (mine, ax_mine, ax_got, z1, act, dpre, d_out, wvo, row(m_gain), w_up, w_down, row(b_down), db1)
        z2a, full, ga, acc = mlp_b(*mlp_args, 0, half // 2, None, None)
        ga_got = lax.ppermute(ga, 'cp', swap)
        z2a_got = lax.ppermute(z2a, 'cp', swap)
        z2b, full, gb, acc = mlp_b(*mlp_args, half // 2, half // 2, acc, full)
        gb_got = lax.ppermute(gb, 'cp', swap)
        dxn, t_part, piece = attn_bwd(
            True, ga, gb, ax_mine, e_mine, xn, qpt, jnp.zeros((CPAD, n), F32), acc, None)
        z2b, dxn = lax.optimization_barrier((z2b, dxn))
        z2b_got = lax.ppermute(z2b, 'cp', swap)
        dxn, t_part, acc = attn_bwd(
            False, ga_got, gb_got, ax_other, e_other, xn, qpt, t_part, piece, dxn)

        t_mine = lax.dynamic_slice_in_dim(t_part, core * (CPAD // 2), CPAD // 2, 0)
        t_send = lax.dynamic_slice_in_dim(t_part, (1 - core) * (CPAD // 2), CPAD // 2, 0)
        t_mine = t_mine + lax.ppermute(t_send, 'cp', swap)
        t_parts = [t_mine]
        for bit in (1, 2, 3):
            t_parts.append(lax.ppermute(t_mine, 'dp', [(k, k ^ bit) for k in range(4)]))
        dx_cm, sums, z_out = x_post(other, x_gain, x_cm, x_mean, x_rstd, dxn, z2a_got, z2b_got, full)
        t_sum = both((t_parts[0] + t_parts[1]) + (t_parts[2] + t_parts[3]), 0)
        sums = small_sum(mesh, sums)
        d_x_gain, d_x_shift = sums[0, :CH], sums[1, :CH]

        d_mid_sum = acc[:n]
        p_low = acc[n:n + CH].astype(BF16)
        d_m_gain, d_m_shift, d_b_down, d_b_up = (acc[VEC_ROW + k] for k in range(4))
        d_w_out = mm_tn(w_value, p_low)
        d_w_value = mm_nt(p_low, w_out)
        t_low = (t_sum[:CH] * qk_scale).astype(BF16)
        d_query = mm_tn(t_low, w_key).astype(BF16)
        d_w_key = mm(t_low, queries)
        d_z_norm = mm_nt(d_query, w_query)
        d_w_query = mm_tn(z_norm, d_query)
        d_lat_ln, d_z_gain, d_z_shift = z_pull(d_z_norm)
        return (z_out, jnp.transpose(dx_cm, (1, 2, 0)), d_lat_ln + d_mid_sum, d_x_gain, d_x_shift, d_z_gain, d_z_shift,
                d_w_query, d_w_key, d_w_value, d_w_out, d_m_gain, d_m_shift, d_w_up, d_b_up, d_w_down, d_b_down)

    return jax.shard_map(step, mesh=mesh, in_specs=in_specs, out_specs=out_specs, check_vma=False)
```

time: 1260 us -> 412 us (0.33)
  matrix products: 688 us -> 28.6 us
  Pallas kernels: 0 us -> 276 us
  waiting for transfers between devices: 260 us -> 57.8 us
  other arithmetic: 210 us -> 8.56 us
  blocking collectives: 53.2 us -> 0 us
    dot_general x24 -> x10, matrix products: 688 us -> 28.6 us  [the longest x3 10.4 us: mm_tn(): lax.dot_general(lhs, rhs, (((0,), (0,)), ((), ())), preferred_element_typ...]
    pallas_call x0 -> x10, Pallas kernels: none -> 276 us  [the longest x1 68.4 us: mlp_a(): pl.pallas_call(mlp_a_kernel, grid_spec=pltpu.PrefetchScalarGridSpec(num_s...]
    psum x3 -> x1, waiting for transfers between devices: 260 us -> 37.9 us  [step(): d_w_up, d_w_down = lax.psum((dw1, dw2), ('dp', 'cp'))]
    reduce_sum x4 -> x0, other arithmetic: 78.5 us -> none  [the longest x3 60.9 us: layer_norm(): return centred * lax.rsqrt(variance + LN_EPS) * ln_gain + ln_shift]
    convert_element_type x3 -> x0, other arithmetic: 67.8 us -> none  [the longest x1 27.9 us: local_step(): d_logits = (attn_probs * (d_probs - row_dot) * qk_scale).astype(LOW_TYPE)]
    psum x4 -> x0, blocking collectives: 49.1 us -> none  [the longest x1 24.5 us: local_step(): lax.psum(shared_grads, ('dp', 'cp'))]
    reduce_sum x2 -> x1, other arithmetic: 25.1 us -> 0.7 us  [layer_norm(): centred = tensor - row_mean]
    reduce_sum x3 -> x1, other arithmetic: 24.3 us -> 1.94 us  [layer_norm(): variance = jnp.mean(centred * centred, axis=-1, keepdims=True)]
  transfers between devices with their start and end apart: 3 -> 11, of which waited for: 2 -> 5; matrix products, arithmetic and copies ran while one was open for 14% -> 9% of each run, Pallas kernels for 0% -> 29%
where the time goes in v1:
time: 412 us; the launch traced here: 409 us
  Pallas kernels  276 us (67%)
  waiting for transfers between devices  57.8 us (14%)
  matrix products  28.6 us (7%)
  local copies, waits for them, and re-layouts  17.9 us (4%)
  between operations  14.6 us (4%)
  other arithmetic  8.56 us (2%)
  starting transfers between devices  5.59 us (1%)
    pallas_call x1, Pallas kernels, mlp_a(): pl.pallas_call(mlp_a_kernel, grid_spec=pltpu.PrefetchScalarGridSpec(num_s...  68.4 us
    pallas_call x2, Pallas kernels, attn_bwd(): pl.pallas_call(kernel, grid=(half,), in_specs=in_specs, out_specs=out_spe...  66.7 us
    pallas_call x2, Pallas kernels, mlp_b(): pl.pallas_call(body, grid_spec=pltpu.PrefetchScalarGridSpec(num_scalar_pr...  58.7 us
    psum x1, waiting for transfers between devices, step(): d_w_up, d_w_down = lax.psum((dw1, dw2), ('dp', 'cp'))  37.9 us
    pallas_call x2, Pallas kernels, attn_fwd(): pl.pallas_call(attn_fwd_kernel, grid_spec=pltpu.PrefetchScalarGridSpec(nu...  30 us
    pallas_call x1, Pallas kernels, x_post(): pl.pallas_call(x_post_kernel, grid_spec=pltpu.PrefetchScalarGridSpec(num_...  29 us
    ppermute x3, waiting for transfers between devices, step(): t_parts.append(lax.ppermute(t_mine, 'dp', [(k, k ^ bit) for k in range(4)]))  18.4 us
    pallas_call x1, Pallas kernels, x_prep(): pl.pallas_call(x_prep_kernel, grid=(m // lanes,), in_specs=[pl.BlockSpec(...  17.1 us
  transfers between devices with their start and end apart: 11, of which 5 were waited for; matrix products, arithmetic and copies ran while one was open for 9% of the time, Pallas kernels for 29%

profile of v1, /device:TPU:0, one launch (start us, length us, event | category | flops | bytes accessed | tf_op | source)
XLA Modules:
  0.0 409.4 jit_solution(10725747717102238096)
XLA Ops:
  7.2 0.0 copy-start
  7.2 0.0 all-reduce.5.cloned.1.call-start
  7.3 0.0 copy-start.11
  7.3 0.0 copy-start.14
  7.3 1.9 reduce_sum.51
  9.2 0.0 copy-start.5
  9.2 1.9 multiply_reduce_fusion.2
  11.1 0.6 copy-done.7
  11.8 0.0 copy-start.13
  11.8 3.0 convolution_convert_fusion.1
  14.8 1.5 fusion.qp_ref
  16.3 0.6 pad_add_fusion.base_ref
  16.9 17.1 %x_prep.1 = (bf16[16,272,1024]{2,1,0:T(8,128)(2,1)}, f32[16,1024]{1,0:T(8,128)}, f32[16,1024]{1,0:T(8,128)}) custom-call(f32[261]{0:T(512)} %gain_ref.3, f32[261]{0:T(512)} %shift_ref.1, bf16[261,16,1024]{2,1,0:T(8,128)(2,1)} %bitcast.27), custom_call_target="tpu_custom_call" | custom-call | flops 3000000000 | bytes 17104896 | tf_op jit(solution)/shard_map/x_prep/pallas_call | solution.py:93
  34.0 15.0 %attn_fwd.3 = (bf16[8,512,1024]{2,1,0:T(8,128)(2,1)}, f32[8,512,384]{2,1,0:T(8,128)}) custom-call(s32[2]{0:T(128)} %pad_add_fusion.base_ref, bf16[512,272]{1,0:T(8,128)(2,1)} %fusion.qp_ref, bf16[16,272,1024]{2,1,0:T(8,128)(2,1)} %get-tuple-element.51.xn_ref.refs_4_), custom_call_target="tpu_custom_call" | custom-call | flops 8589934592 | bytes 12582912 | tf_op jit(solution)/shard_map/attn_fwd/pallas_call | solution.py:130
  49.0 0.8 collective-permute-start
  49.8 0.6 pad_add_fusion.1.base_ref.where_ref
  50.4 2.2 fusion.1.refs_5_
  52.7 3.3 convolution_convert_fusion.2.wvo_ref.refs_6_
  56.0 15.0 %attn_fwd.2 = (bf16[8,512,1024]{2,1,0:T(8,128)(2,1)}, f32[8,512,384]{2,1,0:T(8,128)}) custom-call(s32[2]{0:T(128)} %pad_add_fusion.1.base_ref.where_ref, bf16[512,272]{1,0:T(8,128)(2,1)} %fusion.qp_ref, bf16[16,272,1024]{2,1,0:T(8,128)(2,1)} %get-tuple-element.51.xn_ref.refs_4_), custom_call_target="tpu_custom_call" | custom-call | flops 8589934592 | bytes 12582912 | tf_op jit(solution)/shard_map/attn_fwd/pallas_call | solution.py:130
  71.0 0.0 collective-permute-done.axb_ref.refs_1_
  71.0 68.4 %mlp_a.1 = (f32[8,512,1024]{2,1,0:T(8,128)}, bf16[8,512,1024]{2,1,0:T(8,128)(2,1)}, bf16[8,512,1024]{2,1,0:T(8,128)(2,1)}, f32[1024,1024]{1,0:T(8,128)}, f32[1024,1024]{1,0:T(8,128)}, /*index=5*/f32[1,1024]{1,0:T(1,128)}) custom-call(s32[2]{0:T(128)} %pad_add_fusion.1.base_ref.where_ref, f32[8,512,384]{2,1,0:T(8,128)} %get-tuple-element.52.axa_ref.refs_0_.refs_2_, ...), custom_call_target="tpu_custom_call" | custom-call | flops 38654705664 | bytes 41943040 | tf_op jit(solution)/shard_map/mlp_a/pallas_call | solution.py:203
  139.4 28.9 %mlp_b.2 = (f32[4,512,1024]{2,1,0:T(8,128)}, f32[16,512,1024]{2,1,0:T(8,128)}, f32[4,512,384]{2,1,0:T(8,128)}, f32[896,1024]{1,0:T(8,128)}) custom-call(s32[2]{0:T(128)} %pad_add_fusion.1.base_ref.where_ref, f32[8,512,384]{2,1,0:T(8,128)} %get-tuple-element.52.axa_ref.refs_0_.refs_2_, f32[8,512,384]{2,1,0:T(8,128)} %collective-permute-done.axb_ref.refs_1_, ...), custom_call_target="tpu_custom_call" | custom-call | flops 11945377792 | bytes 37748736 | tf_op jit(solution)/shard_map/mlp_b/pallas_call | solution.py:283
  168.3 29.8 %mlp_b.3 = (f32[4,512,1024]{2,1,0:T(8,128)}, f32[16,512,1024]{2,1,0:T(8,128)}, f32[4,512,384]{2,1,0:T(8,128)}, f32[896,1024]{1,0:T(8,128)}) custom-call(s32[2]{0:T(128)} %pad_add_fusion.1.base_ref.where_ref, f32[8,512,384]{2,1,0:T(8,128)} %get-tuple-element.52.axa_ref.refs_0_.refs_2_, ...), custom_call_target="tpu_custom_call", output_to_operand_aliasing={{1}: (14, {})} | custom-call | flops 11945377792 | bytes 37748736 | tf_op jit(solution)/shard_map/mlp_b/pallas_call | solution.py:283
  198.1 0.0 collective-permute-start.2
  198.1 0.5 collective-permute-start.1
  198.6 0.9 broadcast_in_dim.6.refs_6_
  199.5 35.8 %attn_bwd.2 = (bf16[16,272,1024]{2,1,0:T(8,128)(2,1)}, f32[272,512]{1,0:T(8,128)}, f32[2,56,1024]{2,1,0:T(8,128)}) custom-call(f32[4,512,384]{2,1,0:T(8,128)} %get-tuple-element.58.refs_0_, f32[4,512,384]{2,1,0:T(8,128)} %get-tuple-element.61.refs_1_, f32[8,512,384]{2,1,0:T(8,128)} %get-tuple-element.52.axa_ref.refs_0_.refs_2_, ...), custom_call_target="tpu_custom_call" | custom-call | flops 17179869184 | bytes 25165824 | tf_op jit(solution)/shard_map/attn_bwd/pallas_call | solution.py:475
  235.3 0.0 collective-permute-start.4
  235.3 0.5 collective-permute-start.3
  235.8 0.0 collective-permute-done.2.refs_1_
  235.8 0.0 collective-permute-done.1.refs_0_
  235.8 30.9 %attn_bwd.3 = (bf16[16,272,1024]{2,1,0:T(8,128)(2,1)}, f32[272,512]{1,0:T(8,128)}, f32[896,1024]{1,0:T(8,128)}) custom-call(f32[4,512,384]{2,1,0:T(8,128)} %collective-permute-done.1.refs_0_, f32[4,512,384]{2,1,0:T(8,128)} %collective-permute-done.2.refs_1_, f32[8,512,384]{2,1,0:T(8,128)} %get-tuple-element.53.refs_2_, ...), custom_call_target="tpu_custom_call", output_to_operand_aliasing={{0}: (8, {})} | custom-call | flops 17179869184 | bytes 25165824 | tf_op jit(solution)/shard_map/attn_bwd/pallas_call | solution.py:475
  266.7 1.0 constant_dynamic-slice_fusion
  267.7 0.1 collective-permute-start.5
  267.8 0.0 all-reduce.5.cloned.1.call-update
  267.9 1.6 collective-permute-done.5
  269.4 1.1 dynamic-slice_add_fusion
  270.5 0.5 collective-permute-start.6
  271.0 1.5 collective-permute-start.7
  272.5 1.5 collective-permute-start.8
  274.0 4.8 %convolution_bitcast_fusion = f32[1024,1024]{0,1:T(8,128)} fusion(bf16[261,1024]{1,0:T(8,128)(2,1)} %param.25, f32[896,1024]{1,0:T(8,128)} %get-tuple-element.77), kind=kOutput, calls=%fused_computation.1 | convolution fusion | flops 547356672 | bytes 5275648 | tf_op jit(solution)/shard_map/dot_general | solution.py:46
  278.8 7.2 %collective-permute-done.6 = f32[136,512]{1,0:T(8,128)S(1)} collective-permute-done((f32[136,512]{1,0:T(8,128)S(1)}, f32[136,512]{1,0:T(8,128)S(1)}, u32[]{:S(2)}, u32[]{:S(2)}) %collective-permute-start.6) | collective-permute-done | bytes 278560 | tf_op jit(solution)/shard_map/ppermute | solution.py:677
  286.0 1.4 collective-permute-done.7
  287.4 9.8 %collective-permute-done.8 = f32[136,512]{1,0:T(8,128)S(1)} collective-permute-done((f32[136,512]{1,0:T(8,128)S(1)}, f32[136,512]{1,0:T(8,128)S(1)}, u32[]{:S(2)}, u32[]{:S(2)}) %collective-permute-start.8) | collective-permute-done | bytes 278560 | tf_op jit(solution)/shard_map/ppermute | solution.py:677
  297.2 0.1 add_add_fusion.1
  297.3 0.0 collective-permute-start.9
  297.3 3.0 fusion.8
  300.4 5.5 %copy.38 = f32[1024,1024]{1,0:T(8,128)} copy(f32[1024,1024]{0,1:T(8,128)} %convolution_bitcast_fusion) | data formatting | bytes 8388608
  305.9 1.6 fusion.18
  307.5 0.0 collective-permute-done.9
  307.5 2.0 convolution_convert_fusion
  309.6 2.3 multiply_reduce_fusion
  311.9 0.7 fusion.17
  312.6 2.9 fusion.13
  315.5 1.6 slice_add_fusion
  317.1 3.5 fusion.16
  320.6 0.0 collective-permute-done.4.z2b_ref
  320.6 0.0 collective-permute-done.3.z2a_ref
  320.6 29.0 %x_post.1 = (bf16[261,16,1024]{2,1,0:T(8,128)(2,1)}, f32[2,384]{1,0:T(2,128)}, f32[16,512,1024]{2,1,0:T(8,128)}) custom-call(s32[2]{0:T(128)} %pad_add_fusion.base_ref, f32[261]{0:T(512)} %gain_ref.3, bf16[261,16,1024]{2,1,0:T(8,128)(2,1)} %bitcast.28, f32[16,1024]{1,0:T(8,128)} %get-tuple-element.49.mean_ref, ...), custom_call_target="tpu_custom_call", output_to_operand_aliasing={{2}: (8, {})} | custom-call | flops 6000000000 | bytes 59211776 | tf_op jit(solution)/shard_map/x_post/pallas_call | solution.py:552
  349.6 6.5 %small_sum.1 = f32[2,384]{1,0:T(2,128)} custom-call(f32[2,384]{1,0:T(2,128)} %get-tuple-element.78.x_ref), custom_call_target="tpu_custom_call" | custom-call | tf_op jit(solution)/shard_map/small_sum/pallas_call | solution.py:603
  356.1 1.4 slice_reduce_fusion
  357.5 37.9 %all-reduce.5.cloned.1.call-done = (f32[1024,1024]{1,0:T(8,128)}, f32[1024,1024]{1,0:T(8,128)}) async-done(((f32[1024,1024]{1,0:T(8,128)}, f32[1024,1024]{1,0:T(8,128)}), (f32[1024,1024]{1,0:T(8,128)}, f32[1024,1024]{1,0:T(8,128)})) %all-reduce.5.cloned.1.call-update) | async-done | bytes 8388624 | tf_op jit(solution)/shard_map/psum | solution.py:658
  395.4 4.9 %copy.45 = f32[1024,1024]{1,0:T(8,128)} copy(f32[1024,1024]{1,0:T(8,128)} %get-tuple-element.125) | data formatting | bytes 8388608
  400.3 2.0 copy.46
  (30 shorter events, 0.1 us)
Async XLA Ops:
  7.2 4.6 %copy-start = (bf16[1024,1024]{1,0:T(8,128)(2,1)S(1)}, bf16[1024,1024]{1,0:T(8,128)(2,1)}, u32[]{:S(2)}) copy-start(bf16[1024,1024]{1,0:T(8,128)(2,1)} %param.23) | copy-start | bytes 6291460
  7.2 388.1 %all-reduce.5.cloned.1.call-start = ((), (), s32[]{:S(2)}) async-start(), calls=%async_computation | async-start | bytes 16777216 | tf_op jit(solution)/shard_map/psum | solution.py:658
  7.3 4.5 %copy-start.11 = (f32[1024]{0:T(1024)S(1)}, f32[1024]{0:T(1024)}, u32[]{:S(2)}) copy-start(f32[1024]{0:T(1024)} %param.21) | copy-start | bytes 12292
  7.3 4.5 %copy-start.14 = (f32[1024]{0:T(1024)S(1)}, f32[1024]{0:T(1024)}, u32[]{:S(2)}) copy-start(f32[1024]{0:T(1024)} %param.22) | copy-start | bytes 12292
  9.2 5.6 %copy-start.5 = (f32[512]{0:T(512)}, f32[512]{0:T(512)S(1)}, u32[]{:S(2)}) copy-start(f32[512]{0:T(512)S(1)} %broadcast_multiply_fusion) | copy-start | bytes 6148
  11.1 0.6 copy-start.7
  11.7 3.0 copy-start.9
  11.8 3.0 copy-start.13
  49.0 22.0 %collective-permute-start = (f32[8,512,384]{2,1,0:T(8,128)}, f32[8,512,384]{2,1,0:T(8,128)}, u32[]{:S(2)}, u32[]{:S(2)}) collective-permute-start(f32[8,512,384]{2,1,0:T(8,128)} %get-tuple-element.53.refs_2_), channel_id=1, source_target_pairs={{0,1},{1,0},{2,3},{3,2},{4,5},{5,4},{6,7},{7,6}} | collective-permute-start | bytes 18874376 | tf_op jit(solution)/shard_map/ppermute | solution.py:653
  198.1 37.7 %collective-permute-start.2 = (f32[4,512,384]{2,1,0:T(8,128)}, f32[4,512,384]{2,1,0:T(8,128)}, u32[]{:S(2)}, u32[]{:S(2)}) collective-permute-start(f32[4,512,384]{2,1,0:T(8,128)} %get-tuple-element.61.refs_1_), channel_id=1, source_target_pairs={{0,1},{1,0},{2,3},{3,2},{4,5},{5,4},{6,7},{7,6}} | collective-permute-start | bytes 9437192 | tf_op jit(solution)/shard_map/ppermute | solution.py:664
  198.1 37.7 %collective-permute-start.1 = (f32[4,512,384]{2,1,0:T(8,128)}, f32[4,512,384]{2,1,0:T(8,128)}, u32[]{:S(2)}, u32[]{:S(2)}) collective-permute-start(f32[4,512,384]{2,1,0:T(8,128)} %get-tuple-element.58.refs_0_), channel_id=1, source_target_pairs={{0,1},{1,0},{2,3},{3,2},{4,5},{5,4},{6,7},{7,6}} | collective-permute-start | bytes 9437192 | tf_op jit(solution)/shard_map/ppermute | solution.py:661
  235.3 85.4 %collective-permute-start.4 = (f32[4,512,1024]{2,1,0:T(8,128)}, f32[4,512,1024]{2,1,0:T(8,128)}, u32[]{:S(2)}, u32[]{:S(2)}) collective-permute-start(f32[4,512,1024]{2,1,0:T(8,128)} %get-tuple-element.72), channel_id=1, source_target_pairs={{0,1},{1,0},{2,3},{3,2},{4,5},{5,4},{6,7},{7,6}} | collective-permute-start | bytes 25165832 | tf_op jit(solution)/shard_map/ppermute | solution.py:668
  235.3 85.3 %collective-permute-start.3 = (f32[4,512,1024]{2,1,0:T(8,128)}, f32[4,512,1024]{2,1,0:T(8,128)}, u32[]{:S(2)}, u32[]{:S(2)}) collective-permute-start(f32[4,512,1024]{2,1,0:T(8,128)} %get-tuple-element.71), channel_id=1, source_target_pairs={{0,1},{1,0},{2,3},{3,2},{4,5},{5,4},{6,7},{7,6}} | collective-permute-start | bytes 25165832 | tf_op jit(solution)/shard_map/ppermute | solution.py:662
  267.7 1.7 collective-permute-start.5
  270.5 15.5 %collective-permute-start.6 = (f32[136,512]{1,0:T(8,128)S(1)}, f32[136,512]{1,0:T(8,128)S(1)}, u32[]{:S(2)}, u32[]{:S(2)}) collective-permute-start(f32[136,512]{1,0:T(8,128)S(1)} %dynamic-slice_add_fusion), channel_id=1, source_target_pairs={{0,2},{2,0},{4,6},{6,4},{1,3},{3,1},{5,7},{7,5}} | collective-permute-start | bytes 835592 | tf_op jit(solution)/shard_map/ppermute | solution.py:677
  271.0 16.4 %collective-permute-start.7 = (f32[136,512]{1,0:T(8,128)S(1)}, f32[136,512]{1,0:T(8,128)S(1)}, u32[]{:S(2)}, u32[]{:S(2)}) collective-permute-start(f32[136,512]{1,0:T(8,128)S(1)} %dynamic-slice_add_fusion), channel_id=1, source_target_pairs={{0,4},{2,6},{4,0},{6,2},{1,5},{3,7},{5,1},{7,3}} | collective-permute-start | bytes 835592 | tf_op jit(solution)/shard_map/ppermute | solution.py:677
  272.5 24.7 %collective-permute-start.8 = (f32[136,512]{1,0:T(8,128)S(1)}, f32[136,512]{1,0:T(8,128)S(1)}, u32[]{:S(2)}, u32[]{:S(2)}) collective-permute-start(f32[136,512]{1,0:T(8,128)S(1)} %dynamic-slice_add_fusion), channel_id=1, source_target_pairs={{0,6},{2,4},{4,2},{6,0},{1,7},{3,5},{5,3},{7,1}} | collective-permute-start | bytes 835592 | tf_op jit(solution)/shard_map/ppermute | solution.py:677
  274.0 23.3 %copy-start.4 = (bf16[1024,1024]{1,0:T(8,128)(2,1)S(1)}, bf16[1024,1024]{1,0:T(8,128)(2,1)}, u32[]{:S(2)}) copy-start(bf16[1024,1024]{1,0:T(8,128)(2,1)} %param.26) | copy-start | bytes 6291460
  297.3 10.2 %collective-permute-start.9 = (f32[136,512]{1,0:T(8,128)S(1)}, f32[136,512]{1,0:T(8,128)}, u32[]{:S(2)}, u32[]{:S(2)}) collective-permute-start(f32[136,512]{1,0:T(8,128)S(1)} %add_add_fusion.1), channel_id=1, source_target_pairs={{0,1},{1,0},{2,3},{3,2},{4,5},{5,4},{6,7},{7,6}} | collective-permute-start | bytes 835592 | tf_op jit(solution)/shard_map/ppermute | solution.py:637
  305.9 3.6 copy-start.1
  305.9 3.6 copy-start.6
  305.9 3.6 copy-start.10
  305.9 3.7 copy-start.12
  309.6 2.3 copy-start.8
  311.8 3.6 copy-start.2
  315.5 1.6 copy-start.15
  395.3 4.9 %copy-start.3 = (f32[1024,1024]{1,0:T(8,128)S(1)}, f32[1024,1024]{1,0:T(8,128)}, u32[]{:S(2)}) copy-start(f32[1024,1024]{1,0:T(8,128)} %get-tuple-element.127) | copy-start | bytes 12582916
Sparse Core Ops, SparseCore 0:
  268.0 127.3 all-reduce.4

commit v2 on v0

v2 whole, which is shorter than its diff:
```python
import functools
import math

import jax
import jax.numpy as jnp
from jax import lax
from jax.experimental import pallas as pl
from jax.experimental.pallas import tpu as pltpu
from jax.sharding import PartitionSpec as P


LN_EPS = 1e-5
F32 = jnp.float32
BF16 = jnp.bfloat16
CH = 261
CPAD = 272
AXW = 384
ROW_GAP = 8
ACC_ROWS = 896
VEC_ROW = 784
SUM_LANE = 261
MAX_LANE = 262
INV_LANE = 263
LOG2E = math.log2(math.e)
GELU_A = math.sqrt(2.0 / math.pi)
GELU_B = 0.044715
VMEM_LIMIT = 63 * 1024 * 1024


def layer_norm(tensor, ln_gain, ln_shift):
    row_mean = jnp.mean(tensor, axis=-1, keepdims=True)
    centred = tensor - row_mean
    variance = jnp.mean(centred * centred, axis=-1, keepdims=True)
    return centred * lax.rsqrt(variance + LN_EPS) * ln_gain + ln_shift


def mm(lhs, rhs):
    return lax.dot_general(lhs, rhs, (((1,), (0,)), ((), ())), preferred_element_type=F32)


def mm_nt(lhs, rhs):
    return lax.dot_general(lhs, rhs, (((1,), (1,)), ((), ())), preferred_element_type=F32)


def params(semantics=1):
    return pltpu.CompilerParams(
        vmem_limit_bytes=VMEM_LIMIT, dimension_semantics=("arbitrary",) * semantics)


def whole(shape, **kw):
    return pl.BlockSpec(shape, lambda *_: (0,) * len(shape), **kw)


def once(shape):
    return whole(shape, pipeline_mode=pl.Buffered(1))


def lead(shape, index=lambda i: i):
    return pl.BlockSpec(shape, lambda i, *_: (index(i),) + (0,) * (len(shape) - 1))


def trail(shape):
    return pl.BlockSpec(shape, lambda i, *_: (0,) * (len(shape) - 1) + (i,))


def column(array, lane):
    return array[:, lane:lane + 1]


def cost(flops, nbytes):
    return pl.CostEstimate(flops=int(flops), bytes_accessed=int(nbytes), transcendentals=0)


def x_prep_kernel(gain_ref, shift_ref, x_ref, xn_ref, mean_ref, rstd_ref, rows_ref):
    nb = x_ref.shape[1]
    lanes = x_ref.shape[2]
    pitch = nb + ROW_GAP
    zero = jnp.zeros((nb, lanes), F32)

    def add_up(c, acc):
        return acc + x_ref[c].astype(F32)

    mean = lax.fori_loop(0, CH, add_up, zero, unroll=9) * (1.0 / CH)

    def add_sq(c, acc):
        d = x_ref[c].astype(F32) - mean
        return acc + d * d

    var = lax.fori_loop(0, CH, add_sq, zero, unroll=9) * (1.0 / CH)
    rstd = lax.rsqrt(var + LN_EPS)
    mean_ref[:] = mean
    rstd_ref[:] = rstd

    def put(c, carry):
        xn = (x_ref[c].astype(F32) - mean) * rstd * gain_ref[c] + shift_ref[c]
        rows_ref[pl.ds(pl.multiple_of(c * pitch, ROW_GAP), nb), :] = xn
        return carry

    lax.fori_loop(0, CH, put, 0, unroll=9)
    rows_ref[CH * pitch:CPAD * pitch, :] = jnp.zeros(((CPAD - CH) * pitch, lanes), F32)
    for b in range(nb):
        xn_ref[b] = rows_ref[pl.ds(b, CPAD, stride=pitch), :].astype(BF16)


def x_prep(x_cm, x_gain, x_shift):
    _, nb, m = x_cm.shape
    lanes = 128
    stat = trail((nb, lanes))
    return pl.pallas_call(
        x_prep_kernel,
        grid=(m // lanes,),
        in_specs=[
            pl.BlockSpec(memory_space=pltpu.SMEM),
            pl.BlockSpec(memory_space=pltpu.SMEM),
            trail((CH, nb, lanes)),
        ],
        out_specs=[trail((nb, CPAD, lanes)), stat, stat],
        out_shape=[
            jax.ShapeDtypeStruct((nb, CPAD, m), BF16),
            jax.ShapeDtypeStruct((nb, m), F32),
            jax.ShapeDtypeStruct((nb, m), F32),
        ],
        scratch_shapes=[pltpu.VMEM((CPAD * (nb + ROW_GAP), lanes), F32)],
        compiler_params=params(),
        cost_estimate=cost(3e9, 4 * nb * CH * m),
        name="x_prep",
    )(x_gain, x_shift, x_cm)


def attn_fwd_kernel(base_ref, qp_ref, xn_ref, e_ref, ax_ref):
    xn = xn_ref[0]
    n = qp_ref.shape[0]
    spans = [slice(k * (n // 2), (k + 1) * (n // 2)) for k in range(2)]
    logits = [mm(qp_ref[span, :], xn) for span in spans]
    for span, s in zip(spans, logits):
        top = jnp.max(s, axis=1, keepdims=True)
        e = jnp.exp2(s - top)
        total = jnp.sum(e, axis=1, keepdims=True)
        e_low = e.astype(BF16)
        e_ref[0, span, :] = e_low
        ax = jnp.concatenate([mm_nt(e_low, xn), jnp.zeros((e.shape[0], AXW - CPAD), F32)], axis=1)
        lane = lax.broadcasted_iota(jnp.int32, ax.shape, 1)
        ax_ref[0, span, :] = jnp.where(lane == SUM_LANE, total, jnp.where(lane == MAX_LANE, top, ax))


def attn_fwd(base, qp, xn, half):
    n = qp.shape[0]
    m = xn.shape[2]
    return pl.pallas_call(
        attn_fwd_kernel,
        grid_spec=pltpu.PrefetchScalarGridSpec(
            num_scalar_prefetch=1,
            grid=(half,),
            in_specs=[
                whole((n, CPAD)),
                pl.BlockSpec((1, CPAD, m), lambda i, base: (base[0] + i, 0, 0)),
            ],
            out_specs=[
                lead((1, n, m)),
                lead((1, n, AXW)),
            ],
        ),
        out_shape=[
            jax.ShapeDtypeStruct((half, n, m), BF16),
            jax.ShapeDtypeStruct((half, n, AXW), F32),
        ],
        compiler_params=params(),
        cost_estimate=cost(4 * half * n * m * 512, half * n * m * 3),
        name="attn_fwd",
    )(base, qp, xn)


def places():
    core, chip = lax.axis_index('cp'), lax.axis_index('dp')
    x, y = lax.rem(chip, 2), chip // 2
    at_x = (y * 2 + (1 - x), core)
    at_y = ((1 - y) * 2 + x, core)
    return core, x, y, (chip, 1 - core), at_x, at_y


def meet(devices):
    barrier = pltpu.get_barrier_semaphore()
    for dev in devices:
        pl.semaphore_signal(barrier, inc=1, device_id=dev, device_id_type=pl.DeviceIdType.MESH)
    pl.semaphore_wait(barrier, len(devices))


def remote(src, dst, sems, k, dev):
    return pltpu.make_async_remote_copy(
        src_ref=src, dst_ref=dst, send_sem=sems[0].at[k], recv_sem=sems[1].at[k],
        device_id=dev, device_id_type=pl.DeviceIdType.MESH)


def rows(ref, start, size):
    return ref.at[pl.ds(pl.multiple_of(start, 8), size)]


def take(ref, start, size):
    return ref[pl.ds(pl.multiple_of(start, 8), size), :]


def at_step(step, when, todo):
    pl.when(step == when)(todo)


def dma_sems(count):
    return [pltpu.SemaphoreType.DMA((count,)), pltpu.SemaphoreType.DMA((count,))]


class Carry:
    def __init__(self, in_shape, in_hbm, out_shape, scratch, head, tail, out_hbm=False):
        self.in_shape, self.in_hbm, self.out_shape, self.scratch = in_shape, in_hbm, out_shape, scratch
        self.out_hbm = out_hbm
        self.head, self.tail = head, tail


def start_all(copies):
    for copy in copies:
        copy.start()


def wait_all(copies):
    for copy in copies:
        copy.wait()


class Plan:
    def __init__(self, total):
        self.half, self.quarter, self.eighth, self.part = (total // k for k in (2, 4, 8, 16))
        self.core, self.x, self.y, self.at_core, self.at_x, self.at_y = places()
        self.spot = (self.x * self.eighth, self.quarter + self.y * self.eighth)
        self.away = ((1 - self.x) * self.eighth, self.quarter + (1 - self.y) * self.eighth)
        self.fine = (self.y * self.part, self.x * self.part)
        self.fine_away = ((1 - self.y) * self.part, (1 - self.x) * self.part)
        self.first, self.second = (self.at_x, self.at_y), (self.at_y, self.at_x)


def carry(total, width, stages, at):
    half, _, eighth, part = (total // k for k in (2, 4, 8, 16))
    lo, hi = stages[0], stages[-1]
    in_shape = {0: (total, width), 1: (half, width), 2: (2, eighth, width), 3: (2, part, width)}[lo]
    out_shape = {0: (half, width), 1: (2, eighth, width), 2: (2, part, width), 3: (2, eighth, width), 4: (half, width)}[hi]
    shapes = {}
    if 0 in stages:
        shapes.update(half=(half, width), rx0=(half, width))
    if 1 in stages:
        shapes.update(rx1=(2, eighth, width))
    if 2 in stages:
        shapes.update(rx2=(2, part, width))
    if 1 in stages and 2 in stages:
        shapes.update(mid=(2, eighth, width))
    if 2 in stages and 3 in stages:
        shapes.update(fin=(2, part, width))
    if 3 in stages:
        shapes.update(buf=(2, eighth, width))
    if 4 in stages:
        shapes.update(full=(half, width))
    names = list(shapes)
    count = 2 * len(stages)
    scratch = [pltpu.VMEM(shape, F32) for shape in shapes.values()] + [pltpu.SemaphoreType.DMA((1,))] + dma_sems(count)

    def build(src, refs):
        r = dict(zip(names, refs))
        local, sems = refs[-3], (refs[-2], refs[-1])
        p = Plan(total)
        slot = lambda stage, k: 2 * (stage - lo) + k
        two = (0, 1)
        moves = {}
        if 0 in stages:
            moves[0] = lambda: [pltpu.make_async_copy(rows(src, p.core * half, half), r['half'], local.at[0]),
                                remote(rows(src, (1 - p.core) * half, half), r['rx0'], sems, slot(0, 0), p.at_core)]
        if 1 in stages:
            pair = r.get('half', src)
            moves[1] = lambda: [remote(rows(pair, p.away[k], eighth), r['rx1'].at[k], sems, slot(1, k), p.first[k])
                                for k in two]
        if 2 in stages:
            mid = r.get('mid', src)
            moves[2] = lambda: [remote(rows(mid.at[k], p.fine_away[k], part), r['rx2'].at[k], sems, slot(2, k), p.second[k])
                                for k in two]
        if 3 in stages:
            fin = r.get('fin', src)
            moves[3] = lambda: [remote(fin.at[k], rows(r['buf'].at[k], p.fine[k], part), sems, slot(3, k), p.second[k])
                                for k in two]
        if 4 in stages:
            moves[4] = lambda: [remote(r['buf'].at[k], rows(r['full'], p.spot[k], eighth), sems, slot(4, k), p.first[k])
                                for k in two]

        def before(stage):
            if stage == 3:
                for k in two:
                    r['buf'][k, pl.ds(pl.multiple_of(p.fine[k], 8), part), :] = fin[k]

        def after(stage, out):
            wait_all(moves[stage]())
            if stage == 0:
                r['half'][:] += r['rx0'][:]
                if hi == 0:
                    out[:] = r['half'][:]
            elif stage == 1:
                dst = out if hi == 1 else r['mid']
                for k in two:
                    dst[k] = take(pair, p.spot[k], eighth) + r['rx1'][k]
            elif stage == 2:
                dst = out if hi == 2 else r['fin']
                for k in two:
                    dst[k] = take(mid.at[k], p.fine[k], part) + r['rx2'][k]
            elif stage == 3 and hi == 3:
                out[:] = r['buf'][:]
            elif stage == 4:
                for k in two:
                    r['full'][pl.ds(pl.multiple_of(p.spot[k], 8), eighth), :] = r['buf'][k]
                out[:] = r['full'][:]

        return moves, before, after

    def head(step, src, out, refs):
        for stage, when in zip(stages, at):
            def go(stage=stage):
                moves, before, after = build(src, refs)
                if stage > lo:
                    after(stage - 1, out)
                before(stage)
                start_all(moves[stage]())

            at_step(step, when, go)

    def tail(src, out, refs):
        build(src, refs)[2](hi, out)

    return Carry(in_shape, lo == 0, out_shape, scratch, head, tail)


def carry_rows(shape, start, count, when):
    def move(src, out, refs):
        return remote(src.at[pl.ds(start, count)], out, refs, 0, places()[3])

    def head(step, src, out, refs):
        at_step(step, when, lambda: move(src, out, refs).start())

    def tail(src, out, refs):
        move(src, out, refs).wait()

    return Carry(shape, True, (count,) + shape[1:], dma_sems(1), head, tail, True)


def carrier_call(body, ident, carries, travel, grid, in_specs, args, out_specs, out_shape, aliases, cost_estimate):
    n_in, n_out, n_c = len(in_specs), len(out_specs), len(carries)
    c_in = [pl.BlockSpec(memory_space=pl.ANY) if c.in_hbm else whole(c.in_shape) for c in carries]

    def kernel(*refs):
        ins, c_ins = refs[:n_in], refs[n_in:n_in + n_c]
        rest = refs[n_in + n_c:]
        outs, c_outs, scratch = rest[:n_out], rest[n_out:n_out + n_c], rest[n_out + n_c:]
        parts = []
        for c in carries:
            parts.append(scratch[:len(c.scratch)])
            scratch = scratch[len(c.scratch):]
        step = pl.program_id(0)

        @pl.when(step == 0)
        def _():
            _, _, _, at_core, at_x, at_y = places()
            meet((at_core, at_x, at_y))

        for c, src, out, refs_c in zip(carries, c_ins, c_outs, parts):
            c.head(step, src, out, refs_c)
        body(*ins, *outs)

        @pl.when(step == grid - 1)
        def _():
            for c, src, out, refs_c in zip(carries, c_ins, c_outs, parts):
                c.tail(src, out, refs_c)

    return pl.pallas_call(
        kernel,
        grid=(grid,),
        in_specs=in_specs + c_in,
        out_specs=out_specs + [pl.BlockSpec(memory_space=pl.ANY) if c.out_hbm else whole(c.out_shape) for c in carries],
        out_shape=out_shape + [jax.ShapeDtypeStruct(c.out_shape, F32) for c in carries],
        scratch_shapes=[shape for c in carries for shape in c.scratch],
        input_output_aliases=aliases,
        compiler_params=pltpu.CompilerParams(
            vmem_limit_bytes=VMEM_LIMIT, dimension_semantics=("arbitrary",), collective_id=ident,
            has_side_effects=True),
        cost_estimate=cost_estimate,
    )(*args, *travel)


def combine(mine, other):
    top_a, top_b = column(mine, MAX_LANE), column(other, MAX_LANE)
    top = jnp.maximum(top_a, top_b)
    fa, fb = jnp.exp2(top_a - top), jnp.exp2(top_b - top)
    inv = 1.0 / (column(mine, SUM_LANE) * fa + column(other, SUM_LANE) * fb)
    ax = mine * (fa * inv) + other * (fb * inv)
    lane = lax.broadcasted_iota(jnp.int32, ax.shape, 1)
    return jnp.where(lane < CH, ax, 0.0), top, inv


def mlp_a_kernel(axa_ref, axb_ref, z0_ref, wvo_ref, mg_ref, ms_ref, w1_ref, b1_ref, w2_ref, b2_ref, do_ref,
                 z1_ref, h_ref, slope_ref, z2_ref, full_ref, dw2_ref, act_ref):
    ax, _, _ = combine(axa_ref[0], axb_ref[0])
    z1 = z0_ref[:] + mm(ax[:, :CPAD].astype(BF16), wvo_ref[:])
    z1_ref[0] = z1
    h = layer_norm(z1, mg_ref[:], ms_ref[:]).astype(BF16)
    h_ref[0] = h
    d_out = do_ref[0]

    @pl.when(pl.program_id(0) == 0)
    def _():
        dw2_ref[:] = jnp.zeros_like(dw2_ref)

    n = h.shape[0] // 2
    for rows_of in (slice(0, n), slice(n, 2 * n)):
        pre = mm(h[rows_of], w1_ref[:]) + b1_ref[:]
        sq = pre * pre
        t = jnp.tanh(pre * (GELU_A + (GELU_A * GELU_B) * sq))
        half_t = 0.5 + 0.5 * t
        act = (pre * half_t).astype(BF16)
        slope_ref[0, rows_of] = half_t + (0.5 * pre) * (1.0 - t * t) * (GELU_A + (3.0 * GELU_A * GELU_B) * sq)
        act_ref[rows_of] = act
        z2 = z1_ref[0, rows_of] + mm(act, w2_ref[:]) + b2_ref[:]
        z2_ref[0, rows_of] = z2
        full_ref[0, rows_of] = z2
    dw2_ref[:] += mm(act_ref[:].T, d_out)


def mlp_a(axa, axb, z0, wvo, mg, ms, w1, b1, w2, b2, d_out):
    half, n, _ = axa.shape
    d = z0.shape[1]
    per = lambda c: lead((1, n, c))
    shifted = lead((1, n, d), lambda i: lax.axis_index('cp') * half + i)
    return pl.pallas_call(
        mlp_a_kernel,
        grid=(half,),
        in_specs=[per(AXW), per(AXW), once((n, d)), once((CPAD, d)), whole((1, d)), whole((1, d)),
                  once((d, d)), whole((1, d)), once((d, d)), whole((1, d)), shifted],
        out_specs=[per(d), per(d), per(d), per(d), shifted, whole((d, d))],
        out_shape=[
            jax.ShapeDtypeStruct((half, n, d), F32),
            jax.ShapeDtypeStruct((half, n, d), BF16),
            jax.ShapeDtypeStruct((half, n, d), F32),
            jax.ShapeDtypeStruct((half, n, d), F32),
            jax.ShapeDtypeStruct(d_out.shape, F32),
            jax.ShapeDtypeStruct((d, d), F32),
        ],
        scratch_shapes=[pltpu.VMEM((n, d), BF16)],
        compiler_params=params(),
        cost_estimate=cost(2 * half * n * d * (3 * d + 512), half * n * d * 18),
        name="mlp_a",
    )(axa, axb, z0, wvo, mg, ms, w1, b1, w2, b2, d_out)


def mlp_w_kernel(h_ref, slope_ref, do_ref, w2_ref, dpre_ref, dw1_ref, db1_ref):
    @pl.when(pl.program_id(0) == 0)
    def _():
        dw1_ref[:] = jnp.zeros_like(dw1_ref)
        db1_ref[:] = jnp.zeros_like(db1_ref)

    d_act = mm_nt(do_ref[0], w2_ref[:]).astype(BF16).astype(F32)
    d_pre = d_act * slope_ref[0]
    db1_ref[:] += jnp.sum(d_pre, axis=0, keepdims=True)
    d_pre_low = d_pre.astype(BF16)
    dpre_ref[0] = d_pre_low
    dw1_ref[:] += mm(h_ref[0].T, d_pre_low)


def mlp_w(h, slope, d_out, w2, carries, travel):
    half, n, d = h.shape
    per = lambda c: lead((1, n, c))
    return carrier_call(
        mlp_w_kernel, 5, carries, travel, half,
        [per(d), per(d), lead((1, n, d), lambda i: lax.axis_index('cp') * half + i), whole((d, d))],
        [h, slope, d_out, w2],
        [per(d), whole((d, d)), whole((1, d))],
        [jax.ShapeDtypeStruct((half, n, d), BF16), jax.ShapeDtypeStruct((d, d), F32), jax.ShapeDtypeStruct((1, d), F32)],
        {}, cost(2 * half * n * d * 2 * d, half * n * d * 10))


def mlp_b_kernel(axa_ref, axb_ref, z1_ref, dpre_ref, do_ref, wvo_ref, mg_ref, w1_ref, db1_ref, g_ref, acc_ref):
    ax, top, inv = combine(axa_ref[0], axb_ref[0])
    n, _ = z1_ref.shape[1:]
    z1 = z1_ref[0]
    d_hid = mm_nt(dpre_ref[0], w1_ref[:]).astype(BF16).astype(F32)
    centred = z1 - jnp.mean(z1, axis=1, keepdims=True)
    rstd = lax.rsqrt(jnp.mean(centred * centred, axis=1, keepdims=True) + LN_EPS)
    hat = centred * rstd
    d_hat = d_hid * mg_ref[:]
    mean_a = jnp.mean(d_hat, axis=1, keepdims=True)
    mean_b = jnp.mean(d_hat * hat, axis=1, keepdims=True)
    d_out = do_ref[0].astype(F32)
    d_mid = d_out + rstd * (d_hat - mean_a - hat * mean_b)
    d_mid_low = d_mid.astype(BF16)

    @pl.when(pl.program_id(0) == 0)
    def _():
        acc_ref[:] = jnp.zeros_like(acc_ref)
        acc_ref[VEC_ROW + 3:VEC_ROW + 4, :] = db1_ref[:]

    p = mm(ax[:, :CPAD].astype(BF16).T, d_mid_low)
    acc_ref[0:n, :] += d_mid
    acc_ref[n:n + CPAD, :] += p
    acc_ref[VEC_ROW:VEC_ROW + 1, :] += jnp.sum(d_hid * hat, axis=0, keepdims=True)
    acc_ref[VEC_ROW + 1:VEC_ROW + 2, :] += jnp.sum(d_hid, axis=0, keepdims=True)
    acc_ref[VEC_ROW + 2:VEC_ROW + 3, :] += jnp.sum(d_out, axis=0, keepdims=True)
    d_ax = jnp.concatenate([mm_nt(d_mid_low, wvo_ref[:]), jnp.zeros((n, AXW - CPAD), F32)], axis=1)
    delta = jnp.sum(d_ax * ax, axis=1, keepdims=True)
    lane = lax.broadcasted_iota(jnp.int32, d_ax.shape, 1)
    g_ref[0] = jnp.where(lane == SUM_LANE, delta, jnp.where(lane == MAX_LANE, top, jnp.where(lane == INV_LANE, inv, d_ax)))


def mlp_b(axa, axb, z1, dpre, d_out, wvo, mg, w1, db1, carries, travel):
    half, n, _ = axa.shape
    d = z1.shape[2]
    per = lambda c: lead((1, n, c))
    shifted = lead((1, n, d), lambda i: lax.axis_index('cp') * half + i)
    return carrier_call(
        mlp_b_kernel, 1, carries, travel, half,
        [per(AXW), per(AXW), per(d), per(d), shifted, once((CPAD, d)), whole((1, d)), once((d, d)), whole((1, d))],
        [axa, axb, z1, dpre, d_out, wvo, mg, w1, db1],
        [per(AXW), whole((ACC_ROWS, d))],
        [jax.ShapeDtypeStruct((half, n, AXW), F32), jax.ShapeDtypeStruct((ACC_ROWS, d), F32)],
        {}, cost(2 * half * n * d * (d + 800), half * n * d * 10))


def attn_bwd_body(g_ref, ax_ref, e_ref, xn_ref, qpt_ref, t_in_ref, dxn_ref, t_ref):
    g = g_ref[0]
    xn = xn_ref[0]
    e = e_ref[0]
    beta = jnp.exp2(column(ax_ref[0], MAX_LANE) - column(g, MAX_LANE)) * column(g, INV_LANE)
    lane = lax.broadcasted_iota(jnp.int32, g.shape, 1)
    scaled = g * beta
    d_low = jnp.where(lane < CH, scaled, 0.0)[:, :CPAD].astype(BF16)
    d_a = mm(d_low, xn)
    d_s = (e.astype(F32) * (d_a - column(scaled, SUM_LANE))).astype(BF16)

    @pl.when(pl.program_id(0) == 0)
    def _():
        t_ref[:] = t_in_ref[:]

    t_ref[:] += mm_nt(xn, d_s)
    dxn_ref[0] = (mm(qpt_ref[:], d_s) + mm(d_low.T, e)).astype(BF16)


def attn_bwd(own, g, ax, e, xn, qpt, t_in, dxn_in, ident, carries, travel):
    half, n, m = e.shape
    per = lambda c: lead((1, n, c))

    def at(i):
        core = lax.axis_index('cp')
        return (core if own else 1 - core) * half + i

    shifted = lead((1, CPAD, m), at)
    in_specs = [per(AXW), per(AXW), per(m), shifted, whole((CPAD, n)), whole((CPAD, n))]
    args = [g, ax, e, xn, qpt, t_in]
    aliases = {}
    if dxn_in is not None:
        in_specs.append(pl.BlockSpec(memory_space=pl.ANY))
        args.append(dxn_in)
        aliases = {6: 0}

    def body(*refs):
        attn_bwd_body(*refs[:6], *refs[-2:])

    return carrier_call(
        body, ident, carries, travel, half, in_specs, args,
        [shifted, whole((CPAD, n))],
        [jax.ShapeDtypeStruct(xn.shape, BF16), jax.ShapeDtypeStruct((CPAD, n), F32)],
        aliases, cost(8 * half * n * m * 512, half * n * m * 6))


def x_post_kernel(base_ref, gain_ref, x_ref, mean_ref, rstd_ref, dxn_ref, za_ref, zb_ref, wa_ref, wb_ref, full_in_ref, dx_ref, sums_ref, full_ref, w_ref,
                  rows_ref, dg_ref, ds_ref):
    nb, lanes = x_ref.shape[1:]
    pitch = CPAD + ROW_GAP
    late = pl.program_id(0) >= pl.num_programs(0) // 2
    mine = late == (base_ref[0] == 1)

    @pl.when(late)
    def _():
        full_ref[0] = zb_ref[0]

    @pl.when(jnp.logical_not(late))
    def _():
        full_ref[0] = za_ref[0]

    @pl.when(mine)
    def _():
        w_ref[:] = wa_ref[:]

    @pl.when(jnp.logical_not(mine))
    def _():
        w_ref[:] = wb_ref[:]

    for b in range(nb):
        rows_ref[b * pitch:b * pitch + CPAD, :] = dxn_ref[b].astype(F32)
    zero = jnp.zeros((nb, lanes), F32)
    mean = mean_ref[:]
    rstd = rstd_ref[:]

    @pl.when(pl.program_id(0) == 0)
    def _():
        dg_ref[:] = jnp.zeros_like(dg_ref)
        ds_ref[:] = jnp.zeros_like(ds_ref)

    def gather(c, acc):
        da, db = acc
        hat = (x_ref[c].astype(F32) - mean) * rstd
        dxn = rows_ref[pl.ds(c, nb, stride=pitch), :]
        dh = dxn * gain_ref[c]
        prod = dxn * hat
        dg_ref[c] += prod[:8] + prod[8:]
        ds_ref[c] += dxn[:8] + dxn[8:]
        return da + dh, db + dh * hat

    da, db = lax.fori_loop(0, CH, gather, (zero, zero), unroll=9)
    mean_a = da * (1.0 / CH)
    mean_b = db * (1.0 / CH)

    def put(c, carry):
        hat = (x_ref[c].astype(F32) - mean) * rstd
        dxn = rows_ref[pl.ds(c, nb, stride=pitch), :]
        dx_ref[c] = (rstd * (dxn * gain_ref[c] - mean_a - hat * mean_b)).astype(BF16)
        return carry

    lax.fori_loop(0, CH, put, 0, unroll=9)

    @pl.when(pl.program_id(0) == pl.num_programs(0) - 1)
    def _():
        for k, ref in enumerate((dg_ref, ds_ref)):
            part = jnp.concatenate([jnp.sum(ref[:], axis=1), jnp.zeros((AXW - CH, lanes), F32)], axis=0)
            sums_ref[k:k + 1, :] = jnp.sum(part.T, axis=0, keepdims=True)


def x_post(core, x_gain, x_cm, mean, rstd, dxn, za, zb, full, w_own, w_got):
    _, nb, m = x_cm.shape
    half, n, d = 2 * za.shape[0], *za.shape[1:]
    lanes = m // half
    slab = 2 * w_own.shape[0] // half
    chan = trail((CH, nb, lanes))
    stat = trail((nb, lanes))

    def piece(side):
        last = half // 2 - 1
        return pl.BlockSpec((slab, d), lambda i, core: (
            jnp.clip(i - (core[0] if side else 1 - core[0]) * (half // 2), 0, last), 0))

    return pl.pallas_call(
        x_post_kernel,
        grid_spec=pltpu.PrefetchScalarGridSpec(
            num_scalar_prefetch=1,
            grid=(half,),
            in_specs=[
                pl.BlockSpec(memory_space=pltpu.SMEM),
                chan, stat, stat,
                trail((nb, CPAD, lanes)),
                lead((1, n, d), lambda i: jnp.minimum(i, half // 2 - 1)),
                lead((1, n, d), lambda i: jnp.maximum(i - half // 2, 0)),
                piece(True), piece(False),
                pl.BlockSpec(memory_space=pl.ANY),
            ],
            out_specs=[chan, whole((2, AXW)), pl.BlockSpec((1, n, d), lambda i, core: ((1 - core[0]) * half + i, 0, 0)),
                       lead((slab, d))],
            scratch_shapes=[pltpu.VMEM(((CPAD + ROW_GAP) * nb, lanes), F32),
                            pltpu.VMEM((CH, 8, lanes), F32), pltpu.VMEM((CH, 8, lanes), F32)],
        ),
        out_shape=[
            jax.ShapeDtypeStruct(x_cm.shape, BF16),
            jax.ShapeDtypeStruct((2, AXW), F32),
            jax.ShapeDtypeStruct(full.shape, F32),
            jax.ShapeDtypeStruct((2 * w_own.shape[0], d), F32),
        ],
        input_output_aliases={10: 2},
        compiler_params=params(),
        cost_estimate=cost(6e9, 6 * nb * CH * m + 8 * half * n * d),
        name="x_post",
    )(core, x_gain, x_cm, mean, rstd, dxn, za, zb, w_own, w_got, full)


def finish_kernel(devices, x_ref, ta_ref, tb_ref, tc_ref, td_ref, own_ref, gx_ref, gy_ref, o_ref, t_ref, acc_ref,
                  got_ref, t_all, acc_all, send_sem, recv_sem):
    dp, cp = devices
    my_dp, my_cp = lax.axis_index('dp'), lax.axis_index('cp')
    core, x, y, at_core, _, _ = places()
    peers = [(i, j) for i in range(dp) for j in range(cp)][1:]
    ids = [(lax.rem(my_dp + i, dp), lax.rem(my_cp + j, cp)) for i, j in peers]
    meet(ids)
    copies = [remote(x_ref, got_ref.at[k], (send_sem, recv_sem), k, dev) for k, dev in enumerate(ids)]
    start_all(copies)
    th, ah = ta_ref.shape[0], 4 * own_ref.shape[1]
    eighth = own_ref.shape[1]
    base = core * ah
    t_all[pl.ds(pl.multiple_of(core * th, 8), th), :] = (ta_ref[:] + tb_ref[:]) + (tc_ref[:] + td_ref[:])
    t_copy = remote(rows(t_all, core * th, th), rows(t_all, core * th, th), (send_sem, recv_sem), len(ids), at_core)
    for start, ref in ((x * eighth, own_ref.at[0]), ((1 - x) * eighth, gx_ref),
                       ((2 + y) * eighth, own_ref.at[1]), ((3 - y) * eighth, gy_ref)):
        acc_all[pl.ds(pl.multiple_of(base + start, 8), eighth), :] = ref[:]
    t_copy.start()
    acc_copy = remote(rows(acc_all, base, ah), rows(acc_all, base, ah), (send_sem, recv_sem), len(ids) + 1, at_core)
    acc_copy.start()
    wait_all(copies)
    o_ref[:] = x_ref[:] + jnp.sum(got_ref[:], axis=0)
    t_copy.wait()
    t_ref[:] = t_all[:]
    acc_copy.wait()
    acc_ref[:] = acc_all[:]


def finish(mesh, x, t_parts, own, got_x, got_y):
    count = mesh.size - 1
    t_shape = (2 * t_parts[0].shape[0], t_parts[0].shape[1])
    acc_shape = (8 * own.shape[1], own.shape[2])
    vmem = pl.BlockSpec(memory_space=pltpu.VMEM)
    return pl.pallas_call(
        functools.partial(finish_kernel, (mesh.shape['dp'], mesh.shape['cp'])),
        in_specs=[vmem] * 8,
        out_specs=[vmem] * 3,
        out_shape=[jax.ShapeDtypeStruct(shape, F32) for shape in (x.shape, t_shape, acc_shape)],
        scratch_shapes=[pltpu.VMEM((count,) + x.shape, F32), pltpu.VMEM(t_shape, F32), pltpu.VMEM(acc_shape, F32)]
        + dma_sems(count + 2),
        compiler_params=pltpu.CompilerParams(vmem_limit_bytes=VMEM_LIMIT, collective_id=0, has_side_effects=True),
        name="finish",
    )(x, *t_parts, own, got_x, got_y)


def prologue_kernel(scale, z0_ref, zg_ref, zs_ref, wq_ref, wk_in_ref, wv_in_ref, wo_ref,
                    zn_ref, q_ref, qp_ref, qpt_ref, wvo_ref, wk_ref, wv_ref):
    for src, dst in ((wk_in_ref, wk_ref), (wv_in_ref, wv_ref)):
        dst[256:, :] = jnp.zeros((CPAD - 256, src.shape[1]), BF16)
        dst[:CH, :] = src[:]
    zn = layer_norm(z0_ref[:], zg_ref[:], zs_ref[:]).astype(BF16)
    zn_ref[:] = zn
    q = mm(zn, wq_ref[:]).astype(BF16)
    q_ref[:] = q
    wk = wk_ref[:]
    qp_ref[:] = (mm_nt(q, wk) * (scale * LOG2E)).astype(BF16)
    qpt_ref[:] = (mm_nt(wk, q) * scale).astype(BF16)
    wvo_ref[:] = mm(wv_ref[:], wo_ref[:]).astype(BF16)


def prologue(scale, z0, zg, zs, wq, wk, wv, wo):
    n, d = z0.shape
    vmem = pl.BlockSpec(memory_space=pltpu.VMEM)
    return pl.pallas_call(
        functools.partial(prologue_kernel, scale),
        in_specs=[vmem] * 7,
        out_specs=[vmem] * 7,
        out_shape=[jax.ShapeDtypeStruct(shape, BF16)
                   for shape in ((n, d), (n, d), (n, CPAD), (CPAD, n), (CPAD, d), (CPAD, d), (CPAD, d))],
        compiler_params=pltpu.CompilerParams(vmem_limit_bytes=VMEM_LIMIT),
        cost_estimate=cost(3e9, 12e6),
        name="prologue",
    )(z0, zg, zs, wq, wk, wv, wo)


def final_kernel(scale, t_ref, acc_ref, z0_ref, zg_ref, zn_ref, q_ref, wq_ref, wk_ref, wv_ref, wo_ref,
                 dlat_ref, dzg_ref, dzs_ref, dwq_ref, dwk_ref, dwv_ref, dwo_ref):
    n = z0_ref.shape[0]
    p_low = acc_ref[n:n + CPAD, :].astype(BF16)
    dwo_ref[:] = mm(wv_ref[:].T, p_low)
    dwv_ref[:] = mm_nt(p_low, wo_ref[:])[:CH]
    t_low = (t_ref[:] * scale).astype(BF16)
    dwk_ref[:] = mm(t_low, q_ref[:])[:CH]
    d_q = mm(t_low.T, wk_ref[:]).astype(BF16)
    dwq_ref[:] = mm(zn_ref[:].T, d_q)
    d_zn = mm_nt(d_q, wq_ref[:])
    z0 = z0_ref[:]
    centred = z0 - jnp.mean(z0, axis=1, keepdims=True)
    rstd = lax.rsqrt(jnp.mean(centred * centred, axis=1, keepdims=True) + LN_EPS)
    hat = centred * rstd
    dzg_ref[:] = jnp.sum(d_zn * hat, axis=0, keepdims=True)
    dzs_ref[:] = jnp.sum(d_zn, axis=0, keepdims=True)
    d_hat = d_zn * zg_ref[:]
    mean_a = jnp.mean(d_hat, axis=1, keepdims=True)
    mean_b = jnp.mean(d_hat * hat, axis=1, keepdims=True)
    dlat_ref[:] = acc_ref[:n, :] + rstd * (d_hat - mean_a - hat * mean_b)


def final(scale, t, acc, z0, zg, zn, q, wq, wk, wv, wo):
    n, d = z0.shape
    vmem = pl.BlockSpec(memory_space=pltpu.VMEM)
    shapes = ((n, d), (1, d), (1, d), (d, d), (CH, d), (CH, d), (d, d))
    return pl.pallas_call(
        functools.partial(final_kernel, scale),
        in_specs=[vmem] * 10,
        out_specs=[vmem] * 7,
        out_shape=[jax.ShapeDtypeStruct(shape, F32) for shape in shapes],
        compiler_params=pltpu.CompilerParams(vmem_limit_bytes=VMEM_LIMIT),
        cost_estimate=cost(4e9, 25e6),
        name="final",
    )(t, acc, z0, zg, zn, q, wq, wk, wv, wo)


def solution(mesh):
    x_spec, row_spec = P('dp', 'cp'), P('dp')
    vec_spec = mat_spec = P()
    in_specs = (x_spec, mat_spec, vec_spec, vec_spec, vec_spec, vec_spec, mat_spec, mat_spec, mat_spec, mat_spec,
                vec_spec, vec_spec, mat_spec, vec_spec, mat_spec, vec_spec, row_spec)
    out_specs = (row_spec, x_spec, mat_spec, vec_spec, vec_spec, vec_spec, vec_spec, mat_spec, mat_spec, mat_spec, mat_spec,
                 vec_spec, vec_spec, mat_spec, vec_spec, mat_spec, vec_spec)
    swap = [(0, 1), (1, 0)]

    def step(inputs, latents, x_gain, x_shift, z_gain, z_shift, w_query, w_key, w_value, w_out, m_gain, m_shift, w_up, b_up, w_down, b_down, d_out):
        qk_scale = w_query.shape[1] ** -0.5
        n, d = latents.shape
        half = inputs.shape[0] // 2
        core = lax.axis_index('cp')
        as_ints = lambda *vals: jnp.stack([v.astype(jnp.int32) for v in vals])
        mine = as_ints(core * half, core * (d // 2))
        other = as_ints((1 - core) * half, (1 - core) * (d // 2))
        row = lambda vec: vec.reshape(1, -1)

        x_cm = jnp.transpose(inputs, (2, 0, 1))
        xn, x_mean, x_rstd = x_prep(x_cm, x_gain, x_shift)

        z_norm, queries, qp, qpt, wvo, wk_pad, wv_pad = prologue(
            qk_scale, latents, row(z_gain), row(z_shift), w_query, w_key, w_value, w_out)

        e_other, ax_other = attn_fwd(other, qp, xn, half)
        ax_got = lax.ppermute(ax_other, 'cp', swap)
        e_mine, ax_mine = attn_fwd(mine, qp, xn, half)

        flip = lambda bit: [(k, k ^ bit) for k in range(4)]
        z1, hid, slope, z2, full, dw2 = mlp_a(
            ax_mine, ax_got, latents, wvo, row(m_gain), row(m_shift), w_up, row(b_up), w_down, row(b_down), d_out)
        dpre, dw1, db1, w2_pieces = mlp_w(
            hid, slope, d_out, w_down, [carry(d, d, (0, 1, 2), (0, 2, 6))], [dw2])
        g_mine, acc, w2_half, w1_eighths, za_got = mlp_b(
            ax_mine, ax_got, z1, dpre, d_out, wvo, row(m_gain), w_up, db1,
            [carry(d, d, (3, 4), (0, 2)), carry(d, d, (0, 1), (0, 2)), carry_rows(z2.shape, 0, half // 2, 2)],
            [w2_pieces, dw1, z2])
        g_got = lax.ppermute(g_mine, 'cp', swap)
        dxn, t_part, w1_eighths, acc_half = attn_bwd(
            True, g_mine, ax_mine, e_mine, xn, qpt, jnp.zeros((CPAD, n), F32), None, 3,
            [carry(d, d, (2, 3), (0, 3)), carry(ACC_ROWS, d, (0,), (0,))], [w1_eighths, acc])
        w2_half, dxn = lax.optimization_barrier((w2_half, dxn))
        w2_got = lax.ppermute(w2_half, 'cp', swap)
        dxn, t_part, acc_eighths, zb_got = attn_bwd(
            False, g_got, ax_other, e_other, xn, qpt, t_part, dxn, 4,
            [carry(ACC_ROWS, d, (1, 2, 3), (0, 5, 7)), carry_rows(z2.shape, half // 2, half // 2, 0)],
            [acc_half, z2])
        w1_eighths, dxn = lax.optimization_barrier((w1_eighths, dxn))

        def halves(own):
            got_x = lax.ppermute(own[0], 'dp', flip(1))
            got_y = lax.ppermute(own[1], 'dp', flip(2))
            return got_x, got_y

        w1_x, w1_y = halves(w1_eighths)
        acc_x, acc_y = halves(acc_eighths)

        t_mine = lax.dynamic_slice_in_dim(t_part, core * (CPAD // 2), CPAD // 2, 0)
        t_send = lax.dynamic_slice_in_dim(t_part, (1 - core) * (CPAD // 2), CPAD // 2, 0)
        t_mine = t_mine + lax.ppermute(t_send, 'cp', swap)
        t_parts = [t_mine]
        for bit in (1, 2, 3):
            t_parts.append(lax.ppermute(t_mine, 'dp', [(k, k ^ bit) for k in range(4)]))
        dx_cm, sums, z_out, d_w_down = x_post(
            core.astype(jnp.int32).reshape(1), x_gain, x_cm, x_mean, x_rstd, dxn, za_got, zb_got, full, w2_half, w2_got)
        sums, t_sum, acc = finish(mesh, sums, t_parts, acc_eighths, acc_x, acc_y)
        d_x_gain, d_x_shift = sums[0, :CH], sums[1, :CH]
        order = lambda bit, own, got: jnp.where(
            bit == 0, jnp.concatenate([own, got], 0), jnp.concatenate([got, own], 0))
        chip = lax.axis_index('dp')
        w1_half = jnp.concatenate([
            order(lax.rem(chip, 2), w1_eighths[0], w1_x), order(chip // 2, w1_eighths[1], w1_y)], 0)
        w1_got = lax.ppermute(w1_half, 'cp', swap)
        d_w_up = order(core, w1_half, w1_got)

        d_m_gain, d_m_shift, d_b_down, d_b_up = (acc[VEC_ROW + k] for k in range(4))
        d_lat, d_z_gain, d_z_shift, d_w_query, d_w_key, d_w_value, d_w_out = final(
            qk_scale, t_sum, acc, latents, row(z_gain), z_norm, queries, w_query, wk_pad, wv_pad, w_out)
        return (z_out, jnp.transpose(dx_cm, (1, 2, 0)), d_lat, d_x_gain, d_x_shift, d_z_gain[0], d_z_shift[0],
                d_w_query, d_w_key, d_w_value, d_w_out, d_m_gain, d_m_shift, d_w_up, d_b_up, d_w_down, d_b_down)

    return jax.shard_map(step, mesh=mesh, in_specs=in_specs, out_specs=out_specs, check_vma=False)
```

time: 1260 us -> 335 us (0.27)
  matrix products: 688 us -> 0 us
  Pallas kernels: 0 us -> 290 us
  waiting for transfers between devices: 260 us -> 19.7 us
  other arithmetic: 210 us -> 8.49 us
  blocking collectives: 53.2 us -> 0 us
  local copies, waits for them, and re-layouts: 28.2 us -> 5.92 us
  between operations: 15 us -> 0.85 us
    dot_general x24 -> x0, matrix products: 688 us -> none  [contract(): jnp.einsum(einsum_form, lhs_arr, rhs_arr, preferred_element_type=ACC_TYPE)]
    pallas_call x0 -> x12, Pallas kernels: none -> 290 us  [the longest x4 132 us: carrier_call(): pl.pallas_call(kernel, grid=(grid,), in_specs=in_specs + c_in, out_specs=...]
    psum x3 -> x0, waiting for transfers between devices: 260 us -> none  [the longest x1 180 us: local_step(): lax.psum(mlp_grads, 'dp')]
    reduce_sum x11 -> x0, other arithmetic: 138 us -> none  [the longest x3 60.9 us: layer_norm(): return centred * lax.rsqrt(variance + LN_EPS) * ln_gain + ln_shift]
    convert_element_type x3 -> x0, other arithmetic: 67.8 us -> none  [the longest x1 27.9 us: local_step(): d_logits = (attn_probs * (d_probs - row_dot) * qk_scale).astype(LOW_TYPE)]
    psum x4 -> x0, blocking collectives: 49.1 us -> none  [the longest x1 24.5 us: local_step(): lax.psum(shared_grads, ('dp', 'cp'))]
    unnamed x151 -> x12, local copies, waits for them, and re-layouts: 28.2 us -> 0.03 us
    ppermute x0 -> x12, waiting for transfers between devices: none -> 19.7 us  [the longest x2 10.2 us: halves(): got_y = lax.ppermute(own[1], 'dp', flip(2))]
  transfers between devices with their start and end apart: 3 -> 12, of which waited for: 2 -> 4; matrix products, arithmetic and copies ran while one was open for 14% -> 3% of each run, Pallas kernels for 0% -> 36%
where the time goes in v2:
time: 335 us; the launch traced here: 334 us
  Pallas kernels  290 us (87%)
  waiting for transfers between devices  19.7 us (6%)
  starting transfers between devices  9.01 us (3%)
  other arithmetic  8.49 us (3%)
  local copies, waits for them, and re-layouts  5.92 us (2%)
    pallas_call x4, Pallas kernels, carrier_call(): pl.pallas_call(kernel, grid=(grid,), in_specs=in_specs + c_in, out_specs=...  132 us
    pallas_call x1, Pallas kernels, mlp_a(): pl.pallas_call(mlp_a_kernel, grid=(half,), in_specs=[per(AXW), per(AXW),...  56.5 us
    pallas_call x1, Pallas kernels, x_post(): pl.pallas_call(x_post_kernel, grid_spec=pltpu.PrefetchScalarGridSpec(num_...  29.5 us
    pallas_call x2, Pallas kernels, attn_fwd(): pl.pallas_call(attn_fwd_kernel, grid_spec=pltpu.PrefetchScalarGridSpec(nu...  26.8 us
    pallas_call x1, Pallas kernels, x_prep(): pl.pallas_call(x_prep_kernel, grid=(m // lanes,), in_specs=[pl.BlockSpec(...  16.6 us
    pallas_call x1, Pallas kernels, final(): pl.pallas_call(functools.partial(final_kernel, scale), in_specs=[vmem] *...  12.1 us
    ppermute x2, waiting for transfers between devices, halves(): got_y = lax.ppermute(own[1], 'dp', flip(2))  10.2 us
    pallas_call x1, Pallas kernels, finish(): pl.pallas_call(functools.partial(finish_kernel, (mesh.shape['dp'], mesh.s...  9.42 us
  transfers between devices with their start and end apart: 12, of which 4 were waited for; matrix products, arithmetic and copies ran while one was open for 3% of the time, Pallas kernels for 36%

profile of v2, /device:TPU:0, one launch (start us, length us, event | category | flops | bytes accessed | tf_op | source)
XLA Modules:
  0.0 333.9 jit_solution(1930468184776878730)
XLA Ops:
  0.7 0.6 pad_add_fusion.1.base_ref
  1.2 16.6 %x_prep.1 = (bf16[16,272,1024]{2,1,0:T(8,128)(2,1)}, f32[16,1024]{1,0:T(8,128)}, f32[16,1024]{1,0:T(8,128)}) custom-call(f32[261]{0:T(512)} %gain_ref.3, f32[261]{0:T(512)} %shift_ref.1, bf16[261,16,1024]{2,1,0:T(8,128)(2,1)} %bitcast.27), custom_call_target="tpu_custom_call" | custom-call | flops 3000000000 | bytes 17104896 | tf_op jit(solution)/shard_map/x_prep/pallas_call | solution.py:109
  17.9 7.1 %prologue.1 = (bf16[512,1024]{1,0:T(8,128)(2,1)}, bf16[512,1024]{1,0:T(8,128)(2,1)}, bf16[512,272]{1,0:T(8,128)(2,1)}, bf16[272,512]{1,0:T(8,128)(2,1)}, bf16[27...) custom-call(f32[512,1024]{1,0:T(8,128)} %z0_ref.5, f32[1,1024]{1,0:T(1,128)} %bitcast.40, ...), custom_call_target="tpu_custom_call" | custom-call | flops 3000000000 | bytes 12000000 | tf_op jit(solution)/shard_map/prologue/pallas_call | solution.py:743
  25.0 13.4 %attn_fwd.3 = (bf16[8,512,1024]{2,1,0:T(8,128)(2,1)}, f32[8,512,384]{2,1,0:T(8,128)}) custom-call(s32[2]{0:T(128)} %pad_add_fusion.1.base_ref, bf16[512,272]{1,0:T(8,128)(2,1)} %get-tuple-element.74.qp_ref, bf16[16,272,1024]{2,1,0:T(8,128)(2,1)} %get-tuple-element.75.xn_ref.refs_3_), custom_call_target="tpu_custom_call" | custom-call | flops 8589934592 | bytes 12582912 | tf_op jit(solution)/shard_map/attn_fwd/pallas_call | solution.py:149
  38.4 0.8 collective-permute-start
  39.2 0.6 pad_add_fusion.base_ref
  39.8 13.4 %attn_fwd.2 = (bf16[8,512,1024]{2,1,0:T(8,128)(2,1)}, f32[8,512,384]{2,1,0:T(8,128)}) custom-call(s32[2]{0:T(128)} %pad_add_fusion.base_ref, bf16[512,272]{1,0:T(8,128)(2,1)} %get-tuple-element.74.qp_ref, bf16[16,272,1024]{2,1,0:T(8,128)(2,1)} %get-tuple-element.75.xn_ref.refs_3_), custom_call_target="tpu_custom_call" | custom-call | flops 8589934592 | bytes 12582912 | tf_op jit(solution)/shard_map/attn_fwd/pallas_call | solution.py:149
  53.2 0.0 collective-permute-done.axb_ref.refs_1_
  53.2 56.5 %mlp_a.1 = (f32[8,512,1024]{2,1,0:T(8,128)}, bf16[8,512,1024]{2,1,0:T(8,128)(2,1)}, f32[8,512,1024]{2,1,0:T(8,128)}, f32[8,512,1024]{2,1,0:T(8,128)}, f32[16,512,1024]{2,1,0:T(8,128)}, /*index=5*/f32[1024,1024]{1,0:T(8,128)}) custom-call(f32[8,512,384]{2,1,0:T(8,128)} %get-tuple-element.76.axa_ref.refs_0_.refs_1_, ...), custom_call_target="tpu_custom_call" | custom-call | flops 30064771072 | bytes 75497472 | tf_op jit(solution)/shard_map/mlp_a/pallas_call | solution.py:432
  109.7 34.9 %shard_map.296 = (bf16[8,512,1024]{2,1,0:T(8,128)(2,1)}, f32[1024,1024]{1,0:T(8,128)}, f32[1,1024]{1,0:T(1,128)}, f32[2,64,1024]{2,1,0:T(8,128)}) custom-call(bf16[8,512,1024]{2,1,0:T(8,128)(2,1)} %get-tuple-element.80.refs_0_, f32[8,512,1024]{2,1,0:T(8,128)} %get-tuple-element.81.refs_1_, bf16[16,512,1024]{2,1,0:T(8,128)(2,1)} %refs_4_.1, ...), custom_call_target="tpu_custom_call" | custom-call | flops 17179869184 | bytes 41943040 | tf_op jit(solution)/shard_map/pallas_call | solution.py:374
  144.6 42.9 %shard_map.297 = (f32[8,512,384]{2,1,0:T(8,128)}, f32[896,1024]{1,0:T(8,128)}, f32[512,1024]{1,0:T(8,128)}, f32[2,128,1024]{2,1,0:T(8,128)}, f32[4,512,1024]{2,1,0:T(8,128)}) custom-call(f32[8,512,384]{2,1,0:T(8,128)} %get-tuple-element.76.axa_ref.refs_0_.refs_1_, f32[8,512,384]{2,1,0:T(8,128)} %collective-permute-done.axb_ref.refs_1_, ...), custom_call_target="tpu_custom_call" | custom-call | flops 15300820992 | bytes 41943040 | tf_op jit(solution)/shard_map/pallas_call | solution.py:374
  187.5 0.0 collective-permute-start.1
  187.5 0.9 broadcast_in_dim.3.refs_5_
  188.4 24.4 %shard_map.298 = (bf16[16,272,1024]{2,1,0:T(8,128)(2,1)}, f32[272,512]{1,0:T(8,128)}, f32[2,128,1024]{2,1,0:T(8,128)}, f32[448,1024]{1,0:T(8,128)}) custom-call(f32[8,512,384]{2,1,0:T(8,128)} %get-tuple-element.88.refs_0_, f32[8,512,384]{2,1,0:T(8,128)} %get-tuple-element.76.axa_ref.refs_0_.refs_1_, bf16[8,512,1024]{2,1,0:T(8,128)(2,1)} %get-tuple-element.89.refs_2_, ...), custom_call_target="tpu_custom_call" | custom-call | flops 17179869184 | bytes 25165824 | tf_op jit(solution)/shard_map/pallas_call | solution.py:374
  212.8 0.0 collective-permute-start.2
  212.8 0.0 collective-permute-done.1.refs_0_
  212.8 29.8 %shard_map.299 = (bf16[16,272,1024]{2,1,0:T(8,128)(2,1)}, f32[272,512]{1,0:T(8,128)}, f32[2,112,1024]{2,1,0:T(8,128)}, f32[4,512,1024]{2,1,0:T(8,128)}) custom-call(f32[8,512,384]{2,1,0:T(8,128)} %collective-permute-done.1.refs_0_, f32[8,512,384]{2,1,0:T(8,128)} %get-tuple-element.77.refs_1_, ...), custom_call_target="tpu_custom_call", output_to_operand_aliasing={{0}: (6, {})} | custom-call | flops 17179869184 | bytes 25165824 | tf_op jit(solution)/shard_map/pallas_call | solution.py:374
  242.7 1.3 slice_bitcast_fusion.1
  243.9 0.6 collective-permute-start.10
  244.5 1.5 collective-permute-start.9
  246.0 0.0 copy-start.4
  246.0 0.0 copy-start.2
  246.0 10.2 %collective-permute-done.10 = f32[128,1024]{1,0:T(8,128)S(1)} collective-permute-done((f32[128,1024]{1,0:T(8,128)S(1)}, f32[128,1024]{1,0:T(8,128)S(1)}, u32[]{:S(2)}, u32[]{:S(2)}) %collective-permute-start.10) | collective-permute-done | bytes 524320 | tf_op jit(solution)/shard_map/ppermute | solution.py:845
  256.2 0.1 maximum_select_fusion.2
  256.3 0.0 copy-start
  256.3 0.1 collective-permute-done.9
  256.5 0.1 maximum_select_fusion.1
  256.6 0.0 copy-start.1
  256.6 1.7 pad_maximum_fusion
  258.3 0.0 collective-permute-start.11
  258.3 0.0 copy-done.4
  258.3 0.5 collective-permute-start.3
  258.8 0.0 copy-done.2
  258.8 0.8 slice_bitcast_fusion.2
  259.7 0.0 copy-done
  259.7 0.0 copy-done.1
  259.7 1.4 collective-permute-start.7
  261.1 0.6 collective-permute-start.8
  261.7 1.3 collective-permute-done.3
  263.1 0.0 copy-start.3
  263.1 1.4 collective-permute-start.4
  264.5 0.0 collective-permute-done.2.wb_ref
  264.5 0.6 collective-permute-start.5
  265.2 7.9 %collective-permute-done.7.gx_ref = f32[112,1024]{1,0:T(8,128)S(1)} collective-permute-done((f32[112,1024]{1,0:T(8,128)S(1)}, f32[112,1024]{1,0:T(8,128)S(1)}, u32[]{:S(2)}, u32[]{:S(2)}) %collective-permute-start.7) | collective-permute-done | bytes 458784 | tf_op jit(solution)/shard_map/ppermute | solution.py:844
  273.1 0.0 copy-start.5
  273.1 1.5 collective-permute-start.6
  274.5 29.5 %x_post.1 = (bf16[261,16,1024]{2,1,0:T(8,128)(2,1)}, f32[2,384]{1,0:T(2,128)}, f32[16,512,1024]{2,1,0:T(8,128)}, f32[1024,1024]{1,0:T(8,128)}) custom-call(s32[1]{0:T(128)} %bitcast.base_ref, f32[261]{0:T(512)} %gain_ref.3, bf16[261,16,1024]{2,1,0:T(8,128)(2,1)} %bitcast.28, ...), custom_call_target="tpu_custom_call", output_to_operand_aliasing={{2}: (10, {})} | custom-call | flops 6000000000 | bytes 59211776 | tf_op jit(solution)/shard_map/x_post/pallas_call | solution.py:647
  304.0 0.0 copy-done.3
  304.0 0.0 copy-done.5
  304.0 0.0 collective-permute-done.8.gy_ref
  304.0 0.0 collective-permute-done.4.tb_ref
  304.0 0.0 collective-permute-done.5.tc_ref
  304.0 0.0 collective-permute-done.6.td_ref
  304.1 9.4 %finish.1 = (f32[2,384]{1,0:T(2,128)}, f32[272,512]{1,0:T(8,128)}, f32[896,1024]{1,0:T(8,128)}) custom-call(f32[2,384]{1,0:T(2,128)} %get-tuple-element.108.x_ref, f32[136,512]{1,0:T(8,128)} %copy-done.3, f32[136,512]{1,0:T(8,128)} %collective-permute-done.4.tb_ref, f32[136,512]{1,0:T(8,128)} %collective-permute-done.5.tc_ref, ...), custom_call_target="tpu_custom_call" | custom-call | tf_op jit(solution)/shard_map/finish/pallas_call | solution.py:713
  313.5 1.4 slice_reduce_fusion
  314.8 1.5 fusion
  316.4 12.1 %final.1 = (f32[512,1024]{1,0:T(8,128)}, f32[1,1024]{1,0:T(1,128)}, f32[1,1024]{1,0:T(1,128)}, f32[1024,1024]{1,0:T(8,128)}, f32[261,1024]{1,0:T(8,128)}, /*index=5*/f32[261,1024]{1,0:T(8,128)}, f32[1024,1024]{1,0:T(8,128)}) custom-call(f32[272,512]{1,0:T(8,128)} %get-tuple-element.111.t_ref, f32[896,1024]{1,0:T(8,128)} %get-tuple-element.112.acc_ref, ...), custom_call_target="tpu_custom_call" | custom-call | flops 4000000000 | bytes 25000000 | tf_op jit(solution)/shard_map/final/pallas_call | solution.py:782
  328.5 0.0 collective-permute-done.11
  328.5 5.4 %maximum_select_fusion = f32[1024,1024]{1,0:T(8,128)} fusion(f32[512,1024]{1,0:T(8,128)} %collective-permute-done.11, f32[256,1024]{1,0:T(8,128)} %copy-done, f32[256,1024]{1,0:T(8,128)} %copy-done.1, pred[]{:T(512)S(6)} %eq.9), kind=kLoop, calls=%fused_computation | loop fusion | flops 5242880 | bytes 8388609 | tf_op jit(solution)/shard_map/jit(_where)/select_n | solution.py:861
  (2 shorter events, 0.1 us)
Async XLA Ops:
  38.4 14.8 %collective-permute-start = (f32[8,512,384]{2,1,0:T(8,128)}, f32[8,512,384]{2,1,0:T(8,128)}, u32[]{:S(2)}, u32[]{:S(2)}) collective-permute-start(f32[8,512,384]{2,1,0:T(8,128)} %get-tuple-element.77.refs_1_), channel_id=1, source_target_pairs={{0,1},{1,0},{2,3},{3,2},{4,5},{5,4},{6,7},{7,6}} | collective-permute-start | bytes 18874376 | tf_op jit(solution)/shard_map/ppermute | solution.py:819
  187.5 25.3 %collective-permute-start.1 = (f32[8,512,384]{2,1,0:T(8,128)}, f32[8,512,384]{2,1,0:T(8,128)}, u32[]{:S(2)}, u32[]{:S(2)}) collective-permute-start(f32[8,512,384]{2,1,0:T(8,128)} %get-tuple-element.88.refs_0_), channel_id=1, source_target_pairs={{0,1},{1,0},{2,3},{3,2},{4,5},{5,4},{6,7},{7,6}} | collective-permute-start | bytes 18874376 | tf_op jit(solution)/shard_map/ppermute | solution.py:831
  212.8 51.7 %collective-permute-start.2 = (f32[512,1024]{1,0:T(8,128)}, f32[512,1024]{1,0:T(8,128)}, u32[]{:S(2)}, u32[]{:S(2)}) collective-permute-start(f32[512,1024]{1,0:T(8,128)} %get-tuple-element.104.wa_ref), channel_id=1, source_target_pairs={{0,1},{1,0},{2,3},{3,2},{4,5},{5,4},{6,7},{7,6}} | collective-permute-start | bytes 6291464 | tf_op jit(solution)/shard_map/ppermute | solution.py:836
  243.9 12.3 %collective-permute-start.10 = (f32[128,1024]{1,0:T(8,128)S(1)}, f32[128,1024]{1,0:T(8,128)S(1)}, u32[]{:S(2)}, u32[]{:S(2)}) collective-permute-start(f32[128,1024]{1,0:T(8,128)S(1)} %get-tuple-element.134), channel_id=1, source_target_pairs={{0,4},{2,6},{4,0},{6,2},{1,5},{3,7},{5,1},{7,3}} | collective-permute-start | bytes 1572872 | tf_op jit(solution)/shard_map/ppermute | solution.py:845
  244.5 12.0 %collective-permute-start.9 = (f32[128,1024]{1,0:T(8,128)S(1)}, f32[128,1024]{1,0:T(8,128)S(1)}, u32[]{:S(2)}, u32[]{:S(2)}) collective-permute-start(f32[128,1024]{1,0:T(8,128)S(1)} %get-tuple-element.133), channel_id=1, source_target_pairs={{0,2},{2,0},{4,6},{6,4},{1,3},{3,1},{5,7},{7,5}} | collective-permute-start | bytes 1572872 | tf_op jit(solution)/shard_map/ppermute | solution.py:844
  246.0 12.3 %copy-start.4 = (f32[272,512]{1,0:T(8,128)S(1)}, f32[272,512]{1,0:T(8,128)}, u32[]{:S(2)}) copy-start(f32[272,512]{1,0:T(8,128)} %get-tuple-element.109) | copy-start | bytes 1671172
  246.0 12.9 %copy-start.2 = (f32[2,112,1024]{2,1,0:T(8,128)S(1)}, f32[2,112,1024]{2,1,0:T(8,128)}, u32[]{:S(2)}) copy-start(f32[2,112,1024]{2,1,0:T(8,128)} %get-tuple-element.110.own_ref) | copy-start | bytes 2752516
  256.3 3.3 %copy-start = (f32[256,1024]{1,0:T(8,128)}, f32[256,1024]{1,0:T(8,128)S(1)}, u32[]{:S(2)}) copy-start(f32[256,1024]{1,0:T(8,128)S(1)} %maximum_select_fusion.2) | copy-start | bytes 3145732
  256.6 3.1 copy-start.1
  258.3 70.2 %collective-permute-start.11 = (f32[512,1024]{1,0:T(8,128)}, f32[512,1024]{1,0:T(8,128)}, u32[]{:S(2)}, u32[]{:S(2)}) collective-permute-start(f32[512,1024]{1,0:T(8,128)} %pad_maximum_fusion), channel_id=1, source_target_pairs={{0,1},{1,0},{2,3},{3,2},{4,5},{5,4},{6,7},{7,6}} | collective-permute-start | bytes 6291464 | tf_op jit(solution)/shard_map/ppermute | solution.py:866
  258.3 4.7 %collective-permute-start.3 = (f32[136,512]{1,0:T(8,128)S(1)}, f32[136,512]{1,0:T(8,128)S(1)}, u32[]{:S(2)}, u32[]{:S(2)}) collective-permute-start(f32[136,512]{1,0:T(8,128)S(1)} %constant_dynamic-slice_fusion), channel_id=1, source_target_pairs={{0,1},{1,0},{2,3},{3,2},{4,5},{5,4},{6,7},{7,6}} | collective-permute-start | bytes 835592 | tf_op jit(solution)/shard_map/ppermute | solution.py:853
  259.7 13.4 %collective-permute-start.7 = (f32[112,1024]{1,0:T(8,128)S(1)}, f32[112,1024]{1,0:T(8,128)S(1)}, u32[]{:S(2)}, u32[]{:S(2)}) collective-permute-start(f32[112,1024]{1,0:T(8,128)S(1)} %get-tuple-element.136), channel_id=1, source_target_pairs={{0,2},{2,0},{4,6},{6,4},{1,3},{3,1},{5,7},{7,5}} | collective-permute-start | bytes 1376264 | tf_op jit(solution)/shard_map/ppermute | solution.py:844
  261.1 42.9 %collective-permute-start.8 = (f32[112,1024]{1,0:T(8,128)}, f32[112,1024]{1,0:T(8,128)}, u32[]{:S(2)}, u32[]{:S(2)}) collective-permute-start(f32[112,1024]{1,0:T(8,128)} %get-tuple-element.135), channel_id=1, source_target_pairs={{0,4},{2,6},{4,0},{6,2},{1,5},{3,7},{5,1},{7,3}} | collective-permute-start | bytes 1376264 | tf_op jit(solution)/shard_map/ppermute | solution.py:845
  263.1 40.9 %copy-start.3 = (f32[136,512]{1,0:T(8,128)}, f32[136,512]{1,0:T(8,128)S(1)}, u32[]{:S(2)}) copy-start(f32[136,512]{1,0:T(8,128)S(1)} %dynamic-slice_add_fusion.ta_ref) | copy-start | bytes 835588
  263.1 40.9 %collective-permute-start.4 = (f32[136,512]{1,0:T(8,128)S(1)}, f32[136,512]{1,0:T(8,128)}, u32[]{:S(2)}, u32[]{:S(2)}) collective-permute-start(f32[136,512]{1,0:T(8,128)S(1)} %dynamic-slice_add_fusion.ta_ref), channel_id=1, source_target_pairs={{0,2},{2,0},{4,6},{6,4},{1,3},{3,1},{5,7},{7,5}} | collective-permute-start | bytes 835592 | tf_op jit(solution)/shard_map/ppermute | solution.py:856
  264.5 39.5 %collective-permute-start.5 = (f32[136,512]{1,0:T(8,128)S(1)}, f32[136,512]{1,0:T(8,128)}, u32[]{:S(2)}, u32[]{:S(2)}) collective-permute-start(f32[136,512]{1,0:T(8,128)S(1)} %dynamic-slice_add_fusion.ta_ref), channel_id=1, source_target_pairs={{0,4},{2,6},{4,0},{6,2},{1,5},{3,7},{5,1},{7,3}} | collective-permute-start | bytes 835592 | tf_op jit(solution)/shard_map/ppermute | solution.py:856
  273.1 30.9 %copy-start.5 = (f32[112,1024]{1,0:T(8,128)}, f32[112,1024]{1,0:T(8,128)S(1)}, u32[]{:S(2)}) copy-start(f32[112,1024]{1,0:T(8,128)S(1)} %collective-permute-done.7.gx_ref) | copy-start | bytes 1376260
  273.1 31.0 %collective-permute-start.6 = (f32[136,512]{1,0:T(8,128)S(1)}, f32[136,512]{1,0:T(8,128)}, u32[]{:S(2)}, u32[]{:S(2)}) collective-permute-start(f32[136,512]{1,0:T(8,128)S(1)} %dynamic-slice_add_fusion.ta_ref), channel_id=1, source_target_pairs={{0,6},{2,4},{4,2},{6,0},{1,7},{3,5},{5,3},{7,1}} | collective-permute-start | bytes 835592 | tf_op jit(solution)/shard_map/ppermute | solution.py:856

commit v3 on v2

--- a/solution.py
+++ b/solution.py
@@ -63,6 +63,18 @@
     return pl.BlockSpec(shape, lambda i, *_: (0,) * (len(shape) - 1) + (i,))
 
 
+def row_mean(array):
+    return jnp.mean(array, axis=1, keepdims=True)
+
+
+def row_sum(array):
+    return jnp.sum(array, axis=1, keepdims=True)
+
+
+def col_sum(array):
+    return jnp.sum(array, axis=0, keepdims=True)
+
+
 def column(array, lane):
     return array[:, lane:lane + 1]
 
@@ -71,41 +83,44 @@
     return pl.CostEstimate(flops=int(flops), bytes_accessed=int(nbytes), transcendentals=0)
 
 
-def x_prep_kernel(gain_ref, shift_ref, x_ref, xn_ref, mean_ref, rstd_ref, rows_ref):
-    nb = x_ref.shape[1]
-    lanes = x_ref.shape[2]
+def over_channels(term, zero):
+    third = CH // 3
+    parts = lax.fori_loop(
+        0, third, lambda c, acc: tuple(a + term(c + k * third) for k, a in enumerate(acc)), (zero,) * 3, unroll=29)
+    return sum(parts[1:], parts[0]) * (1.0 / CH)
+
+
+def x_prep_kernel(gain_ref, shift_ref, x_ref, xn_ref, mean_ref, rstd_ref, *rows_refs):
+    nb, lanes = x_ref.shape[1:]
     pitch = nb + ROW_GAP
+    width = lanes // len(rows_refs)
     zero = jnp.zeros((nb, lanes), F32)
-
-    def add_up(c, acc):
-        return acc + x_ref[c].astype(F32)
-
-    mean = lax.fori_loop(0, CH, add_up, zero, unroll=9) * (1.0 / CH)
-
-    def add_sq(c, acc):
+    mean = over_channels(lambda c: x_ref[c].astype(F32), zero)
+
+    def square(c):
         d = x_ref[c].astype(F32) - mean
-        return acc + d * d
-
-    var = lax.fori_loop(0, CH, add_sq, zero, unroll=9) * (1.0 / CH)
-    rstd = lax.rsqrt(var + LN_EPS)
+        return d * d
+
+    rstd = lax.rsqrt(over_channels(square, zero) + LN_EPS)
     mean_ref[:] = mean
     rstd_ref[:] = rstd
 
     def put(c, carry):
         xn = (x_ref[c].astype(F32) - mean) * rstd * gain_ref[c] + shift_ref[c]
-        rows_ref[pl.ds(pl.multiple_of(c * pitch, ROW_GAP), nb), :] = xn
+        for k, ref in enumerate(rows_refs):
+            ref[pl.ds(pl.multiple_of(c * pitch, ROW_GAP), nb), :] = xn[:, k * width:(k + 1) * width]
         return carry
 
     lax.fori_loop(0, CH, put, 0, unroll=9)
-    rows_ref[CH * pitch:CPAD * pitch, :] = jnp.zeros(((CPAD - CH) * pitch, lanes), F32)
-    for b in range(nb):
-        xn_ref[b] = rows_ref[pl.ds(b, CPAD, stride=pitch), :].astype(BF16)
+    for k, ref in enumerate(rows_refs):
+        ref[CH * pitch:CPAD * pitch, :] = jnp.zeros(((CPAD - CH) * pitch, width), F32)
+        for b in range(nb):
+            xn_ref[b, :, k * width:(k + 1) * width] = ref[pl.ds(b, CPAD, stride=pitch), :].astype(BF16)
 
 
 def x_prep(x_cm, x_gain, x_shift):
     _, nb, m = x_cm.shape
-    lanes = 128
-    stat = trail((nb, lanes))
+    lanes = 256
     return pl.pallas_call(
         x_prep_kernel,
         grid=(m // lanes,),
@@ -114,13 +129,13 @@
             pl.BlockSpec(memory_space=pltpu.SMEM),
             trail((CH, nb, lanes)),
         ],
-        out_specs=[trail((nb, CPAD, lanes)), stat, stat],
+        out_specs=[trail((nb, CPAD, lanes)), trail((nb, lanes)), trail((nb, lanes))],
         out_shape=[
             jax.ShapeDtypeStruct((nb, CPAD, m), BF16),
             jax.ShapeDtypeStruct((nb, m), F32),
             jax.ShapeDtypeStruct((nb, m), F32),
         ],
-        scratch_shapes=[pltpu.VMEM((CPAD * (nb + ROW_GAP), lanes), F32)],
+        scratch_shapes=[pltpu.VMEM((CPAD * (nb + ROW_GAP), 128), F32)] * 2,
         compiler_params=params(),
         cost_estimate=cost(3e9, 4 * nb * CH * m),
         name="x_prep",
@@ -135,7 +150,7 @@
     for span, s in zip(spans, logits):
         top = jnp.max(s, axis=1, keepdims=True)
         e = jnp.exp2(s - top)
-        total = jnp.sum(e, axis=1, keepdims=True)
+        total = row_sum(e)
         e_low = e.astype(BF16)
         e_ref[0, span, :] = e_low
         ax = jnp.concatenate([mm_nt(e_low, xn), jnp.zeros((e.shape[0], AXW - CPAD), F32)], axis=1)
@@ -208,8 +223,8 @@
 
 
 class Carry:
-    def __init__(self, in_shape, in_hbm, out_shape, scratch, head, tail, out_hbm=False):
-        self.in_shape, self.in_hbm, self.out_shape, self.scratch = in_shape, in_hbm, out_shape, scratch
+    def __init__(self, in_shape, in_hbm, out_shapes, scratch, head, tail, out_hbm=False):
+        self.in_shape, self.in_hbm, self.out_shapes, self.scratch = in_shape, in_hbm, out_shapes, scratch
         self.out_hbm = out_hbm
         self.head, self.tail = head, tail
 
@@ -239,7 +254,7 @@
     half, _, eighth, part = (total // k for k in (2, 4, 8, 16))
     lo, hi = stages[0], stages[-1]
     in_shape = {0: (total, width), 1: (half, width), 2: (2, eighth, width), 3: (2, part, width)}[lo]
-    out_shape = {0: (half, width), 1: (2, eighth, width), 2: (2, part, width), 3: (2, eighth, width), 4: (half, width)}[hi]
+    out_shape = {0: (half, width), 1: (2, eighth, width), 2: (2, part, width), 3: (eighth, width), 4: (half, width)}[hi]
     shapes = {}
     if 0 in stages:
         shapes.update(half=(half, width), rx0=(half, width))
@@ -305,7 +320,8 @@
                 for k in two:
                     dst[k] = take(mid.at[k], p.fine[k], part) + r['rx2'][k]
             elif stage == 3 and hi == 3:
-                out[:] = r['buf'][:]
+                for k in two:
+                    out[k][:] = r['buf'][k]
             elif stage == 4:
                 for k in two:
                     r['full'][pl.ds(pl.multiple_of(p.spot[k], 8), eighth), :] = r['buf'][k]
@@ -313,7 +329,8 @@
 
         return moves, before, after
 
-    def head(step, src, out, refs):
+    def head(step, src, outs, refs):
+        out = outs if hi == 3 else outs[0]
         for stage, when in zip(stages, at):
             def go(stage=stage):
                 moves, before, after = build(src, refs)
@@ -324,23 +341,24 @@
 
             at_step(step, when, go)
 
-    def tail(src, out, refs):
-        build(src, refs)[2](hi, out)
-
-    return Carry(in_shape, lo == 0, out_shape, scratch, head, tail)
-
-
-def carry_rows(shape, start, count, when):
-    def move(src, out, refs):
-        return remote(src.at[pl.ds(start, count)], out, refs, 0, places()[3])
-
-    def head(step, src, out, refs):
-        at_step(step, when, lambda: move(src, out, refs).start())
-
-    def tail(src, out, refs):
-        move(src, out, refs).wait()
-
-    return Carry(shape, True, (count,) + shape[1:], dma_sems(1), head, tail, True)
+    def tail(src, outs, refs):
+        build(src, refs)[2](hi, outs if hi == 3 else outs[0])
+
+    return Carry(in_shape, lo == 0, [out_shape] * (2 if hi == 3 else 1), scratch, head, tail)
+
+
+def carry_rows(shape, half, start, count, when):
+    def move(src, outs, refs):
+        core, _, _, at_core, _, _ = places()
+        return remote(src.at[pl.ds(core * half + start, count)], outs[0], refs, 0, at_core)
+
+    def head(step, src, outs, refs):
+        at_step(step, when, lambda: move(src, outs, refs).start())
+
+    def tail(src, outs, refs):
+        move(src, outs, refs).wait()
+
+    return Carry(shape, True, [(count,) + shape[1:]], dma_sems(1), head, tail, True)
 
 
 def carrier_call(body, ident, carries, travel, grid, in_specs, args, out_specs, out_shape, aliases, cost_estimate):
@@ -350,9 +368,12 @@
     def kernel(*refs):
         ins, c_ins = refs[:n_in], refs[n_in:n_in + n_c]
         rest = refs[n_in + n_c:]
-        outs, c_outs, scratch = rest[:n_out], rest[n_out:n_out + n_c], rest[n_out + n_c:]
-        parts = []
+        outs, scratch = rest[:n_out], rest[n_out + sum(len(c.out_shapes) for c in carries):]
+        rest = rest[n_out:]
+        c_outs, parts = [], []
         for c in carries:
+            c_outs.append(rest[:len(c.out_shapes)])
+            rest = rest[len(c.out_shapes):]
             parts.append(scratch[:len(c.scratch)])
             scratch = scratch[len(c.scratch):]
         step = pl.program_id(0)
@@ -375,8 +396,9 @@
         kernel,
         grid=(grid,),
         in_specs=in_specs + c_in,
-        out_specs=out_specs + [pl.BlockSpec(memory_space=pl.ANY) if c.out_hbm else whole(c.out_shape) for c in carries],
-        out_shape=out_shape + [jax.ShapeDtypeStruct(c.out_shape, F32) for c in carries],
+        out_specs=out_specs + [pl.BlockSpec(memory_space=pl.ANY) if c.out_hbm else whole(shape)
+                               for c in carries for shape in c.out_shapes],
+        out_shape=out_shape + [jax.ShapeDtypeStruct(shape, F32) for c in carries for shape in c.out_shapes],
         scratch_shapes=[shape for c in carries for shape in c.scratch],
         input_output_aliases=aliases,
         compiler_params=pltpu.CompilerParams(
@@ -397,53 +419,57 @@
 
 
 def mlp_a_kernel(axa_ref, axb_ref, z0_ref, wvo_ref, mg_ref, ms_ref, w1_ref, b1_ref, w2_ref, b2_ref, do_ref,
-                 z1_ref, h_ref, slope_ref, z2_ref, full_ref, dw2_ref, act_ref):
-    ax, _, _ = combine(axa_ref[0], axb_ref[0])
-    z1 = z0_ref[:] + mm(ax[:, :CPAD].astype(BF16), wvo_ref[:])
-    z1_ref[0] = z1
-    h = layer_norm(z1, mg_ref[:], ms_ref[:]).astype(BF16)
-    h_ref[0] = h
-    d_out = do_ref[0]
+                 z1_ref, h_ref, slope_ref, full_ref, dw2_ref, act_ref):
+    count, n, width = z1_ref.shape
+    step = 512
+    flat = lambda ref, cols: ref[:, :, cols].reshape(count * n, step)
 
     @pl.when(pl.program_id(0) == 0)
     def _():
         dw2_ref[:] = jnp.zeros_like(dw2_ref)
 
-    n = h.shape[0] // 2
-    for rows_of in (slice(0, n), slice(n, 2 * n)):
-        pre = mm(h[rows_of], w1_ref[:]) + b1_ref[:]
+    for b in range(count):
+        ax, _, _ = combine(axa_ref[b], axb_ref[b])
+        z1 = z0_ref[:] + mm(ax[:, :CPAD].astype(BF16), wvo_ref[:])
+        z1_ref[b] = z1
+        h_ref[b] = layer_norm(z1, mg_ref[:], ms_ref[:]).astype(BF16)
+    h = h_ref[:].reshape(count * n, width)
+    spans = [slice(lo, lo + step) for lo in range(0, width, step)]
+    for cols in spans:
+        pre = mm(h, w1_ref[:, cols]) + b1_ref[:, cols]
         sq = pre * pre
         t = jnp.tanh(pre * (GELU_A + (GELU_A * GELU_B) * sq))
         half_t = 0.5 + 0.5 * t
-        act = (pre * half_t).astype(BF16)
-        slope_ref[0, rows_of] = half_t + (0.5 * pre) * (1.0 - t * t) * (GELU_A + (3.0 * GELU_A * GELU_B) * sq)
-        act_ref[rows_of] = act
-        z2 = z1_ref[0, rows_of] + mm(act, w2_ref[:]) + b2_ref[:]
-        z2_ref[0, rows_of] = z2
-        full_ref[0, rows_of] = z2
-    dw2_ref[:] += mm(act_ref[:].T, d_out)
+        act_ref[:, cols] = (pre * half_t).astype(BF16)
+        slope = half_t + (0.5 * pre) * (1.0 - t * t) * (GELU_A + (3.0 * GELU_A * GELU_B) * sq)
+        slope_ref[:, :, cols] = slope.reshape(count, n, step)
+    act = act_ref[:]
+    for cols in spans:
+        z2 = flat(z1_ref, cols) + mm(act, w2_ref[:, cols]) + b2_ref[:, cols]
+        full_ref[:, :, cols] = z2.reshape(count, n, step)
+    dw2_ref[:] += mm(act.T, do_ref[:].reshape(count * n, width))
 
 
 def mlp_a(axa, axb, z0, wvo, mg, ms, w1, b1, w2, b2, d_out):
     half, n, _ = axa.shape
     d = z0.shape[1]
-    per = lambda c: lead((1, n, c))
-    shifted = lead((1, n, d), lambda i: lax.axis_index('cp') * half + i)
+    count = 2
+    per = lambda c: lead((count, n, c))
+    shifted = lead((count, n, d), lambda i: lax.axis_index('cp') * (half // count) + i)
     return pl.pallas_call(
         mlp_a_kernel,
-        grid=(half,),
+        grid=(half // count,),
         in_specs=[per(AXW), per(AXW), once((n, d)), once((CPAD, d)), whole((1, d)), whole((1, d)),
                   once((d, d)), whole((1, d)), once((d, d)), whole((1, d)), shifted],
-        out_specs=[per(d), per(d), per(d), per(d), shifted, whole((d, d))],
+        out_specs=[per(d), per(d), per(d), shifted, once((d, d))],
         out_shape=[
             jax.ShapeDtypeStruct((half, n, d), F32),
             jax.ShapeDtypeStruct((half, n, d), BF16),
             jax.ShapeDtypeStruct((half, n, d), F32),
-            jax.ShapeDtypeStruct((half, n, d), F32),
             jax.ShapeDtypeStruct(d_out.shape, F32),
             jax.ShapeDtypeStruct((d, d), F32),
         ],
-        scratch_shapes=[pltpu.VMEM((n, d), BF16)],
+        scratch_shapes=[pltpu.VMEM((count * n, d), BF16)],
         compiler_params=params(),
         cost_estimate=cost(2 * half * n * d * (3 * d + 512), half * n * d * 18),
         name="mlp_a",
@@ -458,7 +484,7 @@
 
     d_act = mm_nt(do_ref[0], w2_ref[:]).astype(BF16).astype(F32)
     d_pre = d_act * slope_ref[0]
-    db1_ref[:] += jnp.sum(d_pre, axis=0, keepdims=True)
+    db1_ref[:] += col_sum(d_pre)
     d_pre_low = d_pre.astype(BF16)
     dpre_ref[0] = d_pre_low
     dw1_ref[:] += mm(h_ref[0].T, d_pre_low)
@@ -481,12 +507,12 @@
     n, _ = z1_ref.shape[1:]
     z1 = z1_ref[0]
     d_hid = mm_nt(dpre_ref[0], w1_ref[:]).astype(BF16).astype(F32)
-    centred = z1 - jnp.mean(z1, axis=1, keepdims=True)
-    rstd = lax.rsqrt(jnp.mean(centred * centred, axis=1, keepdims=True) + LN_EPS)
+    centred = z1 - row_mean(z1)
+    rstd = lax.rsqrt(row_mean(centred * centred) + LN_EPS)
     hat = centred * rstd
     d_hat = d_hid * mg_ref[:]
-    mean_a = jnp.mean(d_hat, axis=1, keepdims=True)
-    mean_b = jnp.mean(d_hat * hat, axis=1, keepdims=True)
+    mean_a = row_mean(d_hat)
+    mean_b = row_mean(d_hat * hat)
     d_out = do_ref[0].astype(F32)
     d_mid = d_out + rstd * (d_hat - mean_a - hat * mean_b)
     d_mid_low = d_mid.astype(BF16)
@@ -499,11 +525,11 @@
     p = mm(ax[:, :CPAD].astype(BF16).T, d_mid_low)
     acc_ref[0:n, :] += d_mid
     acc_ref[n:n + CPAD, :] += p
-    acc_ref[VEC_ROW:VEC_ROW + 1, :] += jnp.sum(d_hid * hat, axis=0, keepdims=True)
-    acc_ref[VEC_ROW + 1:VEC_ROW + 2, :] += jnp.sum(d_hid, axis=0, keepdims=True)
-    acc_ref[VEC_ROW + 2:VEC_ROW + 3, :] += jnp.sum(d_out, axis=0, keepdims=True)
+    acc_ref[VEC_ROW:VEC_ROW + 1, :] += col_sum(d_hid * hat)
+    acc_ref[VEC_ROW + 1:VEC_ROW + 2, :] += col_sum(d_hid)
+    acc_ref[VEC_ROW + 2:VEC_ROW + 3, :] += col_sum(d_out)
     d_ax = jnp.concatenate([mm_nt(d_mid_low, wvo_ref[:]), jnp.zeros((n, AXW - CPAD), F32)], axis=1)
-    delta = jnp.sum(d_ax * ax, axis=1, keepdims=True)
+    delta = row_sum(d_ax * ax)
     lane = lax.broadcasted_iota(jnp.int32, d_ax.shape, 1)
     g_ref[0] = jnp.where(lane == SUM_LANE, delta, jnp.where(lane == MAX_LANE, top, jnp.where(lane == INV_LANE, inv, d_ax)))
 
@@ -535,7 +561,7 @@
 
     @pl.when(pl.program_id(0) == 0)
     def _():
-        t_ref[:] = t_in_ref[:]
+        t_ref[:] = jnp.zeros_like(t_ref) if t_in_ref is None else t_in_ref[:]
 
     t_ref[:] += mm_nt(xn, d_s)
     dxn_ref[0] = (mm(qpt_ref[:], d_s) + mm(d_low.T, e)).astype(BF16)
@@ -550,16 +576,16 @@
         return (core if own else 1 - core) * half + i
 
     shifted = lead((1, CPAD, m), at)
-    in_specs = [per(AXW), per(AXW), per(m), shifted, whole((CPAD, n)), whole((CPAD, n))]
-    args = [g, ax, e, xn, qpt, t_in]
+    in_specs = [per(AXW), per(AXW), per(m), shifted, whole((CPAD, n))]
+    args = [g, ax, e, xn, qpt]
     aliases = {}
-    if dxn_in is not None:
-        in_specs.append(pl.BlockSpec(memory_space=pl.ANY))
-        args.append(dxn_in)
+    if not own:
+        in_specs += [whole((CPAD, n)), pl.BlockSpec(memory_space=pl.ANY)]
+        args += [t_in, dxn_in]
         aliases = {6: 0}
 
     def body(*refs):
-        attn_bwd_body(*refs[:6], *refs[-2:])
+        attn_bwd_body(*refs[:5], None if own else refs[5], *refs[-2:])
 
     return carrier_call(
         body, ident, carries, travel, half, in_specs, args,
@@ -606,20 +632,19 @@
         da, db = acc
         hat = (x_ref[c].astype(F32) - mean) * rstd
         dxn = rows_ref[pl.ds(c, nb, stride=pitch), :]
-        dh = dxn * gain_ref[c]
         prod = dxn * hat
         dg_ref[c] += prod[:8] + prod[8:]
         ds_ref[c] += dxn[:8] + dxn[8:]
-        return da + dh, db + dh * hat
+        return da + dxn * gain_ref[c], db + prod * gain_ref[c]
 
     da, db = lax.fori_loop(0, CH, gather, (zero, zero), unroll=9)
-    mean_a = da * (1.0 / CH)
-    mean_b = db * (1.0 / CH)
+    mean_a = da * (1.0 / CH) * rstd
+    mean_b = db * (1.0 / CH) * rstd * rstd
 
     def put(c, carry):
-        hat = (x_ref[c].astype(F32) - mean) * rstd
+        centred = x_ref[c].astype(F32) - mean
         dxn = rows_ref[pl.ds(c, nb, stride=pitch), :]
-        dx_ref[c] = (rstd * (dxn * gain_ref[c] - mean_a - hat * mean_b)).astype(BF16)
+        dx_ref[c] = (dxn * (gain_ref[c] * rstd) - mean_a - centred * mean_b).astype(BF16)
         return carry
 
     lax.fori_loop(0, CH, put, 0, unroll=9)
@@ -676,50 +701,52 @@
     )(core, x_gain, x_cm, mean, rstd, dxn, za, zb, w_own, w_got, full)
 
 
-def finish_kernel(devices, x_ref, ta_ref, tb_ref, tc_ref, td_ref, own_ref, gx_ref, gy_ref, o_ref, t_ref, acc_ref,
-                  got_ref, t_all, acc_all, send_sem, recv_sem):
-    dp, cp = devices
-    my_dp, my_cp = lax.axis_index('dp'), lax.axis_index('cp')
+def finish_kernel(dp, cp, x_ref, t_refs, acc_refs, w_refs, o_ref, outs, got_ref, wholes, send_sem, recv_sem):
     core, x, y, at_core, _, _ = places()
-    peers = [(i, j) for i in range(dp) for j in range(cp)][1:]
-    ids = [(lax.rem(my_dp + i, dp), lax.rem(my_cp + j, cp)) for i, j in peers]
+    my_dp = lax.axis_index('dp')
+    ids = [(lax.rem(my_dp + i, dp), lax.rem(core + j, cp)) for i in range(dp) for j in range(cp)][1:]
     meet(ids)
-    copies = [remote(x_ref, got_ref.at[k], (send_sem, recv_sem), k, dev) for k, dev in enumerate(ids)]
+    sems = (send_sem, recv_sem)
+    copies = [remote(x_ref, got_ref.at[k], sems, k, dev) for k, dev in enumerate(ids)]
     start_all(copies)
-    th, ah = ta_ref.shape[0], 4 * own_ref.shape[1]
-    eighth = own_ref.shape[1]
-    base = core * ah
-    t_all[pl.ds(pl.multiple_of(core * th, 8), th), :] = (ta_ref[:] + tb_ref[:]) + (tc_ref[:] + td_ref[:])
-    t_copy = remote(rows(t_all, core * th, th), rows(t_all, core * th, th), (send_sem, recv_sem), len(ids), at_core)
-    for start, ref in ((x * eighth, own_ref.at[0]), ((1 - x) * eighth, gx_ref),
-                       ((2 + y) * eighth, own_ref.at[1]), ((3 - y) * eighth, gy_ref)):
-        acc_all[pl.ds(pl.multiple_of(base + start, 8), eighth), :] = ref[:]
-    t_copy.start()
-    acc_copy = remote(rows(acc_all, base, ah), rows(acc_all, base, ah), (send_sem, recv_sem), len(ids) + 1, at_core)
-    acc_copy.start()
+    swaps = []
+    for k, (buf, parts) in enumerate(zip(wholes, (t_refs, acc_refs, w_refs))):
+        half = buf.shape[0] // 2
+        if parts is t_refs:
+            a, b, c, d = (ref[:] for ref in parts)
+            buf[pl.ds(pl.multiple_of(core * half, 8), half), :] = (a + b) + (c + d)
+        else:
+            eighth = half // 4
+            for place, ref in zip((x, 2 + y, 1 - x, 3 - y), parts):
+                buf[pl.ds(pl.multiple_of(core * half + place * eighth, 8), eighth), :] = ref[:]
+        mine = rows(buf, core * half, half)
+        swaps.append(remote(mine, mine, sems, len(ids) + k, at_core))
+        swaps[k].start()
     wait_all(copies)
     o_ref[:] = x_ref[:] + jnp.sum(got_ref[:], axis=0)
-    t_copy.wait()
-    t_ref[:] = t_all[:]
-    acc_copy.wait()
-    acc_ref[:] = acc_all[:]
-
-
-def finish(mesh, x, t_parts, own, got_x, got_y):
+    for swap, out, buf in zip(swaps, outs, wholes):
+        swap.wait()
+        out[:] = buf[:]
+
+
+def finish(mesh, x, t_parts, acc_parts, w_parts):
     count = mesh.size - 1
-    t_shape = (2 * t_parts[0].shape[0], t_parts[0].shape[1])
-    acc_shape = (8 * own.shape[1], own.shape[2])
+    shapes = [(k * part[0].shape[0], part[0].shape[1]) for k, part in ((2, t_parts), (8, acc_parts), (8, w_parts))]
     vmem = pl.BlockSpec(memory_space=pltpu.VMEM)
+
+    def kernel(x_ref, *refs):
+        finish_kernel(mesh.shape['dp'], mesh.shape['cp'], x_ref, refs[:4], refs[4:8], refs[8:12], refs[12], refs[13:16],
+                      refs[16], refs[17:20], *refs[20:])
+
     return pl.pallas_call(
-        functools.partial(finish_kernel, (mesh.shape['dp'], mesh.shape['cp'])),
-        in_specs=[vmem] * 8,
-        out_specs=[vmem] * 3,
-        out_shape=[jax.ShapeDtypeStruct(shape, F32) for shape in (x.shape, t_shape, acc_shape)],
-        scratch_shapes=[pltpu.VMEM((count,) + x.shape, F32), pltpu.VMEM(t_shape, F32), pltpu.VMEM(acc_shape, F32)]
-        + dma_sems(count + 2),
+        kernel,
+        in_specs=[vmem] * 13,
+        out_specs=[vmem] * 4,
+        out_shape=[jax.ShapeDtypeStruct(shape, F32) for shape in (x.shape, *shapes)],
+        scratch_shapes=[pltpu.VMEM(shape, F32) for shape in ((count,) + x.shape, *shapes)] + dma_sems(count + 3),
         compiler_params=pltpu.CompilerParams(vmem_limit_bytes=VMEM_LIMIT, collective_id=0, has_side_effects=True),
         name="finish",
-    )(x, *t_parts, own, got_x, got_y)
+    )(x, *t_parts, *acc_parts, *w_parts)
 
 
 def prologue_kernel(scale, z0_ref, zg_ref, zs_ref, wq_ref, wk_in_ref, wv_in_ref, wo_ref,
@@ -764,14 +791,14 @@
     dwq_ref[:] = mm(zn_ref[:].T, d_q)
     d_zn = mm_nt(d_q, wq_ref[:])
     z0 = z0_ref[:]
-    centred = z0 - jnp.mean(z0, axis=1, keepdims=True)
-    rstd = lax.rsqrt(jnp.mean(centred * centred, axis=1, keepdims=True) + LN_EPS)
+    centred = z0 - row_mean(z0)
+    rstd = lax.rsqrt(row_mean(centred * centred) + LN_EPS)
     hat = centred * rstd
-    dzg_ref[:] = jnp.sum(d_zn * hat, axis=0, keepdims=True)
-    dzs_ref[:] = jnp.sum(d_zn, axis=0, keepdims=True)
+    dzg_ref[:] = col_sum(d_zn * hat)
+    dzs_ref[:] = col_sum(d_zn)
     d_hat = d_zn * zg_ref[:]
-    mean_a = jnp.mean(d_hat, axis=1, keepdims=True)
-    mean_b = jnp.mean(d_hat * hat, axis=1, keepdims=True)
+    mean_a = row_mean(d_hat)
+    mean_b = row_mean(d_hat * hat)
     dlat_ref[:] = acc_ref[:n, :] + rstd * (d_hat - mean_a - hat * mean_b)
 
 
@@ -801,7 +828,7 @@
 
     def step(inputs, latents, x_gain, x_shift, z_gain, z_shift, w_query, w_key, w_value, w_out, m_gain, m_shift, w_up, b_up, w_down, b_down, d_out):
         qk_scale = w_query.shape[1] ** -0.5
-        n, d = latents.shape
+        _, d = latents.shape
         half = inputs.shape[0] // 2
         core = lax.axis_index('cp')
         as_ints = lambda *vals: jnp.stack([v.astype(jnp.int32) for v in vals])
@@ -820,24 +847,24 @@
         e_mine, ax_mine = attn_fwd(mine, qp, xn, half)
 
         flip = lambda bit: [(k, k ^ bit) for k in range(4)]
-        z1, hid, slope, z2, full, dw2 = mlp_a(
+        z1, hid, slope, full, dw2 = mlp_a(
             ax_mine, ax_got, latents, wvo, row(m_gain), row(m_shift), w_up, row(b_up), w_down, row(b_down), d_out)
         dpre, dw1, db1, w2_pieces = mlp_w(
             hid, slope, d_out, w_down, [carry(d, d, (0, 1, 2), (0, 2, 6))], [dw2])
         g_mine, acc, w2_half, w1_eighths, za_got = mlp_b(
             ax_mine, ax_got, z1, dpre, d_out, wvo, row(m_gain), w_up, db1,
-            [carry(d, d, (3, 4), (0, 2)), carry(d, d, (0, 1), (0, 2)), carry_rows(z2.shape, 0, half // 2, 2)],
-            [w2_pieces, dw1, z2])
+            [carry(d, d, (3, 4), (0, 2)), carry(d, d, (0, 1), (0, 2)), carry_rows(full.shape, half, 0, half // 2, 2)],
+            [w2_pieces, dw1, full])
         g_got = lax.ppermute(g_mine, 'cp', swap)
-        dxn, t_part, w1_eighths, acc_half = attn_bwd(
-            True, g_mine, ax_mine, e_mine, xn, qpt, jnp.zeros((CPAD, n), F32), None, 3,
+        dxn, t_part, *w1_eighths, acc_half = attn_bwd(
+            True, g_mine, ax_mine, e_mine, xn, qpt, None, None, 3,
             [carry(d, d, (2, 3), (0, 3)), carry(ACC_ROWS, d, (0,), (0,))], [w1_eighths, acc])
         w2_half, dxn = lax.optimization_barrier((w2_half, dxn))
         w2_got = lax.ppermute(w2_half, 'cp', swap)
-        dxn, t_part, acc_eighths, zb_got = attn_bwd(
+        dxn, t_part, *acc_eighths, zb_got = attn_bwd(
             False, g_got, ax_other, e_other, xn, qpt, t_part, dxn, 4,
-            [carry(ACC_ROWS, d, (1, 2, 3), (0, 5, 7)), carry_rows(z2.shape, half // 2, half // 2, 0)],
-            [acc_half, z2])
+            [carry(ACC_ROWS, d, (1, 2, 3), (0, 5, 7)), carry_rows(full.shape, half, half // 2, half // 2, 0)],
+            [acc_half, full])
         w1_eighths, dxn = lax.optimization_barrier((w1_eighths, dxn))
 
         def halves(own):
@@ -856,15 +883,9 @@
             t_parts.append(lax.ppermute(t_mine, 'dp', [(k, k ^ bit) for k in range(4)]))
         dx_cm, sums, z_out, d_w_down = x_post(
             core.astype(jnp.int32).reshape(1), x_gain, x_cm, x_mean, x_rstd, dxn, za_got, zb_got, full, w2_half, w2_got)
-        sums, t_sum, acc = finish(mesh, sums, t_parts, acc_eighths, acc_x, acc_y)
+        sums, t_sum, acc, d_w_up = finish(
+            mesh, sums, t_parts, [*acc_eighths, acc_x, acc_y], [*w1_eighths, w1_x, w1_y])
         d_x_gain, d_x_shift = sums[0, :CH], sums[1, :CH]
-        order = lambda bit, own, got: jnp.where(
-            bit == 0, jnp.concatenate([own, got], 0), jnp.concatenate([got, own], 0))
-        chip = lax.axis_index('dp')
-        w1_half = jnp.concatenate([
-            order(lax.rem(chip, 2), w1_eighths[0], w1_x), order(chip // 2, w1_eighths[1], w1_y)], 0)
-        w1_got = lax.ppermute(w1_half, 'cp', swap)
-        d_w_up = order(core, w1_half, w1_got)
 
         d_m_gain, d_m_shift, d_b_down, d_b_up = (acc[VEC_ROW + k] for k in range(4))
         d_lat, d_z_gain, d_z_shift, d_w_query, d_w_key, d_w_value, d_w_out = final(

time: 335 us -> 315 us (0.940)
  waiting for transfers between devices: 19.7 us -> 8 us
  other arithmetic: 8.49 us -> 2.16 us
  Pallas kernels: 290 us -> 286 us
  local copies, waits for them, and re-layouts: 5.92 us -> 9.66 us
    ppermute x2, waiting for transfers between devices: 10.2 us -> 0.01 us  [halves(): got_y = lax.ppermute(own[1], 'dp', flip(2))]
    unnamed x12 -> x9, local copies, waits for them, and re-layouts: 0.03 us -> 5.8 us
    select_n x3 -> x0, other arithmetic: 5.6 us -> none  [step(): jnp.where(bit == 0, jnp.concatenate([own, got], 0), jnp.concatenate([got,...]
  transfers between devices with their start and end apart: 12 -> 11, of which waited for: 4 -> 1; matrix products, arithmetic and copies ran while one was open for 3% -> 1% of each run, Pallas kernels for 36% -> 31%
where the time goes in v3:
time: 315 us; the launch traced here: 314 us
  Pallas kernels  286 us (91%)
  local copies, waits for them, and re-layouts  9.66 us (3%)
  waiting for transfers between devices  8 us (3%)
  starting transfers between devices  7.53 us (2%)
    pallas_call x4, Pallas kernels, carrier_call(): pl.pallas_call(kernel, grid=(grid,), in_specs=in_specs + c_in, out_specs=...  132 us
    pallas_call x1, Pallas kernels, mlp_a(): pl.pallas_call(mlp_a_kernel, grid=(half // count,), in_specs=[per(AXW), p...  50.9 us
    pallas_call x1, Pallas kernels, x_post(): pl.pallas_call(x_post_kernel, grid_spec=pltpu.PrefetchScalarGridSpec(num_...  29.1 us
    pallas_call x2, Pallas kernels, attn_fwd(): pl.pallas_call(attn_fwd_kernel, grid_spec=pltpu.PrefetchScalarGridSpec(nu...  26.7 us
    pallas_call x1, Pallas kernels, finish(): pl.pallas_call(kernel, in_specs=[vmem] * 13, out_specs=[vmem] * 4, out_sh...  14.2 us
    pallas_call x1, Pallas kernels, x_prep(): pl.pallas_call(x_prep_kernel, grid=(m // lanes,), in_specs=[pl.BlockSpec(...  14 us
    pallas_call x1, Pallas kernels, final(): pl.pallas_call(functools.partial(final_kernel, scale), in_specs=[vmem] *...  12.1 us
    ppermute x2, waiting for transfers between devices, halves(): got_x = lax.ppermute(own[0], 'dp', flip(1))  7.98 us
  transfers between devices with their start and end apart: 11, of which 1 were waited for; matrix products, arithmetic and copies ran while one was open for 1% of the time, Pallas kernels for 31%

profile of v3, /device:TPU:0, one launch (start us, length us, event | category | flops | bytes accessed | tf_op | source)
XLA Modules:
  0.0 314.2 jit_solution(6633038775751223777)
XLA Ops:
  0.7 0.6 pad_add_fusion.1.base_ref
  1.2 14.0 %x_prep.1 = (bf16[16,272,1024]{2,1,0:T(8,128)(2,1)}, f32[16,1024]{1,0:T(8,128)}, f32[16,1024]{1,0:T(8,128)}) custom-call(f32[261]{0:T(512)} %gain_ref.3, f32[261]{0:T(512)} %shift_ref.1, bf16[261,16,1024]{2,1,0:T(8,128)(2,1)} %bitcast.19), custom_call_target="tpu_custom_call" | custom-call | flops 3000000000 | bytes 17104896 | tf_op jit(solution)/shard_map/x_prep/pallas_call | solution.py:124
  15.2 7.1 %prologue.1 = (bf16[512,1024]{1,0:T(8,128)(2,1)}, bf16[512,1024]{1,0:T(8,128)(2,1)}, bf16[512,272]{1,0:T(8,128)(2,1)}, bf16[272,512]{1,0:T(8,128)(2,1)}, bf16[27...) custom-call(f32[512,1024]{1,0:T(8,128)} %z0_ref.5, f32[1,1024]{1,0:T(1,128)} %bitcast.32, ...), custom_call_target="tpu_custom_call" | custom-call | flops 3000000000 | bytes 12000000 | tf_op jit(solution)/shard_map/prologue/pallas_call | solution.py:770
  22.3 13.3 %attn_fwd.3 = (bf16[8,512,1024]{2,1,0:T(8,128)(2,1)}, f32[8,512,384]{2,1,0:T(8,128)}) custom-call(s32[2]{0:T(128)} %pad_add_fusion.1.base_ref, bf16[512,272]{1,0:T(8,128)(2,1)} %get-tuple-element.77.qp_ref, bf16[16,272,1024]{2,1,0:T(8,128)(2,1)} %get-tuple-element.78.xn_ref.refs_3_), custom_call_target="tpu_custom_call" | custom-call | flops 8589934592 | bytes 12582912 | tf_op jit(solution)/shard_map/attn_fwd/pallas_call | solution.py:164
  35.6 0.8 collective-permute-start
  36.5 0.6 pad_add_fusion.base_ref
  37.1 13.4 %attn_fwd.2 = (bf16[8,512,1024]{2,1,0:T(8,128)(2,1)}, f32[8,512,384]{2,1,0:T(8,128)}) custom-call(s32[2]{0:T(128)} %pad_add_fusion.base_ref, bf16[512,272]{1,0:T(8,128)(2,1)} %get-tuple-element.77.qp_ref, bf16[16,272,1024]{2,1,0:T(8,128)(2,1)} %get-tuple-element.78.xn_ref.refs_3_), custom_call_target="tpu_custom_call" | custom-call | flops 8589934592 | bytes 12582912 | tf_op jit(solution)/shard_map/attn_fwd/pallas_call | solution.py:164
  50.5 0.0 collective-permute-done.axb_ref.refs_1_
  50.5 50.9 %mlp_a.1 = (f32[8,512,1024]{2,1,0:T(8,128)}, bf16[8,512,1024]{2,1,0:T(8,128)(2,1)}, f32[8,512,1024]{2,1,0:T(8,128)}, f32[16,512,1024]{2,1,0:T(8,128)}, f32[1024,1024]{1,0:T(8,128)}) custom-call(f32[8,512,384]{2,1,0:T(8,128)} %get-tuple-element.79.axa_ref.refs_0_.refs_1_, f32[8,512,384]{2,1,0:T(8,128)} %collective-permute-done.axb_ref.refs_1_, ...), custom_call_target="tpu_custom_call" | custom-call | flops 30064771072 | bytes 75497472 | tf_op jit(solution)/shard_map/mlp_a/pallas_call | solution.py:459
  101.4 34.7 %shard_map.296 = (bf16[8,512,1024]{2,1,0:T(8,128)(2,1)}, f32[1024,1024]{1,0:T(8,128)}, f32[1,1024]{1,0:T(1,128)}, f32[2,64,1024]{2,1,0:T(8,128)}) custom-call(bf16[8,512,1024]{2,1,0:T(8,128)(2,1)} %get-tuple-element.83.refs_0_, f32[8,512,1024]{2,1,0:T(8,128)} %get-tuple-element.84.refs_1_, bf16[16,512,1024]{2,1,0:T(8,128)(2,1)} %refs_4_.1, ...), custom_call_target="tpu_custom_call" | custom-call | flops 17179869184 | bytes 41943040 | tf_op jit(solution)/shard_map/pallas_call | solution.py:395
  136.1 43.0 %shard_map.297 = (f32[8,512,384]{2,1,0:T(8,128)}, f32[896,1024]{1,0:T(8,128)}, f32[512,1024]{1,0:T(8,128)}, f32[2,128,1024]{2,1,0:T(8,128)}, f32[4,512,1024]{2,1,0:T(8,128)}) custom-call(f32[8,512,384]{2,1,0:T(8,128)} %get-tuple-element.79.axa_ref.refs_0_.refs_1_, f32[8,512,384]{2,1,0:T(8,128)} %collective-permute-done.axb_ref.refs_1_, ...), custom_call_target="tpu_custom_call" | custom-call | flops 15300820992 | bytes 41943040 | tf_op jit(solution)/shard_map/pallas_call | solution.py:395
  179.1 0.0 collective-permute-start.1
  179.2 24.2 %shard_map.298 = (bf16[16,272,1024]{2,1,0:T(8,128)(2,1)}, f32[272,512]{1,0:T(8,128)}, f32[128,1024]{1,0:T(8,128)}, f32[128,1024]{1,0:T(8,128)}, f32[448,1024]{1,0:T(8,128)}) custom-call(f32[8,512,384]{2,1,0:T(8,128)} %get-tuple-element.91.refs_0_, f32[8,512,384]{2,1,0:T(8,128)} %get-tuple-element.79.axa_ref.refs_0_.refs_1_, ...), custom_call_target="tpu_custom_call" | custom-call | flops 17179869184 | bytes 25165824 | tf_op jit(solution)/shard_map/pallas_call | solution.py:395
  203.4 0.0 collective-permute-start.2
  203.5 0.0 collective-permute-done.1.refs_0_
  203.5 0.0 copy-start.1
  203.5 30.0 %shard_map.299 = (bf16[16,272,1024]{2,1,0:T(8,128)(2,1)}, f32[272,512]{1,0:T(8,128)}, f32[112,1024]{1,0:T(8,128)}, f32[112,1024]{1,0:T(8,128)}, f32[4,512,1024]{2,1,0:T(8,128)}) custom-call(f32[8,512,384]{2,1,0:T(8,128)} %collective-permute-done.1.refs_0_, f32[8,512,384]{2,1,0:T(8,128)} %get-tuple-element.80.refs_1_, ...), custom_call_target="tpu_custom_call", output_to_operand_aliasing={{0}: (6, {})} | custom-call | flops 17179869184 | bytes 25165824 | tf_op jit(solution)/shard_map/pallas_call | solution.py:395
  233.5 1.0 constant_dynamic-slice_fusion
  234.5 0.0 collective-permute-start.3
  234.5 0.5 collective-permute-start.7
  235.0 1.5 collective-permute-start.8
  236.5 0.0 copy-done.1
  236.5 0.5 collective-permute-start.9
  237.1 0.0 collective-permute-done.3
  237.1 1.5 collective-permute-start.10
  238.6 1.0 dynamic-slice_add_fusion.refs_0_
  239.6 0.0 copy-start
  239.6 0.0 collective-permute-done.2.wb_ref
  239.6 0.5 collective-permute-start.4
  240.1 8.0 %collective-permute-done.7.refs_6_ = f32[112,1024]{1,0:T(8,128)S(1)} collective-permute-done((f32[112,1024]{1,0:T(8,128)}, f32[112,1024]{1,0:T(8,128)S(1)}, u32[]{:S(2)}, u32[]{:S(2)}) %collective-permute-start.7) | collective-permute-done | bytes 458784 | tf_op jit(solution)/shard_map/ppermute | solution.py:871
  248.1 0.0 copy-start.2
  248.1 0.5 collective-permute-start.5
  248.6 0.2 copy-done.2
  248.9 0.0 collective-permute-done.8.refs_7_
  248.9 0.0 copy-start.3
  248.9 0.8 copy-done.3
  249.7 1.5 collective-permute-start.6
  251.1 29.1 %x_post.1 = (bf16[261,16,1024]{2,1,0:T(8,128)(2,1)}, f32[2,384]{1,0:T(2,128)}, f32[16,512,1024]{2,1,0:T(8,128)}, f32[1024,1024]{1,0:T(8,128)}) custom-call(s32[1]{0:T(128)} %bitcast.base_ref, f32[261]{0:T(512)} %gain_ref.3, bf16[261,16,1024]{2,1,0:T(8,128)(2,1)} %bitcast.20, ...), custom_call_target="tpu_custom_call", output_to_operand_aliasing={{2}: (10, {})} | custom-call | flops 6000000000 | bytes 59211776 | tf_op jit(solution)/shard_map/x_post/pallas_call | solution.py:672
  280.2 0.0 copy-done
  280.2 0.0 collective-permute-done.9.refs_10_
  280.2 0.0 collective-permute-done.10.refs_11_
  280.2 0.0 collective-permute-done.4.refs_1_
  280.2 0.0 collective-permute-done.5.refs_2_
  280.3 0.0 collective-permute-done.6.refs_3_
  280.3 14.2 %finish.1 = (f32[2,384]{1,0:T(2,128)}, f32[272,512]{1,0:T(8,128)}, f32[896,1024]{1,0:T(8,128)}, f32[1024,1024]{1,0:T(8,128)}) custom-call(f32[2,384]{1,0:T(2,128)} %get-tuple-element.111.x_ref, f32[136,512]{1,0:T(8,128)} %copy-done, f32[136,512]{1,0:T(8,128)} %collective-permute-done.4.refs_1_, f32[136,512]{1,0:T(8,128)} %collective-permute-done.5.refs_2_, ...), custom_call_target="tpu_custom_call" | custom-call | tf_op jit(solution)/shard_map/finish/pallas_call | solution.py:741
  294.4 1.3 slice_reduce_fusion
  295.8 1.5 fusion
  297.3 12.1 %final.1 = (f32[512,1024]{1,0:T(8,128)}, f32[1,1024]{1,0:T(1,128)}, f32[1,1024]{1,0:T(1,128)}, f32[1024,1024]{1,0:T(8,128)}, f32[261,1024]{1,0:T(8,128)}, /*index=5*/f32[261,1024]{1,0:T(8,128)}, f32[1024,1024]{1,0:T(8,128)}) custom-call(f32[272,512]{1,0:T(8,128)} %get-tuple-element.117.t_ref, f32[896,1024]{1,0:T(8,128)} %get-tuple-element.118.acc_ref, ...), custom_call_target="tpu_custom_call" | custom-call | flops 4000000000 | bytes 25000000 | tf_op jit(solution)/shard_map/final/pallas_call | solution.py:809
  309.4 4.8 %copy.39 = f32[1024,1024]{1,0:T(8,128)} copy(f32[1024,1024]{1,0:T(8,128)} %get-tuple-element.169) | data formatting | bytes 8388608
Async XLA Ops:
  35.6 14.8 %collective-permute-start = (f32[8,512,384]{2,1,0:T(8,128)}, f32[8,512,384]{2,1,0:T(8,128)}, u32[]{:S(2)}, u32[]{:S(2)}) collective-permute-start(f32[8,512,384]{2,1,0:T(8,128)} %get-tuple-element.80.refs_1_), channel_id=1, source_target_pairs={{0,1},{1,0},{2,3},{3,2},{4,5},{5,4},{6,7},{7,6}} | collective-permute-start | bytes 18874376 | tf_op jit(solution)/shard_map/ppermute | solution.py:846
  179.1 24.3 %collective-permute-start.1 = (f32[8,512,384]{2,1,0:T(8,128)}, f32[8,512,384]{2,1,0:T(8,128)}, u32[]{:S(2)}, u32[]{:S(2)}) collective-permute-start(f32[8,512,384]{2,1,0:T(8,128)} %get-tuple-element.91.refs_0_), channel_id=1, source_target_pairs={{0,1},{1,0},{2,3},{3,2},{4,5},{5,4},{6,7},{7,6}} | collective-permute-start | bytes 18874376 | tf_op jit(solution)/shard_map/ppermute | solution.py:858
  203.4 36.2 %collective-permute-start.2 = (f32[512,1024]{1,0:T(8,128)}, f32[512,1024]{1,0:T(8,128)}, u32[]{:S(2)}, u32[]{:S(2)}) collective-permute-start(f32[512,1024]{1,0:T(8,128)} %get-tuple-element.108.wa_ref), channel_id=1, source_target_pairs={{0,1},{1,0},{2,3},{3,2},{4,5},{5,4},{6,7},{7,6}} | collective-permute-start | bytes 6291464 | tf_op jit(solution)/shard_map/ppermute | solution.py:863
  203.5 33.1 %copy-start.1 = (f32[128,1024]{1,0:T(8,128)S(1)}, f32[128,1024]{1,0:T(8,128)}, u32[]{:S(2)}) copy-start(f32[128,1024]{1,0:T(8,128)} %get-tuple-element.115.refs_8_) | copy-start | bytes 1572868
  234.5 2.6 collective-permute-start.3
  234.5 13.6 %collective-permute-start.7 = (f32[112,1024]{1,0:T(8,128)}, f32[112,1024]{1,0:T(8,128)S(1)}, u32[]{:S(2)}, u32[]{:S(2)}) collective-permute-start(f32[112,1024]{1,0:T(8,128)} %get-tuple-element.113.refs_4_), channel_id=1, source_target_pairs={{0,2},{2,0},{4,6},{6,4},{1,3},{3,1},{5,7},{7,5}} | collective-permute-start | bytes 1376264 | tf_op jit(solution)/shard_map/ppermute | solution.py:871
  235.0 13.8 %collective-permute-start.8 = (f32[112,1024]{1,0:T(8,128)}, f32[112,1024]{1,0:T(8,128)S(1)}, u32[]{:S(2)}, u32[]{:S(2)}) collective-permute-start(f32[112,1024]{1,0:T(8,128)} %get-tuple-element.114.refs_5_), channel_id=1, source_target_pairs={{0,4},{2,6},{4,0},{6,2},{1,5},{3,7},{5,1},{7,3}} | collective-permute-start | bytes 1376264 | tf_op jit(solution)/shard_map/ppermute | solution.py:872
  236.5 43.7 %collective-permute-start.9 = (f32[128,1024]{1,0:T(8,128)S(1)}, f32[128,1024]{1,0:T(8,128)}, u32[]{:S(2)}, u32[]{:S(2)}) collective-permute-start(f32[128,1024]{1,0:T(8,128)S(1)} %copy-done.1), channel_id=1, source_target_pairs={{0,2},{2,0},{4,6},{6,4},{1,3},{3,1},{5,7},{7,5}} | collective-permute-start | bytes 1572872 | tf_op jit(solution)/shard_map/ppermute | solution.py:871
  237.1 43.1 %collective-permute-start.10 = (f32[128,1024]{1,0:T(8,128)}, f32[128,1024]{1,0:T(8,128)}, u32[]{:S(2)}, u32[]{:S(2)}) collective-permute-start(f32[128,1024]{1,0:T(8,128)} %get-tuple-element.116.refs_9_), channel_id=1, source_target_pairs={{0,4},{2,6},{4,0},{6,2},{1,5},{3,7},{5,1},{7,3}} | collective-permute-start | bytes 1572872 | tf_op jit(solution)/shard_map/ppermute | solution.py:872
  239.6 40.6 %copy-start = (f32[136,512]{1,0:T(8,128)}, f32[136,512]{1,0:T(8,128)S(1)}, u32[]{:S(2)}) copy-start(f32[136,512]{1,0:T(8,128)S(1)} %dynamic-slice_add_fusion.refs_0_) | copy-start | bytes 835588
  239.6 40.6 %collective-permute-start.4 = (f32[136,512]{1,0:T(8,128)S(1)}, f32[136,512]{1,0:T(8,128)}, u32[]{:S(2)}, u32[]{:S(2)}) collective-permute-start(f32[136,512]{1,0:T(8,128)S(1)} %dynamic-slice_add_fusion.refs_0_), channel_id=1, source_target_pairs={{0,2},{2,0},{4,6},{6,4},{1,3},{3,1},{5,7},{7,5}} | collective-permute-start | bytes 835592 | tf_op jit(solution)/shard_map/ppermute | solution.py:883
  248.1 0.8 copy-start.2
  248.1 32.1 %collective-permute-start.5 = (f32[136,512]{1,0:T(8,128)S(1)}, f32[136,512]{1,0:T(8,128)}, u32[]{:S(2)}, u32[]{:S(2)}) collective-permute-start(f32[136,512]{1,0:T(8,128)S(1)} %dynamic-slice_add_fusion.refs_0_), channel_id=1, source_target_pairs={{0,4},{2,6},{4,0},{6,2},{1,5},{3,7},{5,1},{7,3}} | collective-permute-start | bytes 835592 | tf_op jit(solution)/shard_map/ppermute | solution.py:883
  248.9 0.8 copy-start.3
  249.7 30.6 %collective-permute-start.6 = (f32[136,512]{1,0:T(8,128)S(1)}, f32[136,512]{1,0:T(8,128)}, u32[]{:S(2)}, u32[]{:S(2)}) collective-permute-start(f32[136,512]{1,0:T(8,128)S(1)} %dynamic-slice_add_fusion.refs_0_), channel_id=1, source_target_pairs={{0,6},{2,4},{4,2},{6,0},{1,7},{3,5},{5,3},{7,1}} | collective-permute-start | bytes 835592 | tf_op jit(solution)/shard_map/ppermute | solution.py:883

commit v4 on v3

--- a/solution.py
+++ b/solution.py
@@ -637,7 +637,7 @@
         ds_ref[c] += dxn[:8] + dxn[8:]
         return da + dxn * gain_ref[c], db + prod * gain_ref[c]
 
-    da, db = lax.fori_loop(0, CH, gather, (zero, zero), unroll=9)
+    da, db = lax.fori_loop(0, CH, gather, (zero, zero), unroll=29)
     mean_a = da * (1.0 / CH) * rstd
     mean_b = db * (1.0 / CH) * rstd * rstd
 
@@ -647,7 +647,7 @@
         dx_ref[c] = (dxn * (gain_ref[c] * rstd) - mean_a - centred * mean_b).astype(BF16)
         return carry
 
-    lax.fori_loop(0, CH, put, 0, unroll=9)
+    lax.fori_loop(0, CH, put, 0, unroll=29)
 
     @pl.when(pl.program_id(0) == pl.num_programs(0) - 1)
     def _():
@@ -779,9 +779,10 @@
     )(z0, zg, zs, wq, wk, wv, wo)
 
 
-def final_kernel(scale, t_ref, acc_ref, z0_ref, zg_ref, zn_ref, q_ref, wq_ref, wk_ref, wv_ref, wo_ref,
-                 dlat_ref, dzg_ref, dzs_ref, dwq_ref, dwk_ref, dwv_ref, dwo_ref):
+def final_kernel(scale, t_ref, acc_ref, z0_ref, zg_ref, zn_ref, q_ref, wq_ref, wk_ref, wv_ref, wo_ref, dw1_ref,
+                 dlat_ref, dzg_ref, dzs_ref, dwq_ref, dwk_ref, dwv_ref, dwo_ref, dw_up_ref):
     n = z0_ref.shape[0]
+    dw_up_ref[:] = dw1_ref[:]
     p_low = acc_ref[n:n + CPAD, :].astype(BF16)
     dwo_ref[:] = mm(wv_ref[:].T, p_low)
     dwv_ref[:] = mm_nt(p_low, wo_ref[:])[:CH]
@@ -802,19 +803,19 @@
     dlat_ref[:] = acc_ref[:n, :] + rstd * (d_hat - mean_a - hat * mean_b)
 
 
-def final(scale, t, acc, z0, zg, zn, q, wq, wk, wv, wo):
+def final(scale, t, acc, z0, zg, zn, q, wq, wk, wv, wo, dw1):
     n, d = z0.shape
     vmem = pl.BlockSpec(memory_space=pltpu.VMEM)
-    shapes = ((n, d), (1, d), (1, d), (d, d), (CH, d), (CH, d), (d, d))
+    shapes = ((n, d), (1, d), (1, d), (d, d), (CH, d), (CH, d), (d, d), (d, d))
     return pl.pallas_call(
         functools.partial(final_kernel, scale),
-        in_specs=[vmem] * 10,
-        out_specs=[vmem] * 7,
+        in_specs=[vmem] * 11,
+        out_specs=[vmem] * 8,
         out_shape=[jax.ShapeDtypeStruct(shape, F32) for shape in shapes],
         compiler_params=pltpu.CompilerParams(vmem_limit_bytes=VMEM_LIMIT),
         cost_estimate=cost(4e9, 25e6),
         name="final",
-    )(t, acc, z0, zg, zn, q, wq, wk, wv, wo)
+    )(t, acc, z0, zg, zn, q, wq, wk, wv, wo, dw1)
 
 
 def solution(mesh):
@@ -888,8 +889,8 @@
         d_x_gain, d_x_shift = sums[0, :CH], sums[1, :CH]
 
         d_m_gain, d_m_shift, d_b_down, d_b_up = (acc[VEC_ROW + k] for k in range(4))
-        d_lat, d_z_gain, d_z_shift, d_w_query, d_w_key, d_w_value, d_w_out = final(
-            qk_scale, t_sum, acc, latents, row(z_gain), z_norm, queries, w_query, wk_pad, wv_pad, w_out)
+        d_lat, d_z_gain, d_z_shift, d_w_query, d_w_key, d_w_value, d_w_out, d_w_up = final(
+            qk_scale, t_sum, acc, latents, row(z_gain), z_norm, queries, w_query, wk_pad, wv_pad, w_out, d_w_up)
         return (z_out, jnp.transpose(dx_cm, (1, 2, 0)), d_lat, d_x_gain, d_x_shift, d_z_gain[0], d_z_shift[0],
                 d_w_query, d_w_key, d_w_value, d_w_out, d_m_gain, d_m_shift, d_w_up, d_b_up, d_w_down, d_b_down)
 

time: 315 us -> 312 us (level)
  local copies, waits for them, and re-layouts: 9.66 us -> 4.88 us
    unnamed x9 -> x8, local copies, waits for them, and re-layouts: 5.8 us -> 1.02 us
where the time goes in v4:
time: 312 us; the launch traced here: 311 us
  Pallas kernels  288 us (92%)
  waiting for transfers between devices  8 us (3%)
  starting transfers between devices  7.53 us (2%)
  local copies, waits for them, and re-layouts  4.88 us (2%)
    pallas_call x4, Pallas kernels, carrier_call(): pl.pallas_call(kernel, grid=(grid,), in_specs=in_specs + c_in, out_specs=...  132 us
    pallas_call x1, Pallas kernels, mlp_a(): pl.pallas_call(mlp_a_kernel, grid=(half // count,), in_specs=[per(AXW), p...  50.9 us
    pallas_call x1, Pallas kernels, x_post(): pl.pallas_call(x_post_kernel, grid_spec=pltpu.PrefetchScalarGridSpec(num_...  28.1 us
    pallas_call x2, Pallas kernels, attn_fwd(): pl.pallas_call(attn_fwd_kernel, grid_spec=pltpu.PrefetchScalarGridSpec(nu...  26.7 us
    pallas_call x1, Pallas kernels, final(): pl.pallas_call(functools.partial(final_kernel, scale), in_specs=[vmem] *...  14.7 us
    pallas_call x1, Pallas kernels, finish(): pl.pallas_call(kernel, in_specs=[vmem] * 13, out_specs=[vmem] * 4, out_sh...  14.2 us
    pallas_call x1, Pallas kernels, x_prep(): pl.pallas_call(x_prep_kernel, grid=(m // lanes,), in_specs=[pl.BlockSpec(...  14 us
    ppermute x2, waiting for transfers between devices, halves(): got_x = lax.ppermute(own[0], 'dp', flip(1))  7.98 us
  transfers between devices with their start and end apart: 11, of which 1 were waited for; matrix products, arithmetic and copies ran while one was open for 1% of the time, Pallas kernels for 31%

profile of v4, /device:TPU:0, one launch (start us, length us, event | category | flops | bytes accessed | tf_op | source)
XLA Modules:
  0.0 311.0 jit_solution(12801735614876135625)
XLA Ops:
  0.7 0.6 pad_add_fusion.1.base_ref
  1.2 14.0 %x_prep.1 = (bf16[16,272,1024]{2,1,0:T(8,128)(2,1)}, f32[16,1024]{1,0:T(8,128)}, f32[16,1024]{1,0:T(8,128)}) custom-call(f32[261]{0:T(512)} %gain_ref.3, f32[261]{0:T(512)} %shift_ref.1, bf16[261,16,1024]{2,1,0:T(8,128)(2,1)} %bitcast.19), custom_call_target="tpu_custom_call" | custom-call | flops 3000000000 | bytes 17104896 | tf_op jit(solution)/shard_map/x_prep/pallas_call | solution.py:124
  15.2 7.1 %prologue.1 = (bf16[512,1024]{1,0:T(8,128)(2,1)}, bf16[512,1024]{1,0:T(8,128)(2,1)}, bf16[512,272]{1,0:T(8,128)(2,1)}, bf16[272,512]{1,0:T(8,128)(2,1)}, bf16[27...) custom-call(f32[512,1024]{1,0:T(8,128)} %z0_ref.5, f32[1,1024]{1,0:T(1,128)} %bitcast.23, ...), custom_call_target="tpu_custom_call" | custom-call | flops 3000000000 | bytes 12000000 | tf_op jit(solution)/shard_map/prologue/pallas_call | solution.py:770
  22.3 13.3 %attn_fwd.3 = (bf16[8,512,1024]{2,1,0:T(8,128)(2,1)}, f32[8,512,384]{2,1,0:T(8,128)}) custom-call(s32[2]{0:T(128)} %pad_add_fusion.1.base_ref, bf16[512,272]{1,0:T(8,128)(2,1)} %get-tuple-element.78.qp_ref, bf16[16,272,1024]{2,1,0:T(8,128)(2,1)} %get-tuple-element.79.xn_ref.refs_3_), custom_call_target="tpu_custom_call" | custom-call | flops 8589934592 | bytes 12582912 | tf_op jit(solution)/shard_map/attn_fwd/pallas_call | solution.py:164
  35.6 0.8 collective-permute-start
  36.5 0.6 pad_add_fusion.base_ref
  37.1 13.4 %attn_fwd.2 = (bf16[8,512,1024]{2,1,0:T(8,128)(2,1)}, f32[8,512,384]{2,1,0:T(8,128)}) custom-call(s32[2]{0:T(128)} %pad_add_fusion.base_ref, bf16[512,272]{1,0:T(8,128)(2,1)} %get-tuple-element.78.qp_ref, bf16[16,272,1024]{2,1,0:T(8,128)(2,1)} %get-tuple-element.79.xn_ref.refs_3_), custom_call_target="tpu_custom_call" | custom-call | flops 8589934592 | bytes 12582912 | tf_op jit(solution)/shard_map/attn_fwd/pallas_call | solution.py:164
  50.5 0.0 collective-permute-done.axb_ref.refs_1_
  50.5 50.9 %mlp_a.1 = (f32[8,512,1024]{2,1,0:T(8,128)}, bf16[8,512,1024]{2,1,0:T(8,128)(2,1)}, f32[8,512,1024]{2,1,0:T(8,128)}, f32[16,512,1024]{2,1,0:T(8,128)}, f32[1024,1024]{1,0:T(8,128)}) custom-call(f32[8,512,384]{2,1,0:T(8,128)} %get-tuple-element.80.axa_ref.refs_0_.refs_1_, f32[8,512,384]{2,1,0:T(8,128)} %collective-permute-done.axb_ref.refs_1_, ...), custom_call_target="tpu_custom_call" | custom-call | flops 30064771072 | bytes 75497472 | tf_op jit(solution)/shard_map/mlp_a/pallas_call | solution.py:459
  101.4 34.7 %shard_map.296 = (bf16[8,512,1024]{2,1,0:T(8,128)(2,1)}, f32[1024,1024]{1,0:T(8,128)}, f32[1,1024]{1,0:T(1,128)}, f32[2,64,1024]{2,1,0:T(8,128)}) custom-call(bf16[8,512,1024]{2,1,0:T(8,128)(2,1)} %get-tuple-element.84.refs_0_, f32[8,512,1024]{2,1,0:T(8,128)} %get-tuple-element.85.refs_1_, bf16[16,512,1024]{2,1,0:T(8,128)(2,1)} %refs_4_.1, ...), custom_call_target="tpu_custom_call" | custom-call | flops 17179869184 | bytes 41943040 | tf_op jit(solution)/shard_map/pallas_call | solution.py:395
  136.1 43.0 %shard_map.297 = (f32[8,512,384]{2,1,0:T(8,128)}, f32[896,1024]{1,0:T(8,128)}, f32[512,1024]{1,0:T(8,128)}, f32[2,128,1024]{2,1,0:T(8,128)}, f32[4,512,1024]{2,1,0:T(8,128)}) custom-call(f32[8,512,384]{2,1,0:T(8,128)} %get-tuple-element.80.axa_ref.refs_0_.refs_1_, f32[8,512,384]{2,1,0:T(8,128)} %collective-permute-done.axb_ref.refs_1_, ...), custom_call_target="tpu_custom_call" | custom-call | flops 15300820992 | bytes 41943040 | tf_op jit(solution)/shard_map/pallas_call | solution.py:395
  179.1 0.0 collective-permute-start.1
  179.2 24.2 %shard_map.298 = (bf16[16,272,1024]{2,1,0:T(8,128)(2,1)}, f32[272,512]{1,0:T(8,128)}, f32[128,1024]{1,0:T(8,128)}, f32[128,1024]{1,0:T(8,128)}, f32[448,1024]{1,0:T(8,128)}) custom-call(f32[8,512,384]{2,1,0:T(8,128)} %get-tuple-element.92.refs_0_, f32[8,512,384]{2,1,0:T(8,128)} %get-tuple-element.80.axa_ref.refs_0_.refs_1_, ...), custom_call_target="tpu_custom_call" | custom-call | flops 17179869184 | bytes 25165824 | tf_op jit(solution)/shard_map/pallas_call | solution.py:395
  203.4 0.0 collective-permute-start.2
  203.5 0.0 collective-permute-done.1.refs_0_
  203.5 0.0 copy-start.1
  203.5 30.0 %shard_map.299 = (bf16[16,272,1024]{2,1,0:T(8,128)(2,1)}, f32[272,512]{1,0:T(8,128)}, f32[112,1024]{1,0:T(8,128)}, f32[112,1024]{1,0:T(8,128)}, f32[4,512,1024]{2,1,0:T(8,128)}) custom-call(f32[8,512,384]{2,1,0:T(8,128)} %collective-permute-done.1.refs_0_, f32[8,512,384]{2,1,0:T(8,128)} %get-tuple-element.81.refs_1_, ...), custom_call_target="tpu_custom_call", output_to_operand_aliasing={{0}: (6, {})} | custom-call | flops 17179869184 | bytes 25165824 | tf_op jit(solution)/shard_map/pallas_call | solution.py:395
  233.5 1.0 constant_dynamic-slice_fusion
  234.5 0.0 collective-permute-start.3
  234.5 0.5 collective-permute-start.7
  235.0 1.5 collective-permute-start.8
  236.5 0.0 copy-done.1
  236.5 0.5 collective-permute-start.9
  237.1 0.0 collective-permute-done.3
  237.1 1.5 collective-permute-start.10
  238.6 1.0 dynamic-slice_add_fusion.refs_0_
  239.6 0.0 copy-start
  239.6 0.0 collective-permute-done.2.wb_ref
  239.6 0.5 collective-permute-start.4
  240.1 8.0 %collective-permute-done.7.refs_6_ = f32[112,1024]{1,0:T(8,128)S(1)} collective-permute-done((f32[112,1024]{1,0:T(8,128)}, f32[112,1024]{1,0:T(8,128)S(1)}, u32[]{:S(2)}, u32[]{:S(2)}) %collective-permute-start.7) | collective-permute-done | bytes 458784 | tf_op jit(solution)/shard_map/ppermute | solution.py:872
  248.1 0.0 copy-start.2
  248.1 0.5 collective-permute-start.5
  248.6 0.2 copy-done.2
  248.9 0.0 collective-permute-done.8.refs_7_
  248.9 0.0 copy-start.3
  248.9 0.8 copy-done.3
  249.7 1.5 collective-permute-start.6
  251.1 28.1 %x_post.1 = (bf16[261,16,1024]{2,1,0:T(8,128)(2,1)}, f32[2,384]{1,0:T(2,128)}, f32[16,512,1024]{2,1,0:T(8,128)}, f32[1024,1024]{1,0:T(8,128)}) custom-call(s32[1]{0:T(128)} %bitcast.base_ref, f32[261]{0:T(512)} %gain_ref.3, bf16[261,16,1024]{2,1,0:T(8,128)(2,1)} %bitcast.20, ...), custom_call_target="tpu_custom_call", output_to_operand_aliasing={{2}: (10, {})} | custom-call | flops 6000000000 | bytes 59211776 | tf_op jit(solution)/shard_map/x_post/pallas_call | solution.py:672
  279.2 0.0 copy-done
  279.2 0.0 collective-permute-done.9.refs_10_
  279.2 0.0 collective-permute-done.10.refs_11_
  279.2 0.0 collective-permute-done.4.refs_1_
  279.3 0.0 collective-permute-done.5.refs_2_
  279.3 0.0 collective-permute-done.6.refs_3_
  279.3 14.2 %finish.1 = (f32[2,384]{1,0:T(2,128)}, f32[272,512]{1,0:T(8,128)}, f32[896,1024]{1,0:T(8,128)}, f32[1024,1024]{1,0:T(8,128)}) custom-call(f32[2,384]{1,0:T(2,128)} %get-tuple-element.112.x_ref, f32[136,512]{1,0:T(8,128)} %copy-done, f32[136,512]{1,0:T(8,128)} %collective-permute-done.4.refs_1_, f32[136,512]{1,0:T(8,128)} %collective-permute-done.5.refs_2_, ...), custom_call_target="tpu_custom_call" | custom-call | tf_op jit(solution)/shard_map/finish/pallas_call | solution.py:741
  293.4 1.3 slice_reduce_fusion
  294.8 1.5 fusion
  296.3 14.7 %final.1 = (f32[512,1024]{1,0:T(8,128)}, f32[1,1024]{1,0:T(1,128)}, f32[1,1024]{1,0:T(1,128)}, f32[1024,1024]{1,0:T(8,128)}, f32[261,1024]{1,0:T(8,128)}, /*inde...) custom-call(f32[272,512]{1,0:T(8,128)} %get-tuple-element.118.t_ref, ...), custom_call_target="tpu_custom_call" | custom-call | flops 4000000000 | bytes 25000000 | tf_op jit(solution)/shard_map/final/pallas_call | solution.py:810
Async XLA Ops:
  35.6 14.8 %collective-permute-start = (f32[8,512,384]{2,1,0:T(8,128)}, f32[8,512,384]{2,1,0:T(8,128)}, u32[]{:S(2)}, u32[]{:S(2)}) collective-permute-start(f32[8,512,384]{2,1,0:T(8,128)} %get-tuple-element.81.refs_1_), channel_id=1, source_target_pairs={{0,1},{1,0},{2,3},{3,2},{4,5},{5,4},{6,7},{7,6}} | collective-permute-start | bytes 18874376 | tf_op jit(solution)/shard_map/ppermute | solution.py:847
  179.1 24.3 %collective-permute-start.1 = (f32[8,512,384]{2,1,0:T(8,128)}, f32[8,512,384]{2,1,0:T(8,128)}, u32[]{:S(2)}, u32[]{:S(2)}) collective-permute-start(f32[8,512,384]{2,1,0:T(8,128)} %get-tuple-element.92.refs_0_), channel_id=1, source_target_pairs={{0,1},{1,0},{2,3},{3,2},{4,5},{5,4},{6,7},{7,6}} | collective-permute-start | bytes 18874376 | tf_op jit(solution)/shard_map/ppermute | solution.py:859
  203.4 36.2 %collective-permute-start.2 = (f32[512,1024]{1,0:T(8,128)}, f32[512,1024]{1,0:T(8,128)}, u32[]{:S(2)}, u32[]{:S(2)}) collective-permute-start(f32[512,1024]{1,0:T(8,128)} %get-tuple-element.109.wa_ref), channel_id=1, source_target_pairs={{0,1},{1,0},{2,3},{3,2},{4,5},{5,4},{6,7},{7,6}} | collective-permute-start | bytes 6291464 | tf_op jit(solution)/shard_map/ppermute | solution.py:864
  203.5 33.1 %copy-start.1 = (f32[128,1024]{1,0:T(8,128)S(1)}, f32[128,1024]{1,0:T(8,128)}, u32[]{:S(2)}) copy-start(f32[128,1024]{1,0:T(8,128)} %get-tuple-element.116.refs_8_) | copy-start | bytes 1572868
  234.5 2.6 collective-permute-start.3
  234.5 13.6 %collective-permute-start.7 = (f32[112,1024]{1,0:T(8,128)}, f32[112,1024]{1,0:T(8,128)S(1)}, u32[]{:S(2)}, u32[]{:S(2)}) collective-permute-start(f32[112,1024]{1,0:T(8,128)} %get-tuple-element.114.refs_4_), channel_id=1, source_target_pairs={{0,2},{2,0},{4,6},{6,4},{1,3},{3,1},{5,7},{7,5}} | collective-permute-start | bytes 1376264 | tf_op jit(solution)/shard_map/ppermute | solution.py:872
  235.0 13.8 %collective-permute-start.8 = (f32[112,1024]{1,0:T(8,128)}, f32[112,1024]{1,0:T(8,128)S(1)}, u32[]{:S(2)}, u32[]{:S(2)}) collective-permute-start(f32[112,1024]{1,0:T(8,128)} %get-tuple-element.115.refs_5_), channel_id=1, source_target_pairs={{0,4},{2,6},{4,0},{6,2},{1,5},{3,7},{5,1},{7,3}} | collective-permute-start | bytes 1376264 | tf_op jit(solution)/shard_map/ppermute | solution.py:873
  236.5 42.7 %collective-permute-start.9 = (f32[128,1024]{1,0:T(8,128)S(1)}, f32[128,1024]{1,0:T(8,128)}, u32[]{:S(2)}, u32[]{:S(2)}) collective-permute-start(f32[128,1024]{1,0:T(8,128)S(1)} %copy-done.1), channel_id=1, source_target_pairs={{0,2},{2,0},{4,6},{6,4},{1,3},{3,1},{5,7},{7,5}} | collective-permute-start | bytes 1572872 | tf_op jit(solution)/shard_map/ppermute | solution.py:872
  237.1 42.2 %collective-permute-start.10 = (f32[128,1024]{1,0:T(8,128)}, f32[128,1024]{1,0:T(8,128)}, u32[]{:S(2)}, u32[]{:S(2)}) collective-permute-start(f32[128,1024]{1,0:T(8,128)} %get-tuple-element.117.refs_9_), channel_id=1, source_target_pairs={{0,4},{2,6},{4,0},{6,2},{1,5},{3,7},{5,1},{7,3}} | collective-permute-start | bytes 1572872 | tf_op jit(solution)/shard_map/ppermute | solution.py:873
  239.6 39.6 %copy-start = (f32[136,512]{1,0:T(8,128)}, f32[136,512]{1,0:T(8,128)S(1)}, u32[]{:S(2)}) copy-start(f32[136,512]{1,0:T(8,128)S(1)} %dynamic-slice_add_fusion.refs_0_) | copy-start | bytes 835588
  239.6 39.7 %collective-permute-start.4 = (f32[136,512]{1,0:T(8,128)S(1)}, f32[136,512]{1,0:T(8,128)}, u32[]{:S(2)}, u32[]{:S(2)}) collective-permute-start(f32[136,512]{1,0:T(8,128)S(1)} %dynamic-slice_add_fusion.refs_0_), channel_id=1, source_target_pairs={{0,2},{2,0},{4,6},{6,4},{1,3},{3,1},{5,7},{7,5}} | collective-permute-start | bytes 835592 | tf_op jit(solution)/shard_map/ppermute | solution.py:884
  248.1 0.8 copy-start.2
  248.1 31.1 %collective-permute-start.5 = (f32[136,512]{1,0:T(8,128)S(1)}, f32[136,512]{1,0:T(8,128)}, u32[]{:S(2)}, u32[]{:S(2)}) collective-permute-start(f32[136,512]{1,0:T(8,128)S(1)} %dynamic-slice_add_fusion.refs_0_), channel_id=1, source_target_pairs={{0,4},{2,6},{4,0},{6,2},{1,5},{3,7},{5,1},{7,3}} | collective-permute-start | bytes 835592 | tf_op jit(solution)/shard_map/ppermute | solution.py:884
  248.9 0.8 copy-start.3
  249.7 29.6 %collective-permute-start.6 = (f32[136,512]{1,0:T(8,128)S(1)}, f32[136,512]{1,0:T(8,128)}, u32[]{:S(2)}, u32[]{:S(2)}) collective-permute-start(f32[136,512]{1,0:T(8,128)S(1)} %dynamic-slice_add_fusion.refs_0_), channel_id=1, source_target_pairs={{0,6},{2,4},{4,2},{6,0},{1,7},{3,5},{5,3},{7,1}} | collective-permute-start | bytes 835592 | tf_op jit(solution)/shard_map/ppermute | solution.py:884
